TPU v7x, 32 devices: a whole 2x2x4 slice. The times are simulated.
32 devices in a mesh: dp: 8 (over y, x, core), blk: 4 (over z).
Axes of the slice: x: 2, y: 2, z: 4, core: 2. Of those that a mesh axis runs over, the one named last changes fastest.
Arguments:
- layer_input: bfloat16 [8, 1024, 2048], P('dp', 'blk'), may hold values from -6 to 6
- queries: bfloat16 [8, 1024, 1024], P('dp', 'blk'), may hold values from -28 to 28
- key_rows: bfloat16 [8, 1024, 1024], P('dp', 'blk'), may hold values from -4 to 4
- value_rows: bfloat16 [8, 1024, 1024], P('dp', 'blk'), may hold values from -6 to 6
- context: bfloat16 [8, 1024, 1024], P('dp', 'blk'), may hold values from -6 to 6
- grad_context: bfloat16 [8, 1024, 1024], P('dp', 'blk'), may hold values from -6 to 6
- grad_output: bfloat16 [8, 1024, 2048], P('dp', 'blk'), may hold values from -6 to 6
- earlier_mass: float32 [8, 4, 1024], P('dp', None, 'blk'), may hold values from 3 to 7
- grad_queries: float32 [8, 1024, 1024], P('dp', 'blk'), may hold values from -0.12 to 0.12
- grad_keys: float32 [8, 1024, 1024], P('dp', 'blk'), may hold values from -0.12 to 0.12
- grad_values: float32 [8, 1024, 1024], P('dp', 'blk'), may hold values from -0.12 to 0.12
- documents: int32 [8, 1024], P('dp', 'blk'), may hold values from 0 to 2, as said below
- weights: float32 [4, 2048, 1024], P(None, 'blk', 'dp'), may hold values from -0.125 to 0.125
- row_factor: float32 [4, 2048], P(None, 'blk'), may hold values from 1.2207032e-07 to 0.00012207031
- column_factor: float32 [4, 1024], P(None, 'dp'), may hold values from 1.2207032e-07 to 0.00012207031
Outputs:
- new_weights: float32 [4, 2048, 1024], P(None, 'blk', 'dp')
- new_row_factor: float32 [4, 2048], P(None, 'blk')
- new_column_factor: float32 [4, 1024], P(None, 'dp')
Inputs may be any that keep to these rules, and one draw needn't show every extreme that they name: Read in order of position, a sequence's document numbers never fall; each sequence has three documents of 128 positions or more.
All inputs are finite; a program needn't handle non-finite values.
Results may differ from a plain program's by a relative error of at most 0.022.
Values may be sent and summed in bfloat16 or wider, within the bound.
No kernel may reach another device: no remote copies, remote signals or barrier semaphores. Data moves between devices by JAX's collectives and lax.ppermute only.
A program may use at most 128 MiB of HBM per device.

v0:
```python
import math

import jax
import jax.numpy as jnp
from jax import lax
from jax.sharding import PartitionSpec as P

beta_two = 0.9
learn_rate = 0.05
tiny_square = 1e-30


def passed_along(value, axis, steps):
    count = lax.axis_size(axis)
    pairs = [(source, (source + steps) % count) for source in range(count)]
    return lax.ppermute(value, axis, pairs)


def as_sent(array):
    return jax.tree.map(lambda a: a.astype(jnp.bfloat16) if a.dtype == jnp.float32 else a, array)


def folded_rows(block_index, blocks, row_count):
    half = row_count // 2
    local = jnp.arange(row_count, dtype=jnp.int32)
    lower = block_index * half + local
    upper = (2 * blocks - 1 - block_index) * half + local - half
    return jnp.where(local < half, lower, upper)


def attend_back(queries, key_rows, value_rows, context, grad_context, earlier_mass, allowed):
    row_count = queries.shape[0]
    key_count = key_rows.shape[0]
    head_count = earlier_mass.shape[0]
    head_size = queries.shape[1] // head_count
    scale_factor = 1.0 / math.sqrt(head_size)
    query_heads = queries.reshape(row_count, head_count, head_size)
    key_heads = key_rows.reshape(key_count, head_count, head_size)
    value_heads = value_rows.reshape(key_count, head_count, head_size)
    context_heads = context.reshape(row_count, head_count, head_size)
    grad_heads = grad_context.reshape(row_count, head_count, head_size)
    scores = (
        jnp.einsum("thd,shd->hts", query_heads, key_heads, preferred_element_type=jnp.float32)
        * scale_factor
    )
    open_pairs = allowed[None]
    peak_score = jnp.maximum(earlier_mass, jnp.max(jnp.where(open_pairs, scores, -jnp.inf), axis=2))
    shifted = jnp.where(open_pairs, jnp.exp(scores - peak_score[:, :, None]), 0.0)
    total_mass = jnp.exp(earlier_mass - peak_score) + jnp.sum(shifted, axis=2)
    log_norm = peak_score + jnp.log(total_mass)
    attention = jnp.where(open_pairs, jnp.exp(scores - log_norm[:, :, None]), 0.0)
    attention_low = attention.astype(jnp.bfloat16)
    row_dot = jnp.sum(context_heads.astype(jnp.float32) * grad_heads.astype(jnp.float32), axis=2).T
    grad_attention = jnp.einsum(
        "thd,shd->hts", grad_heads, value_heads, preferred_element_type=jnp.float32
    )
    grad_scores = (attention * (grad_attention - row_dot[:, :, None]) * scale_factor).astype(
        jnp.bfloat16
    )
    query_step = jnp.einsum(
        "hts,shd->thd", grad_scores, key_heads, preferred_element_type=jnp.float32
    ).reshape(row_count, -1)
    key_step = jnp.einsum(
        "hts,thd->shd", grad_scores, query_heads, preferred_element_type=jnp.float32
    ).reshape(key_count, -1)
    value_step = jnp.einsum(
        "hts,thd->shd", attention_low, grad_heads, preferred_element_type=jnp.float32
    ).reshape(key_count, -1)
    return (query_step, key_step, value_step)


def body(
    layer_input,
    queries,
    key_rows,
    value_rows,
    context,
    grad_context,
    grad_output,
    earlier_mass,
    grad_queries,
    grad_keys,
    grad_values,
    documents,
    weights,
    row_factor,
    column_factor,
):
    blocks = lax.axis_size("blk")
    data_count = lax.axis_size("dp")
    block_index = lax.axis_index("blk")
    row_count = queries.shape[1]
    own_docs = documents[0]
    doc_float = own_docs.astype(jnp.bfloat16)

    def fetch_next(held):
        return passed_along((held[0], held[1], held[2]), "blk", -1)

    nearer = fetch_next((key_rows[0], value_rows[0], doc_float))
    further = fetch_next(nearer)
    seen_keys = jnp.concatenate([nearer[0], further[0]], axis=0)
    seen_values = jnp.concatenate([nearer[1], further[1]], axis=0)
    seen_docs = jnp.concatenate([nearer[2], further[2]], axis=0).astype(jnp.int32)
    own_pos = folded_rows(block_index, blocks, row_count)
    near_pos = folded_rows((block_index + 1) % blocks, blocks, row_count)
    far_pos = folded_rows((block_index + 2) % blocks, blocks, row_count)
    seen_pos = jnp.concatenate([near_pos, far_pos], axis=0)
    allowed = (seen_pos[None, :] <= own_pos[:, None]) & (seen_docs[None, :] == own_docs[:, None])
    query_step, key_step, value_step = attend_back(
        queries[0], seen_keys, seen_values, context[0], grad_context[0], earlier_mass[0], allowed
    )
    near_part = (key_step[:row_count], value_step[:row_count])
    far_part = (key_step[row_count:], value_step[row_count:])

    def send_back(pair):
        return passed_along((as_sent(pair[0]), as_sent(pair[1])), "blk", 1)

    moved = send_back(far_part)
    home = send_back((moved[0] + near_part[0], moved[1] + near_part[1]))
    query_total = grad_queries[0] + query_step
    key_total = grad_keys[0] + home[0]
    value_total = grad_values[0] + home[1]
    right_low = jnp.stack([query_total, key_total, value_total], axis=1).astype(jnp.bfloat16)
    layer_rows = layer_input[0]
    output_rows = grad_output[0]
    context_rows = context[0]
    all_tokens = data_count * blocks * row_count
    part_inner = jnp.einsum(
        "twh,td->hwd", right_low, layer_rows, preferred_element_type=jnp.float32
    )
    part_output = jnp.einsum(
        "th,td->hd", context_rows, output_rows, preferred_element_type=jnp.float32
    )
    summed = lax.psum_scatter(
        jnp.concatenate([part_inner, part_output[:, None, :]], axis=1).astype(jnp.bfloat16),
        "dp",
        scatter_dimension=0,
        tiled=True,
    )
    grouped = lax.psum_scatter(summed, "blk", scatter_dimension=2, tiled=True).astype(jnp.float32)
    gradient = jnp.transpose(grouped, (1, 2, 0)) / all_tokens
    local_rows = gradient.shape[1]
    local_cols = gradient.shape[2]
    full_rows = local_rows * blocks
    full_cols = local_cols * data_count
    squares = gradient * gradient + tiny_square
    row_part = jnp.sum(squares, axis=2)
    col_part = jnp.sum(squares, axis=1)
    row_sum = lax.psum(row_part, "dp")
    col_sum = lax.psum(col_part, "blk")
    new_row_factor = beta_two * row_factor + (1.0 - beta_two) * row_sum / full_cols
    new_column_factor = beta_two * column_factor + (1.0 - beta_two) * col_sum / full_rows
    row_mean = lax.psum(jnp.sum(new_row_factor, axis=1), "blk") / full_rows
    second = new_row_factor[:, :, None] * new_column_factor[:, None, :] / row_mean[:, None, None]
    new_weights = weights - learn_rate * gradient * lax.rsqrt(second)
    return (new_weights, new_row_factor, new_column_factor)


def solution(mesh):
    placed = (
        P("dp", "blk", None),
        P("dp", "blk", None),
        P("dp", "blk", None),
        P("dp", "blk", None),
        P("dp", "blk", None),
        P("dp", "blk", None),
        P("dp", "blk", None),
        P("dp", None, "blk"),
        P("dp", "blk", None),
        P("dp", "blk", None),
        P("dp", "blk", None),
        P("dp", "blk"),
        P(None, "blk", "dp"),
        P(None, "blk"),
        P(None, "dp"),
    )
    return jax.shard_map(
        body,
        mesh=mesh,
        in_specs=placed,
        out_specs=(P(None, "blk", "dp"), P(None, "blk"), P(None, "dp")),
        check_vma=False,
    )
```

profile of v0, /device:TPU:0, one launch (start us, length us, event | category | flops | bytes accessed | tf_op | source)
XLA Modules:
  0.0 330.0 jit_solution(4937158496629812129)
XLA Ops:
  8.1 5.1 %collective-permute-start.2 = (bf16[256]{0:T(256)(128)(2,1)S(1)}, bf16[256]{0:T(256)(128)(2,1)S(1)}, u32[]{:S(2)}, u32[]{:S(2)}) collective-permute-start(bf16[256]{0:T(256)(128)(2,1)S(1)} %convert_element_type.64), channel_id=1, source_target_pairs={{0,3},{1,0},{2,1},{3,2},{4,7},{5,4},{6,5},{7,6},{8,11},{9,8},{10,9... | collective-permute-start | bytes 1544 | tf_op jit(solution)/shard_map/ppermute | solution.py:16
  13.1 2.0 copy.48
  15.6 2.1 copy.51
  19.4 4.5 %convert_bitcast_fusion.1 = bf16[1024,1,2048]{2,0,1:T(8,128)(2,1)} fusion(bf16[1,256,2048]{2,1,0:T(8,128)(2,1)} %param.21, bf16[1,256,1024]{2,1,0:T(8,128)(2,1)S(1)} %copy-done.6), kind=kOutput, calls=%fused_computation.2 | convolution fusion | flops 1075838976 | bytes 5767168 | tf_op jit(solution)/shard_map/th,td->hd/dot_general | solution.py:131
  23.9 6.4 %collective-permute-done = bf16[256,1024]{0,1:T(8,128)(2,1)} collective-permute-done((bf16[256,1024]{0,1:T(8,128)(2,1)}, bf16[256,1024]{0,1:T(8,128)(2,1)}, u32[]{:S(2)}, u32[]{:S(2)}) %collective-permute-start) | collective-permute-done | bytes 524320 | tf_op jit(solution)/shard_map/ppermute | solution.py:16
  30.3 2.2 collective-permute-start.1
  34.8 1.6 copy.56
  36.4 1.3 copy.47
  37.7 1.6 copy.59
  39.3 12.1 %collective-permute-done.3 = bf16[256]{0:T(256)(128)(2,1)S(1)} collective-permute-done((bf16[256]{0:T(256)(128)(2,1)S(1)}, bf16[256]{0:T(256)(128)(2,1)S(1)}, u32[]{:S(2)}, u32[]{:S(2)}) %collective-permute-start.3) | collective-permute-done | bytes 544 | tf_op jit(solution)/shard_map/ppermute | solution.py:16
  51.6 2.3 collective-permute-start.5
  56.4 8.0 %collective-permute-done.5 = bf16[256,1024]{0,1:T(8,128)(2,1)S(1)} collective-permute-done((bf16[256,1024]{0,1:T(8,128)(2,1)}, bf16[256,1024]{0,1:T(8,128)(2,1)S(1)}, u32[]{:S(2)}, u32[]{:S(2)}) %collective-permute-start.5) | collective-permute-done | bytes 524320 | tf_op jit(solution)/shard_map/ppermute | solution.py:16
  70.0 13.9 %collective-permute-done.6 = bf16[256,1024]{0,1:T(8,128)(2,1)S(1)} collective-permute-done((bf16[256,1024]{0,1:T(8,128)(2,1)S(1)}, bf16[256,1024]{0,1:T(8,128)(2,1)S(1)}, u32[]{:S(2)}, u32[]{:S(2)}) %collective-permute-start.6) | collective-permute-done | bytes 524320 | tf_op jit(solution)/shard_map/ppermute | solution.py:16
  84.2 11.0 %collective-permute-done.8 = bf16[256,1024]{0,1:T(8,128)(2,1)S(1)} collective-permute-done((bf16[256,1024]{0,1:T(8,128)(2,1)S(1)}, bf16[256,1024]{0,1:T(8,128)(2,1)S(1)}, u32[]{:S(2)}, u32[]{:S(2)}) %collective-permute-start.8) | collective-permute-done | bytes 524320 | tf_op jit(solution)/shard_map/ppermute | solution.py:16
  95.8 10.6 %collective-permute-done.7 = bf16[256,1024]{0,1:T(8,128)(2,1)S(1)} collective-permute-done((bf16[256,1024]{0,1:T(8,128)(2,1)S(1)}, bf16[256,1024]{0,1:T(8,128)(2,1)S(1)}, u32[]{:S(2)}, u32[]{:S(2)}) %collective-permute-start.7) | collective-permute-done | bytes 524320 | tf_op jit(solution)/shard_map/ppermute | solution.py:16
  106.5 8.3 %collective-permute-done.9 = bf16[256,1024]{0,1:T(8,128)(2,1)S(1)} collective-permute-done((bf16[256,1024]{0,1:T(8,128)(2,1)S(1)}, bf16[256,1024]{0,1:T(8,128)(2,1)S(1)}, u32[]{:S(2)}, u32[]{:S(2)}) %collective-permute-start.9) | collective-permute-done | bytes 524320 | tf_op jit(solution)/shard_map/ppermute | solution.py:16
  115.0 6.4 %convert_bitcast_fusion = bf16[1024,3,2048]{2,0,1:T(8,128)(2,1)} fusion(bf16[256,1,1024]{0,2,1:T(8,128)(2,1)S(1)} %fusion.34, bf16[256,1,1024]{0,2,1:T(8,128)(2,1)S(1)} %fusion.33, bf16[256,1,1024]{0,2,1:T(8,128)(2,1)S(1)} %fusion.22, bf16[1,256,2048]{2,1,0:T(8,128)(2,1)S(1)} %copy-done), kind=kOutput, calls=%fused_computation.1 | convolution fusion | flops 3229089792 | bytes 15204352 | tf_op jit(solution)/shard_map/twh,td->hwd/dot_general | solution.py:128
  121.3 12.2 %pad_maximum_fusion = bf16[1024,4,2048]{2,0,1:T(8,128)(2,1)} fusion(bf16[1024,1,2048]{2,0,1:T(8,128)(2,1)S(1)} %copy-done.2, bf16[1024,3,2048]{2,0,1:T(8,128)(2,1)} %convert_bitcast_fusion), kind=kLoop, calls=%fused_computation | loop fusion | flops 8388608 | bytes 33554432 | tf_op jit(solution)/shard_map/concatenate | solution.py:135
  133.6 115.7 %reduce-scatter.3.cloned.1.call-done = bf16[128,4,2048]{2,0,1:T(8,128)(2,1)} async-done(((bf16[1024,4,2048]{2,0,1:T(8,128)(2,1)}), bf16[128,4,2048]{2,0,1:T(8,128)(2,1)}) %reduce-scatter.3.cloned.1.call-update) | async-done | bytes 2097168 | tf_op jit(solution)/shard_map/reduce_scatter | solution.py:134
  249.7 45.6 %reduce-scatter.5.cloned.1.call-done = bf16[128,4,512]{2,0,1:T(8,128)(2,1)} async-done(((bf16[128,4,2048]{2,0,1:T(8,128)(2,1)}), bf16[128,4,512]{2,0,1:T(8,128)(2,1)}) %reduce-scatter.5.cloned.1.call-update) | async-done | bytes 524304 | tf_op jit(solution)/shard_map/reduce_scatter | solution.py:140
  295.2 1.3 fusion.19
  296.6 13.5 %psum.21 = f32[4,512]{1,0:T(4,128)S(1)} all-reduce(f32[4,512]{1,0:T(4,128)S(1)} %get-tuple-element.13), channel_id=1, replica_groups=mesh['dp'=8,'blk'=4] {'dp'}, use_global_device_ids=true, to_apply=%region_6.7 | all-reduce | flops 2048 | bytes 16384 | tf_op jit(solution)/shard_map/psum | solution.py:149
  310.2 10.2 %all-reduce = (f32[4]{0:T(128)S(1)}, f32[4,128]{1,0:T(4,128)S(1)}) all-reduce(f32[4]{0:T(128)S(1)} %get-tuple-element.16, f32[4,128]{1,0:T(4,128)S(1)} %bitcast.123), channel_id=1, replica_groups=mesh['dp'=8,'blk'=4] {'blk'}, use_global_device_ids=true, to_apply=%region_10.11 | all-reduce | flops 516 | bytes 4128 | tf_op jit(solution)/shard_map/psum | solution.py:153
  320.5 1.4 fusion.16
  (90 shorter events, 16.3 us)
Async XLA Ops:
  7.2 107.8 %copy-start = (bf16[1,256,2048]{2,1,0:T(8,128)(2,1)S(1)}, bf16[1,256,2048]{2,1,0:T(8,128)(2,1)}, u32[]{:S(2)}) copy-start(bf16[1,256,2048]{2,1,0:T(8,128)(2,1)} %param.15) | copy-start | bytes 3145732
  7.2 11.3 %copy-start.6 = (bf16[1,256,1024]{2,1,0:T(8,128)(2,1)S(1)}, bf16[1,256,1024]{2,1,0:T(8,128)(2,1)}, u32[]{:S(2)}) copy-start(bf16[1,256,1024]{2,1,0:T(8,128)(2,1)} %param.19) | copy-start | bytes 1572868
  7.2 242.1 %reduce-scatter.3.cloned.1.call-start = ((), (), s32[]{:S(2)}) async-start(), calls=%async_computation.2 | async-start | bytes 18874368 | tf_op jit(solution)/shard_map/reduce_scatter | solution.py:134
  8.1 25.7 %collective-permute-start.2 = (bf16[256]{0:T(256)(128)(2,1)S(1)}, bf16[256]{0:T(256)(128)(2,1)S(1)}, u32[]{:S(2)}, u32[]{:S(2)}) collective-permute-start(bf16[256]{0:T(256)(128)(2,1)S(1)} %convert_element_type.64), channel_id=1, source_target_pairs={{0,3},{1,0},{2,1},{3,2},{4,7},{5,4},{6,5},{7,6},{8,11},{9,8},{10,9... | collective-permute-start | bytes 1544 | tf_op jit(solution)/shard_map/ppermute | solution.py:16
  15.2 15.1 %collective-permute-start = (bf16[256,1024]{0,1:T(8,128)(2,1)}, bf16[256,1024]{0,1:T(8,128)(2,1)}, u32[]{:S(2)}, u32[]{:S(2)}) collective-permute-start(bf16[256,1024]{0,1:T(8,128)(2,1)} %bitcast.1), channel_id=1, source_target_pairs={{0,3},{1,0},{2,1},{3,2},{4,7},{5,4},{6,5},{7,6},{8,11},{9,8},{10,9... | collective-permute-start | bytes 1572872 | tf_op jit(solution)/shard_map/ppermute | solution.py:16
  17.7 33.9 %collective-permute-start.4 = (bf16[256,1024]{0,1:T(8,128)(2,1)}, bf16[256,1024]{0,1:T(8,128)(2,1)}, u32[]{:S(2)}, u32[]{:S(2)}) collective-permute-start(bf16[256,1024]{0,1:T(8,128)(2,1)} %bitcast.6), channel_id=1, source_target_pairs={{0,3},{1,0},{2,1},{3,2},{4,7},{5,4},{6,5},{7,6},{8,11},{9,8},{10,9... | collective-permute-start | bytes 1572872 | tf_op jit(solution)/shard_map/ppermute | solution.py:16
  19.4 14.3 %copy-start.12 = (bf16[1,256,1024]{2,1,0:T(8,128)(2,1)S(1)}, bf16[1,256,1024]{2,1,0:T(8,128)(2,1)}, u32[]{:S(2)}) copy-start(bf16[1,256,1024]{2,1,0:T(8,128)(2,1)} %param.16) | copy-start | bytes 1572868
  30.3 23.6 %collective-permute-start.1 = (bf16[256,1024]{0,1:T(8,128)(2,1)}, bf16[256,1024]{0,1:T(8,128)(2,1)}, u32[]{:S(2)}, u32[]{:S(2)}) collective-permute-start(bf16[256,1024]{0,1:T(8,128)(2,1)} %collective-permute-done), channel_id=1, source_target_pairs={{0,3},{1,0},{2,1},{3,2},{4,7},{5,4},{6,5},{7,6},{8,11},{9,8},{10,9... | collective-permute-start | bytes 1572872 | tf_op jit(solution)/shard_map/ppermute | solution.py:16
  33.7 17.6 %collective-permute-start.3 = (bf16[256]{0:T(256)(128)(2,1)S(1)}, bf16[256]{0:T(256)(128)(2,1)S(1)}, u32[]{:S(2)}, u32[]{:S(2)}) collective-permute-start(bf16[256]{0:T(256)(128)(2,1)S(1)} %collective-permute-done.2), channel_id=1, source_target_pairs={{0,3},{1,0},{2,1},{3,2},{4,7},{5,4},{6,5},{7,6},{8,11},{9,8},{10,9... | collective-permute-start | bytes 1544 | tf_op jit(solution)/shard_map/ppermute | solution.py:16
  36.4 15.0 %copy-start.18 = (s32[1,256]{1,0:T(1,128)S(1)}, s32[1,256]{1,0:T(1,128)}, u32[]{:S(2)}) copy-start(s32[1,256]{1,0:T(1,128)} %param.26) | copy-start | bytes 3076
  39.3 15.9 %copy-start.7 = (bf16[1,256,1024]{1,2,0:T(8,128)(2,1)S(1)}, bf16[1,256,1024]{1,2,0:T(8,128)(2,1)}, u32[]{:S(2)}) copy-start(bf16[1,256,1024]{1,2,0:T(8,128)(2,1)} %copy.69) | copy-start | bytes 1572868
  51.6 12.8 %collective-permute-start.5 = (bf16[256,1024]{0,1:T(8,128)(2,1)}, bf16[256,1024]{0,1:T(8,128)(2,1)S(1)}, u32[]{:S(2)}, u32[]{:S(2)}) collective-permute-start(bf16[256,1024]{0,1:T(8,128)(2,1)} %collective-permute-done.4), channel_id=1, source_target_pairs={{0,3},{1,0},{2,1},{3,2},{4,7},{5,4},{6,5},{7,6},{8,11},{9,8},{10,9... | collective-permute-start | bytes 1572872 | tf_op jit(solution)/shard_map/ppermute | solution.py:16
  67.1 16.9 %collective-permute-start.6 = (bf16[256,1024]{0,1:T(8,128)(2,1)S(1)}, bf16[256,1024]{0,1:T(8,128)(2,1)S(1)}, u32[]{:S(2)}, u32[]{:S(2)}) collective-permute-start(bf16[256,1024]{0,1:T(8,128)(2,1)S(1)} %bitcast.120), channel_id=1, source_target_pairs={{0,1},{1,2},{2,3},{3,0},{4,5},{5,6},{6,7},{7,4},{8,9},{9,10},{10,1... | collective-permute-start | bytes 1572872 | tf_op jit(solution)/shard_map/ppermute | solution.py:16
  68.4 15.5 %slice-start.1 = ((f32[512,4,256]{0,2,1:T(8,128)}), f32[256,4,256]{0,2,1:T(8,128)S(1)}, s32[]{:S(2)}) async-start(f32[512,4,256]{0,2,1:T(8,128)} %copy-done.4), calls=%async_computation.5 | async-start | bytes 2097152 | tf_op jit(solution)/shard_map/slice | solution.py:112
  68.4 26.8 %collective-permute-start.8 = (bf16[256,1024]{0,1:T(8,128)(2,1)S(1)}, bf16[256,1024]{0,1:T(8,128)(2,1)S(1)}, u32[]{:S(2)}, u32[]{:S(2)}) collective-permute-start(bf16[256,1024]{0,1:T(8,128)(2,1)S(1)} %bitcast.121), channel_id=1, source_target_pairs={{0,1},{1,2},{2,3},{3,0},{4,5},{5,6},{6,7},{7,4},{8,9},{9,10},{10,1... | collective-permute-start | bytes 1572872 | tf_op jit(solution)/shard_map/ppermute | solution.py:16
  70.0 25.6 %copy-start.5 = (f32[1,256,1024]{1,2,0:T(8,128)S(1)}, f32[1,256,1024]{1,2,0:T(8,128)}, u32[]{:S(2)}) copy-start(f32[1,256,1024]{1,2,0:T(8,128)} %copy.47) | copy-start | bytes 3145732
  83.9 11.2 %slice-start = ((f32[512,4,256]{0,2,1:T(8,128)}), f32[256,4,256]{0,2,1:T(8,128)S(1)}, s32[]{:S(2)}) async-start(f32[512,4,256]{0,2,1:T(8,128)} %copy-done.3), calls=%async_computation.4 | async-start | bytes 2097152 | tf_op jit(solution)/shard_map/slice | solution.py:112
  84.1 22.3 %collective-permute-start.7 = (bf16[256,1024]{0,1:T(8,128)(2,1)S(1)}, bf16[256,1024]{0,1:T(8,128)(2,1)S(1)}, u32[]{:S(2)}, u32[]{:S(2)}) collective-permute-start(bf16[256,1024]{0,1:T(8,128)(2,1)S(1)} %fusion.27), channel_id=1, source_target_pairs={{0,1},{1,2},{2,3},{3,0},{4,5},{5,6},{6,7},{7,4},{8,9},{9,10},{10,1... | collective-permute-start | bytes 1572872 | tf_op jit(solution)/shard_map/ppermute | solution.py:16
  95.3 19.5 %collective-permute-start.9 = (bf16[256,1024]{0,1:T(8,128)(2,1)S(1)}, bf16[256,1024]{0,1:T(8,128)(2,1)S(1)}, u32[]{:S(2)}, u32[]{:S(2)}) collective-permute-start(bf16[256,1024]{0,1:T(8,128)(2,1)S(1)} %fusion.25), channel_id=1, source_target_pairs={{0,1},{1,2},{2,3},{3,0},{4,5},{5,6},{6,7},{7,4},{8,9},{9,10},{10,1... | collective-permute-start | bytes 1572872 | tf_op jit(solution)/shard_map/ppermute | solution.py:16
  133.6 115.8 %copy-start.10 = (f32[4,512,128]{2,1,0:T(8,128)S(1)}, f32[4,512,128]{2,1,0:T(8,128)}, u32[]{:S(2)}) copy-start(f32[4,512,128]{2,1,0:T(8,128)} %param.27) | copy-start | bytes 3145732
  133.6 161.7 %reduce-scatter.5.cloned.1.call-start = ((), (), s32[]{:S(2)}) async-start(), calls=%async_computation.3 | async-start | bytes 2621440 | tf_op jit(solution)/shard_map/reduce_scatter | solution.py:140
  249.3 60.8 %copy-start.16 = (f32[4,512]{1,0:T(4,128)S(1)}, f32[4,512]{1,0:T(4,128)}, u32[]{:S(2)}) copy-start(f32[4,512]{1,0:T(4,128)} %param.28) | copy-start | bytes 24580
  249.3 71.1 %copy-start.17 = (f32[4,128]{1,0:T(4,128)S(1)}, f32[4,128]{1,0:T(4,128)}, u32[]{:S(2)}) copy-start(f32[4,128]{1,0:T(4,128)} %param.29) | copy-start | bytes 6148
  310.2 13.0 %copy-start.13 = (f32[4,512]{1,0:T(4,128)}, f32[4,512]{1,0:T(4,128)S(1)}, u32[]{:S(2)}) copy-start(f32[4,512]{1,0:T(4,128)S(1)} %get-tuple-element.17) | copy-start | bytes 24580
  (9 other events, 38.9 us)
Sparse Core Ops, SparseCore 0:
  133.7 115.5 reduce-scatter.2
  251.6 43.6 reduce-scatter.4
where the time goes:
time: 331 us; the launch traced here: 330 us
  waiting for transfers between devices  232 us (70%)
  blocking collectives  23.7 us (7%)
  other arithmetic  20.1 us (6%)
  between operations  14.4 us (4%)
  local copies, waits for them, and re-layouts  14.1 us (4%)
  matrix products  14 us (4%)
  starting transfers between devices  12.1 us (4%)
    reduce_scatter x1, waiting for transfers between devices, body(): lax.psum_scatter(jnp.concatenate([part_inner, part_output[:, None, :]], a...  116 us
    ppermute x10, waiting for transfers between devices, passed_along(): return lax.ppermute(value, axis, pairs)  70.3 us
    reduce_scatter x1, waiting for transfers between devices, body(): lax.psum_scatter(summed, 'blk', scatter_dimension=2, tiled=True)  45.6 us
    psum x1, blocking collectives, body(): row_sum = lax.psum(row_part, 'dp')  13.5 us
    concatenate x1, other arithmetic, body(): jnp.concatenate([part_inner, part_output[:, None, :]], axis=1)  12.2 us
    ppermute x10, starting transfers between devices, passed_along(): return lax.ppermute(value, axis, pairs)  12 us
    unnamed x45, local copies, waits for them, and re-layouts  10.9 us
    psum x1, blocking collectives, body(): row_mean = lax.psum(jnp.sum(new_row_factor, axis=1), 'blk') / full_rows  10.2 us
  transfers between devices with their start and end apart: 12, of which 9 were waited for; matrix products, arithmetic and copies ran while one was open for 6% of the time, Pallas kernels for 0%

commit v1 on v0

--- a/solution.py
+++ b/solution.py
@@ -3,7 +3,10 @@
 import jax
 import jax.numpy as jnp
 from jax import lax
+from jax.experimental import pallas as pl
+from jax.experimental.pallas import tpu as pltpu
 from jax.sharding import PartitionSpec as P
+
 
 beta_two = 0.9
 learn_rate = 0.05
@@ -69,7 +72,7 @@
     return (query_step, key_step, value_step)
 
 
-def body(
+def ring_body(
     layer_input,
     queries,
     key_rows,
@@ -156,6 +159,373 @@
     return (new_weights, new_row_factor, new_column_factor)
 
 
+def swapped(value, mask):
+    count = lax.axis_size("dp")
+    return lax.ppermute(value, "dp", [(source, source ^ mask) for source in range(count)])
+
+
+def rotated(value, steps):
+    count = lax.axis_size("blk")
+    pairs = [(source, (source + steps) % count) for source in range(count)]
+    return lax.ppermute(value, "blk", pairs)
+
+
+def split_three(value):
+    high = value.astype(jnp.bfloat16).astype(jnp.float32)
+    middle = (value - high).astype(jnp.bfloat16).astype(jnp.float32)
+    return (high, middle, value - high - middle)
+
+
+def pack_kernel(blocks, place_ref, *refs):
+    stored, outs = refs[:7], refs[7 : 7 + blocks]
+    held, dot_ref, arrived = refs[7 + blocks : 14 + blocks], refs[14 + blocks], refs[15 + blocks]
+    copies = [
+        pltpu.make_async_copy(source, target, arrived.at[index])
+        for index, (source, target) in enumerate(zip(stored, held))
+    ]
+    for copy in copies:
+        copy.start()
+    for copy in copies:
+        copy.wait()
+    query_ref, key_ref, value_ref, grad_ref, context_ref, mass_ref, docs_ref = held
+    rows = query_ref.shape[1]
+    head_size = query_ref.shape[2] // blocks
+    lane = lax.broadcasted_iota(jnp.int32, (rows, 128), 1)
+    dots = jnp.zeros((rows, 128), jnp.float32)
+    for head in range(blocks):
+        columns = slice(head * head_size, (head + 1) * head_size)
+        product = context_ref[0, :, columns].astype(jnp.float32) * grad_ref[0, :, columns].astype(
+            jnp.float32
+        )
+        dots = jnp.where(lane == head, jnp.sum(product, axis=1, keepdims=True), dots)
+    dot_ref[...] = dots.T
+    docs = docs_ref[...].astype(jnp.float32)
+    line = lax.broadcasted_iota(jnp.int32, (16, rows), 0)
+    for step in range(blocks):
+        head = lax.rem(place_ref[0] + step, blocks)
+        columns = pl.ds(pl.multiple_of(head * head_size, head_size), head_size)
+        for index, ref in enumerate((query_ref, key_ref, value_ref, grad_ref)):
+            outs[step][index * rows : (index + 1) * rows] = ref[0, :, columns]
+        terms = split_three(mass_ref[0, pl.ds(head, 1), :]) + split_three(dot_ref[pl.ds(head, 1), :])
+        side = jnp.where(line == 6, docs, 0.0)
+        for index, term in enumerate(terms):
+            side = jnp.where(line == index, term, side)
+        outs[step][4 * rows :] = side.astype(jnp.bfloat16)
+
+
+def head_kernel(blocks, place_ref, *refs):
+    packs = refs[:blocks]
+    value_outs, key_outs, query_outs = (
+        refs[(1 + index) * blocks : (2 + index) * blocks] for index in range(3)
+    )
+    weight_ref, slope_ref = refs[4 * blocks :]
+    rows = weight_ref.shape[2]
+    half = rows // 2
+    scale_factor = 1.0 / math.sqrt(packs[0].shape[1])
+    local_down = lax.broadcasted_iota(jnp.int32, (rows, 1), 0)
+    local_across = lax.broadcasted_iota(jnp.int32, (1, rows), 1)
+    block_of = [lax.rem(place_ref[0] + step, blocks) for step in range(blocks)]
+
+    def part_of(step, index):
+        return packs[step][index * rows : (index + 1) * rows]
+
+    def positions(local, block):
+        lower = block * half + local
+        upper = (2 * blocks - 1 - block) * half + local - half
+        return jnp.where(local < half, lower, upper)
+
+    def times(left, right, left_dim, right_dim):
+        return lax.dot_general(
+            left,
+            right,
+            (((left_dim,), (right_dim,)), ((), ())),
+            preferred_element_type=jnp.float32,
+        )
+
+    sides = []
+    for step in range(blocks):
+        side = packs[step][4 * rows :].astype(jnp.float32)
+        mass = side[0:1] + side[1:2] + side[2:3]
+        row_dot = side[3:4] + side[4:5] + side[5:6]
+        sides.append((mass, row_dot, side[6:7]))
+    for step in range(blocks):
+        visited = [(step + 1) % blocks, (step + 2) % blocks]
+        line = lax.broadcasted_iota(jnp.int32, (8, rows), 0)
+        down = jnp.where(line == 0, sides[step][0], jnp.where(line == 1, sides[step][1], sides[step][2])).T
+        mass, row_dot, docs = down[:, 0:1], down[:, 1:2], down[:, 2:3]
+        own_pos = positions(local_down, block_of[step])
+        scored = []
+        for other in visited:
+            score = times(part_of(step, 0), part_of(other, 1), 1, 1) * scale_factor
+            allowed = (positions(local_across, block_of[other]) <= own_pos) & (
+                sides[other][2] == docs
+            )
+            scored.append(jnp.where(allowed, score, -jnp.inf))
+        peak = mass
+        for score in scored:
+            peak = jnp.maximum(peak, jnp.max(score, axis=1, keepdims=True))
+        shifted = [jnp.exp(score - peak) for score in scored]
+        total = jnp.exp(mass - peak)
+        for part in shifted:
+            total = total + jnp.sum(part, axis=1, keepdims=True)
+        inverse = 1.0 / total
+        query_step = None
+        for index, other in enumerate(visited):
+            attention = shifted[index] * inverse
+            grad_attention = times(part_of(step, 3), part_of(other, 2), 1, 1)
+            slope = (attention * (grad_attention - row_dot) * scale_factor).astype(jnp.bfloat16)
+            weight_ref[step, index] = attention.astype(jnp.bfloat16)
+            slope_ref[step, index] = slope
+            part = times(slope, part_of(other, 1), 1, 0)
+            query_step = part if query_step is None else query_step + part
+        query_outs[step][...] = query_step.astype(jnp.bfloat16)
+    for step in range(blocks):
+        near, far = (step - 1) % blocks, (step - 2) % blocks
+        value_step = times(weight_ref[near, 0], part_of(near, 3), 0, 0) + times(
+            weight_ref[far, 1], part_of(far, 3), 0, 0
+        )
+        value_outs[step][...] = value_step.astype(jnp.bfloat16)
+        key_step = times(slope_ref[near, 0], part_of(near, 0), 0, 0) + times(
+            slope_ref[far, 1], part_of(far, 0), 0, 0
+        )
+        key_outs[step][...] = key_step.astype(jnp.bfloat16)
+
+
+def gather_kernel(blocks, place_ref, *refs):
+    parts = refs[:blocks]
+    earlier = refs[blocks]
+    outs = refs[blocks + 1 :]
+    head_size = parts[0].shape[1]
+    for index in range(blocks):
+        head = lax.bitwise_xor(place_ref[1], index)
+        source = lax.rem(place_ref[0] - head + blocks, blocks)
+        columns = pl.ds(pl.multiple_of(head * head_size, head_size), head_size)
+        for step in range(blocks):
+
+            @pl.when(source == step)
+            def add(step=step, index=index, columns=columns):
+                total = earlier[0, :, columns] + parts[step][...].astype(jnp.float32)
+                outs[index][...] = total.astype(jnp.bfloat16)
+
+
+def weight_kernel(blocks, place_ref, own_ref, beside_ref, below_ref, upper_ref, lower_ref, *refs):
+    rights = refs[:blocks]
+    keep_ref, send_ref = refs[blocks:]
+    features, width = keep_ref.shape
+    chunk = features // blocks
+    core = place_ref[2]
+    for index in range(blocks):
+        where = slice(index * chunk, (index + 1) * chunk)
+        if index < blocks // 2:
+            across = upper_ref[where]
+        else:
+            across = lower_ref[(index - blocks // 2) * chunk : (index - blocks // 2 + 1) * chunk]
+        total = None
+        for left, right in zip((own_ref[where], beside_ref[where], below_ref[where], across), rights):
+            part = jnp.dot(left, right[...], preferred_element_type=jnp.float32)
+            total = part if total is None else total + part
+        first, second = total[:, :width], total[:, width:]
+        keep_ref[where] = jnp.where(core == 0, first, second)
+        send_ref[where] = jnp.where(core == 0, second, first).astype(jnp.bfloat16)
+
+
+def share_kernel(blocks, place_ref, keep_ref, other_ref, *outs):
+    chunk = keep_ref.shape[0] // blocks
+    for step in range(blocks):
+        start = lax.rem(place_ref[0] + step, blocks) * chunk
+        where = pl.ds(pl.multiple_of(start, chunk), chunk)
+        total = keep_ref[where] + other_ref[where].astype(jnp.float32)
+        outs[step][...] = total.astype(outs[step].dtype)
+
+
+def head_body(
+    layer_input,
+    queries,
+    key_rows,
+    value_rows,
+    context,
+    grad_context,
+    grad_output,
+    earlier_mass,
+    grad_queries,
+    grad_keys,
+    grad_values,
+    documents,
+    weights,
+    row_factor,
+    column_factor,
+):
+    blocks = lax.axis_size("blk")
+    data_count = lax.axis_size("dp")
+    block = lax.axis_index("blk")
+    data = lax.axis_index("dp")
+    core = data % 2
+    chip = data // 2
+    rows = queries.shape[1]
+    units = queries.shape[2]
+    features = layer_input.shape[2]
+    head_size = units // blocks
+    width = units // data_count
+    vmem = pl.BlockSpec(memory_space=pltpu.VMEM)
+    smem = pl.BlockSpec(memory_space=pltpu.SMEM)
+    place = jnp.stack([block, chip, core])
+
+    def call(kernel, shapes, *arrays, scratch=(), read=vmem, mib=10):
+        return pl.pallas_call(
+            kernel,
+            out_shape=shapes,
+            in_specs=[smem] + [read] * len(arrays),
+            out_specs=[vmem] * len(shapes),
+            scratch_shapes=list(scratch),
+            compiler_params=pltpu.CompilerParams(vmem_limit_bytes=mib * 2**20),
+        )(place, *arrays)
+
+    def low(*shape):
+        return jax.ShapeDtypeStruct(shape, jnp.bfloat16)
+
+    sent = call(
+        lambda *refs: pack_kernel(blocks, *refs),
+        [low(4 * rows + 16, head_size)] * blocks,
+        queries,
+        key_rows,
+        value_rows,
+        grad_context,
+        context,
+        earlier_mass,
+        documents,
+        scratch=[pltpu.VMEM((1, rows, units), jnp.bfloat16)] * 5
+        + [
+            pltpu.VMEM(earlier_mass.shape, jnp.float32),
+            pltpu.VMEM(documents.shape, jnp.int32),
+            pltpu.VMEM((128, rows), jnp.float32),
+            pltpu.SemaphoreType.DMA((7,)),
+        ],
+        read=pl.BlockSpec(memory_space=pltpu.HBM),
+        mib=58,
+    )
+    packs = [sent[0]] + [None] * (blocks - 1)
+    for step in range(1, blocks):
+        packs[blocks - step] = rotated(sent[step], step)
+
+    turned = layer_input[0].T
+    mid = features // 2
+    beside, below = swapped(turned, 2), swapped(turned, 4)
+    upper = swapped(beside[:mid], 4)
+    lower = swapped(below[mid:], 2)
+
+    part_output = jnp.einsum(
+        "th,td->dh", context[0], grad_output[0], preferred_element_type=jnp.float32
+    ).astype(jnp.bfloat16)
+
+    def columns_for(core_index):
+        return jnp.stack(
+            [
+                lax.dynamic_slice(part_output, (0, (2 * g + core_index) * width), (features, width))
+                for g in range(blocks)
+            ]
+        )
+
+    chip_output = (
+        columns_for(core).astype(jnp.float32)
+        + swapped(columns_for(1 - core), 1).astype(jnp.float32)
+    ).astype(jnp.bfloat16)
+    output_sum = lax.dynamic_index_in_dim(chip_output, chip, 0, False).astype(jnp.float32)
+    for m in range(2, data_count, 2):
+        output_sum = output_sum + swapped(
+            lax.dynamic_index_in_dim(chip_output, chip ^ (m // 2), 0, False), m
+        ).astype(jnp.float32)
+
+    steps = call(
+        lambda *refs: head_kernel(blocks, *refs),
+        [low(rows, head_size)] * (3 * blocks),
+        *packs,
+        scratch=[pltpu.VMEM((blocks, 2, rows, rows), jnp.bfloat16)] * 2,
+    )
+    output_pieces = output_sum.reshape(blocks, features // blocks, width)
+    totals = {"o": lax.dynamic_index_in_dim(output_pieces, block, 0, False)}
+    for step in range(1, blocks):
+        piece = lax.dynamic_index_in_dim(output_pieces, (block + step) % blocks, 0, False)
+        piece = rotated(piece.astype(jnp.bfloat16), step)
+        totals["o"] = totals["o"] + piece.astype(jnp.float32)
+    for g, (name, earlier) in enumerate(
+        (("v", grad_values), ("k", grad_keys), ("q", grad_queries))
+    ):
+        made = steps[g * blocks : (g + 1) * blocks]
+        parts = [made[0]] + [rotated(made[step], step) for step in range(1, blocks)]
+        rights = call(
+            lambda *refs: gather_kernel(blocks, *refs),
+            [low(rows, head_size)] * blocks,
+            *parts,
+            earlier,
+        )
+        rights = [rights[0]] + [swapped(rights[index], 2 * index) for index in range(1, blocks)]
+        keep, send = call(
+            lambda *refs: weight_kernel(blocks, *refs),
+            [jax.ShapeDtypeStruct((features, width), jnp.float32), low(features, width)],
+            turned,
+            beside,
+            below,
+            upper,
+            lower,
+            *rights,
+        )
+        other = swapped(send, 1)
+        shape = (features // blocks, width)
+        shares = call(
+            lambda *refs: share_kernel(blocks, *refs),
+            [jax.ShapeDtypeStruct(shape, jnp.float32)] + [low(*shape)] * (blocks - 1),
+            keep,
+            other,
+        )
+        totals[name] = shares[0]
+        for step in range(1, blocks):
+            piece = rotated(shares[step], step)
+            totals[name] = totals[name] + piece.astype(jnp.float32)
+    all_tokens = data_count * blocks * rows
+    gradient = jnp.stack([totals[name] for name in "qkvo"]) / all_tokens
+    return factored_update(gradient, weights, row_factor, column_factor, blocks, data_count)
+
+
+def factored_update(gradient, weights, row_factor, column_factor, blocks, data_count):
+    matrices = gradient.shape[0]
+    full_rows = gradient.shape[1] * blocks
+    full_cols = gradient.shape[2] * data_count
+    lanes = gradient.shape[2]
+    squares = gradient * gradient + tiny_square
+    row_part = jnp.sum(squares, axis=2)
+    factor_part = jnp.sum(row_factor, axis=1, keepdims=True)
+    factor_part = jnp.broadcast_to(factor_part, (matrices, lanes))
+    sent = jnp.concatenate([jnp.sum(squares, axis=1), factor_part], axis=1)
+    along = sent
+    for step in range(1, blocks):
+        along = along + rotated(sent, step)
+    col_sum, factor_sum = along[:, :lanes], along[:, lanes]
+    new_column_factor = beta_two * column_factor + (1.0 - beta_two) * col_sum / full_rows
+    both = jnp.broadcast_to(jnp.sum(col_sum, axis=1, keepdims=True), (matrices, lanes))
+    both = jnp.concatenate([row_part, both], axis=1)
+    chips = both
+    for m in range(2, data_count, 2):
+        chips = chips + swapped(both, m)
+    chips = chips + swapped(chips, 1)
+    row_sum, all_sum = chips[:, :-lanes], chips[:, -1]
+    new_row_factor = beta_two * row_factor + (1.0 - beta_two) * row_sum / full_cols
+    row_mean = (beta_two * factor_sum + (1.0 - beta_two) * all_sum / full_cols) / full_rows
+    second = new_row_factor[:, :, None] * new_column_factor[:, None, :] / row_mean[:, None, None]
+    new_weights = weights - learn_rate * gradient * lax.rsqrt(second)
+    return (new_weights, new_row_factor, new_column_factor)
+
+
+def chosen_body(*arrays):
+    blocks = lax.axis_size("blk")
+    data_count = lax.axis_size("dp")
+    heads = arrays[7].shape[1]
+    rows, units = arrays[1].shape[1:]
+    head_size = units // heads
+    if heads == blocks == 4 and data_count == 2 * blocks and rows == head_size and rows % 128 == 0:
+        return head_body(*arrays)
+    return ring_body(*arrays)
+
+
 def solution(mesh):
     placed = (
         P("dp", "blk", None),
@@ -175,7 +545,7 @@
         P(None, "dp"),
     )
     return jax.shard_map(
-        body,
+        chosen_body,
         mesh=mesh,
         in_specs=placed,
         out_specs=(P(None, "blk", "dp"), P(None, "blk"), P(None, "dp")),

time: 331 us -> 220 us (0.66)
  waiting for transfers between devices: 232 us -> 106 us
  starting transfers between devices: 12.1 us -> 59 us
  Pallas kernels: 0 us -> 25.1 us
  blocking collectives: 23.7 us -> 0 us
  between operations: 14.4 us -> 1.05 us
  matrix products: 14 us -> 4.32 us
  other arithmetic: 20.1 us -> 10.7 us
    reduce_scatter x2 -> x0, waiting for transfers between devices: 161 us -> none  [the longest x1 116 us: body(): lax.psum_scatter(jnp.concatenate([part_inner, part_output[:, None, :]], a...]
    ppermute x10 -> x51, starting transfers between devices: 12 us -> 59 us  [the longest x27 40.6 us: rotated(): return lax.ppermute(value, 'blk', pairs)]
    ppermute x10 -> x51, waiting for transfers between devices: 70.3 us -> 106 us  [the longest x27 78.2 us: rotated(): return lax.ppermute(value, 'blk', pairs)]
    pallas_call x0 -> x11, Pallas kernels: none -> 25.1 us  [call(): pl.pallas_call(kernel, out_shape=shapes, in_specs=[smem] + [read] * len(a...]
    psum x2 -> x0, blocking collectives: 23.7 us -> none  [the longest x1 13.5 us: body(): row_sum = lax.psum(row_part, 'dp')]
    concatenate x4 -> x2, other arithmetic: 14.6 us -> 0.01 us  [the longest x1 0.01 us: factored_update(): both = jnp.concatenate([row_part, both], axis=1)]
    dot_general x7 -> x1, matrix products: 14 us -> 4.32 us  [head_body(): jnp.einsum('th,td->dh', context[0], grad_output[0], preferred_element_typ...]
    unnamed x45 -> x61, local copies, waits for them, and re-layouts: 10.9 us -> 6.4 us
  transfers between devices with their start and end apart: 12 -> 51, of which waited for: 9 -> 25; matrix products, arithmetic and copies ran while one was open for 6% -> 9% of each run, Pallas kernels for 0% -> 11%
where the time goes in v1:
time: 220 us; the launch traced here: 219 us
  waiting for transfers between devices  106 us (48%)
  starting transfers between devices  59 us (27%)
  Pallas kernels  25.1 us (11%)
  local copies, waits for them, and re-layouts  12.6 us (6%)
  other arithmetic  10.7 us (5%)
  matrix products  4.32 us (2%)
    ppermute x27, waiting for transfers between devices, rotated(): return lax.ppermute(value, 'blk', pairs)  78.2 us
    ppermute x27, starting transfers between devices, rotated(): return lax.ppermute(value, 'blk', pairs)  40.6 us
    ppermute x24, waiting for transfers between devices, swapped(): lax.ppermute(value, 'dp', [(source, source ^ mask) for source in range(co...  28.2 us
    pallas_call x11, Pallas kernels, call(): pl.pallas_call(kernel, out_shape=shapes, in_specs=[smem] + [read] * len(a...  25.1 us
    ppermute x24, starting transfers between devices, swapped(): lax.ppermute(value, 'dp', [(source, source ^ mask) for source in range(co...  18.4 us
    unnamed x61, local copies, waits for them, and re-layouts  6.4 us
  transfers between devices with their start and end apart: 51, of which 25 were waited for; matrix products, arithmetic and copies ran while one was open for 9% of the time, Pallas kernels for 11%

profile of v1, /device:TPU:0, one launch (start us, length us, event | category | flops | bytes accessed | tf_op | source)
XLA Modules:
  0.0 219.2 jit_solution(7272028268854216023)
XLA Ops:
  2.2 3.0 %collective-permute-start = (bf16[2048,256]{1,0:T(8,128)(2,1)S(1)}, bf16[2048,256]{1,0:T(8,128)(2,1)S(1)}, u32[]{:S(2)}, u32[]{:S(2)}) collective-permute-start(bf16[2048,256]{1,0:T(8,128)(2,1)S(1)} %bitcast.60), channel_id=1, source_target_pairs={{0,8},{4,12},{8,0},{12,4},{16,24},{20,28},{24,16},{28,20},{1,9},{5... | collective-permute-start | bytes 3145736 | tf_op jit(solution)/shard_map/ppermute | solution.py:164
  7.4 4.1 %shard_map.166 = (bf16[1040,256]{1,0:T(8,128)(2,1)}, bf16[1040,256]{1,0:T(8,128)(2,1)}, bf16[1040,256]{1,0:T(8,128)(2,1)}, bf16[1040,256]{1,0:T(8,128)(2,1)}) custom-call(s32[3]{0:T(128)} %pad_add_fusion.refs_0_, bf16[1,256,1024]{2,1,0:T(8,128)(2,1)} %refs_1_.1, bf16[1,256,1024]{2,1,0:T(8,128)(2,1)} %refs_2_.1, bf16[1,256,1024]{2,1,0:T(8,128)(2,1)} %refs_3_.1, ...), custom_call_target="tpu_custom_call" | custom-call | tf_op jit(solution)/shard_map/pallas_call | solution.py:374
  11.6 3.7 %collective-permute-start.4 = (bf16[1040,256]{1,0:T(8,128)(2,1)}, bf16[1040,256]{1,0:T(8,128)(2,1)}, u32[]{:S(2)}, u32[]{:S(2)}) collective-permute-start(bf16[1040,256]{1,0:T(8,128)(2,1)} %get-tuple-element.50), channel_id=1, source_target_pairs={{0,3},{1,0},{2,1},{3,2},{4,7},{5,4},{6,5},{7,6},{8,11},{9,8},{10,9... | collective-permute-start | bytes 1597448 | tf_op jit(solution)/shard_map/ppermute | solution.py:170
  15.2 4.3 %convolution_convert_fusion = bf16[2048,1024]{1,0:T(8,128)(2,1)} fusion(bf16[1,256,2048]{2,1,0:T(8,128)(2,1)S(1)} %copy-done, bf16[1,256,1024]{2,1,0:T(8,128)(2,1)} %refs_5_.4), kind=kOutput, calls=%fused_computation.1 | convolution fusion | flops 1075838976 | bytes 5767168 | tf_op jit(solution)/shard_map/th,td->dh/dot_general | solution.py:416
  19.5 3.7 %dynamic-slice_bitcast_fusion.10 = (bf16[1,2048,128]{2,1,0:T(8,128)(2,1)}, bf16[1,2048,128]{2,1,0:T(8,128)(2,1)S(1)}, bf16[1,2048,128]{2,1,0:T(8,128)(2,1)S(1)},...) fusion(bf16[2048,1024]{1,0:T(8,128)(2,1)} %convolution_convert_, ...), kind=kLoop, calls=%fused_computation.23 | loop fusion | bytes 8388640 | tf_op jit(solution)/shard_map/stack | solution.py:421
  26.8 34.6 %collective-permute-done.5.refs_3_ = bf16[1040,256]{1,0:T(8,128)(2,1)S(1)} collective-permute-done((bf16[1040,256]{1,0:T(8,128)(2,1)S(1)}, bf16[1040,256]{1,0:T(8,128)(2,1)S(1)}, u32[]{:S(2)}, u32[]{:S(2)}) %collective-permute-start.5) | collective-permute-done | bytes 532512 | tf_op jit(solution)/shard_map/ppermute | solution.py:170
  61.4 4.8 %shard_map.167 = (bf16[256,256]{1,0:T(8,128)(2,1)S(1)}, bf16[256,256]{1,0:T(8,128)(2,1)S(1)}, bf16[256,256]{1,0:T(8,128)(2,1)S(1)}, bf16[256,256]{1,0:T(8,128)(2...) custom-call(s32[3]{0:T(128)S(1)} %copy-done.15, ...), custom_call_target="tpu_custom_call" | custom-call | tf_op jit(solution)/shard_map/pallas_call | solution.py:374
  75.0 4.2 %collective-permute-done.28.refs_3_ = bf16[256,256]{1,0:T(8,128)(2,1)S(1)} collective-permute-done((bf16[256,256]{1,0:T(8,128)(2,1)S(1)}, bf16[256,256]{1,0:T(8,128)(2,1)S(1)}, u32[]{:S(2)}, u32[]{:S(2)}) %collective-permute-start.28) | collective-permute-done | bytes 131104 | tf_op jit(solution)/shard_map/ppermute | solution.py:170
  81.1 3.4 %collective-permute-start.18 = (bf16[256,256]{1,0:T(8,128)(2,1)S(1)}, bf16[256,256]{1,0:T(8,128)(2,1)S(1)}, u32[]{:S(2)}, u32[]{:S(2)}) collective-permute-start(bf16[256,256]{1,0:T(8,128)(2,1)S(1)} %get-tuple-element.69), channel_id=1, source_target_pairs={{0,2},{1,3},{2,0},{3,1},{4,6},{5,7},{6,4},{7,5},{8,10},{9,11},{10,... | collective-permute-start | bytes 393224 | tf_op jit(solution)/shard_map/ppermute | solution.py:170
  89.1 3.0 %collective-permute-done.18.refs_3_ = bf16[256,256]{1,0:T(8,128)(2,1)S(1)} collective-permute-done((bf16[256,256]{1,0:T(8,128)(2,1)S(1)}, bf16[256,256]{1,0:T(8,128)(2,1)S(1)}, u32[]{:S(2)}, u32[]{:S(2)}) %collective-permute-start.18) | collective-permute-done | bytes 131104 | tf_op jit(solution)/shard_map/ppermute | solution.py:170
  93.9 3.5 %collective-permute-done.30.refs_7_ = bf16[256,256]{1,0:T(8,128)(2,1)S(1)} collective-permute-done((bf16[256,256]{1,0:T(8,128)(2,1)S(1)}, bf16[256,256]{1,0:T(8,128)(2,1)S(1)}, u32[]{:S(2)}, u32[]{:S(2)}) %collective-permute-start.30) | collective-permute-done | bytes 131104 | tf_op jit(solution)/shard_map/ppermute | solution.py:164
  100.2 4.0 %collective-permute-done.32.refs_9_ = bf16[256,256]{1,0:T(8,128)(2,1)S(1)} collective-permute-done((bf16[256,256]{1,0:T(8,128)(2,1)S(1)}, bf16[256,256]{1,0:T(8,128)(2,1)S(1)}, u32[]{:S(2)}, u32[]{:S(2)}) %collective-permute-start.32) | collective-permute-done | bytes 131104 | tf_op jit(solution)/shard_map/ppermute | solution.py:164
  107.1 3.3 %shard_map.175 = (f32[2048,128]{1,0:T(8,128)S(1)}, bf16[2048,128]{1,0:T(8,128)(2,1)}) custom-call(s32[3]{0:T(128)S(1)} %copy-done.15, bf16[2048,256]{1,0:T(8,128)(2,1)S(1)} %bitcast.62, bf16[2048,256]{1,0:T(8,128)(2,1)S(1)} %collective-permute-done.refs_2_, bf16[2048,256]{1,0:T(8,128)(2,1)} %collective-permute-done.1.refs_3_, ...), custom_call_target="tpu_custom_call" | custom-call | tf_op jit(solution)/shard_map/pallas_call | solution.py:374
  111.5 3.4 %shard_map.172 = (f32[2048,128]{1,0:T(8,128)S(1)}, bf16[2048,128]{1,0:T(8,128)(2,1)}) custom-call(s32[3]{0:T(128)S(1)} %copy-done.15, bf16[2048,256]{1,0:T(8,128)(2,1)S(1)} %bitcast.63, bf16[2048,256]{1,0:T(8,128)(2,1)S(1)} %collective-permute-done.refs_2_, bf16[2048,256]{1,0:T(8,128)(2,1)} %collective-permute-done.1.refs_3_, ...), custom_call_target="tpu_custom_call" | custom-call | tf_op jit(solution)/shard_map/pallas_call | solution.py:374
  115.4 5.0 %collective-permute-start.8 = (bf16[256,256]{1,0:T(8,128)(2,1)S(1)}, bf16[256,256]{1,0:T(8,128)(2,1)S(1)}, u32[]{:S(2)}, u32[]{:S(2)}) collective-permute-start(bf16[256,256]{1,0:T(8,128)(2,1)S(1)} %get-tuple-element.55), channel_id=1, source_target_pairs={{0,2},{1,3},{2,0},{3,1},{4,6},{5,7},{6,4},{7,5},{8,10},{9,11},{10,... | collective-permute-start | bytes 393224 | tf_op jit(solution)/shard_map/ppermute | solution.py:170
  120.4 6.2 %collective-permute-done.8.refs_3_ = bf16[256,256]{1,0:T(8,128)(2,1)S(1)} collective-permute-done((bf16[256,256]{1,0:T(8,128)(2,1)S(1)}, bf16[256,256]{1,0:T(8,128)(2,1)S(1)}, u32[]{:S(2)}, u32[]{:S(2)}) %collective-permute-start.8) | collective-permute-done | bytes 131104 | tf_op jit(solution)/shard_map/ppermute | solution.py:170
  130.0 4.9 %collective-permute-done.10.refs_7_ = bf16[256,256]{1,0:T(8,128)(2,1)S(1)} collective-permute-done((bf16[256,256]{1,0:T(8,128)(2,1)S(1)}, bf16[256,256]{1,0:T(8,128)(2,1)S(1)}, u32[]{:S(2)}, u32[]{:S(2)}) %collective-permute-start.10) | collective-permute-done | bytes 131104 | tf_op jit(solution)/shard_map/ppermute | solution.py:164
  135.1 5.9 %collective-permute-done.12.refs_9_ = bf16[256,256]{1,0:T(8,128)(2,1)} collective-permute-done((bf16[256,256]{1,0:T(8,128)(2,1)}, bf16[256,256]{1,0:T(8,128)(2,1)}, u32[]{:S(2)}, u32[]{:S(2)}) %collective-permute-start.12) | collective-permute-done | bytes 131104 | tf_op jit(solution)/shard_map/ppermute | solution.py:164
  148.1 3.8 %collective-permute-start.36 = (bf16[512,128]{1,0:T(8,128)(2,1)S(1)}, bf16[512,128]{1,0:T(8,128)(2,1)S(1)}, u32[]{:S(2)}, u32[]{:S(2)}) collective-permute-start(bf16[512,128]{1,0:T(8,128)(2,1)S(1)} %get-tuple-element.94), channel_id=1, source_target_pairs={{0,3},{1,0},{2,1},{3,2},{4,7},{5,4},{6,5},{7,6},{8,11},{9,8},{10,9... | collective-permute-start | bytes 393224 | tf_op jit(solution)/shard_map/ppermute | solution.py:170
  154.4 3.2 %collective-permute-start.26 = (bf16[512,128]{1,0:T(8,128)(2,1)}, bf16[512,128]{1,0:T(8,128)(2,1)}, u32[]{:S(2)}, u32[]{:S(2)}) collective-permute-start(bf16[512,128]{1,0:T(8,128)(2,1)} %get-tuple-element.80), channel_id=1, source_target_pairs={{0,3},{1,0},{2,1},{3,2},{4,7},{5,4},{6,5},{7,6},{8,11},{9,8},{10,9... | collective-permute-start | bytes 393224 | tf_op jit(solution)/shard_map/ppermute | solution.py:170
  170.3 7.6 %collective-permute-done.25 = bf16[512,128]{1,0:T(8,128)(2,1)S(1)} collective-permute-done((bf16[512,128]{1,0:T(8,128)(2,1)S(1)}, bf16[512,128]{1,0:T(8,128)(2,1)S(1)}, u32[]{:S(2)}, u32[]{:S(2)}) %collective-permute-start.25) | collective-permute-done | bytes 131104 | tf_op jit(solution)/shard_map/ppermute | solution.py:170
  181.0 5.9 %collective-permute-done.39 = bf16[2048,128]{1,0:T(8,128)(2,1)} collective-permute-done((bf16[2048,128]{1,0:T(8,128)(2,1)}, bf16[2048,128]{1,0:T(8,128)(2,1)}, u32[]{:S(2)}, u32[]{:S(2)}) %collective-permute-start.39) | collective-permute-done | bytes 524320 | tf_op jit(solution)/shard_map/ppermute | solution.py:164
  191.7 3.6 %collective-permute-done.43 = bf16[512,128]{1,0:T(8,128)(2,1)S(1)} collective-permute-done((bf16[512,128]{1,0:T(8,128)(2,1)S(1)}, bf16[512,128]{1,0:T(8,128)(2,1)S(1)}, u32[]{:S(2)}, u32[]{:S(2)}) %collective-permute-start.43) | collective-permute-done | bytes 131104 | tf_op jit(solution)/shard_map/ppermute | solution.py:170
  195.3 6.5 %collective-permute-done.42 = bf16[512,128]{1,0:T(8,128)(2,1)S(1)} collective-permute-done((bf16[512,128]{1,0:T(8,128)(2,1)S(1)}, bf16[512,128]{1,0:T(8,128)(2,1)S(1)}, u32[]{:S(2)}, u32[]{:S(2)}) %collective-permute-start.42) | collective-permute-done | bytes 131104 | tf_op jit(solution)/shard_map/ppermute | solution.py:170
  (177 shorter events, 82.7 us)
Async XLA Ops:
  2.2 66.6 %collective-permute-start = (bf16[2048,256]{1,0:T(8,128)(2,1)S(1)}, bf16[2048,256]{1,0:T(8,128)(2,1)S(1)}, u32[]{:S(2)}, u32[]{:S(2)}) collective-permute-start(bf16[2048,256]{1,0:T(8,128)(2,1)S(1)} %bitcast.60), channel_id=1, source_target_pairs={{0,8},{4,12},{8,0},{12,4},{16,24},{20,28},{24,16},{28,20},{1,9},{5... | collective-permute-start | bytes 3145736 | tf_op jit(solution)/shard_map/ppermute | solution.py:164
  5.3 66.5 %collective-permute-start.1 = (bf16[2048,256]{1,0:T(8,128)(2,1)S(1)}, bf16[2048,256]{1,0:T(8,128)(2,1)}, u32[]{:S(2)}, u32[]{:S(2)}) collective-permute-start(bf16[2048,256]{1,0:T(8,128)(2,1)S(1)} %bitcast.61), channel_id=1, source_target_pairs={{0,16},{4,20},{8,24},{12,28},{16,0},{20,4},{24,8},{28,12},{1,17},{... | collective-permute-start | bytes 3145736 | tf_op jit(solution)/shard_map/ppermute | solution.py:164
  11.6 15.2 %collective-permute-start.4 = (bf16[1040,256]{1,0:T(8,128)(2,1)}, bf16[1040,256]{1,0:T(8,128)(2,1)}, u32[]{:S(2)}, u32[]{:S(2)}) collective-permute-start(bf16[1040,256]{1,0:T(8,128)(2,1)} %get-tuple-element.50), channel_id=1, source_target_pairs={{0,3},{1,0},{2,1},{3,2},{4,7},{5,4},{6,5},{7,6},{8,11},{9,8},{10,9... | collective-permute-start | bytes 1597448 | tf_op jit(solution)/shard_map/ppermute | solution.py:170
  24.9 129.4 %collective-permute-start.37 = (bf16[4,2048,128]{2,1,0:T(8,128)(2,1)}, bf16[4,2048,128]{2,1,0:T(8,128)(2,1)}, u32[]{:S(2)}, u32[]{:S(2)}) collective-permute-start(bf16[4,2048,128]{2,1,0:T(8,128)(2,1)} %pad_maximum_fusion), channel_id=1, source_target_pairs={{0,4},{4,0},{8,12},{12,8},{16,20},{20,16},{24,28},{28,24},{1,5},{5... | collective-permute-start | bytes 6291464 | tf_op jit(solution)/shard_map/ppermute | solution.py:164
  24.9 36.4 %collective-permute-start.5 = (bf16[1040,256]{1,0:T(8,128)(2,1)S(1)}, bf16[1040,256]{1,0:T(8,128)(2,1)S(1)}, u32[]{:S(2)}, u32[]{:S(2)}) collective-permute-start(bf16[1040,256]{1,0:T(8,128)(2,1)S(1)} %copy-done.29), channel_id=1, source_target_pairs={{0,2},{1,3},{2,0},{3,1},{4,6},{5,7},{6,4},{7,5},{8,10},{9,11},{10,... | collective-permute-start | bytes 1597448 | tf_op jit(solution)/shard_map/ppermute | solution.py:170
  26.7 34.6 %collective-permute-start.6 = (bf16[1040,256]{1,0:T(8,128)(2,1)S(1)}, bf16[1040,256]{1,0:T(8,128)(2,1)S(1)}, u32[]{:S(2)}, u32[]{:S(2)}) collective-permute-start(bf16[1040,256]{1,0:T(8,128)(2,1)S(1)} %copy-done.28), channel_id=1, source_target_pairs={{0,1},{1,2},{2,3},{3,0},{4,5},{5,6},{6,7},{7,4},{8,9},{9,10},{10,1... | collective-permute-start | bytes 1597448 | tf_op jit(solution)/shard_map/ppermute | solution.py:170
  66.8 12.4 %collective-permute-start.28 = (bf16[256,256]{1,0:T(8,128)(2,1)S(1)}, bf16[256,256]{1,0:T(8,128)(2,1)S(1)}, u32[]{:S(2)}, u32[]{:S(2)}) collective-permute-start(bf16[256,256]{1,0:T(8,128)(2,1)S(1)} %get-tuple-element.83), channel_id=1, source_target_pairs={{0,2},{1,3},{2,0},{3,1},{4,6},{5,7},{6,4},{7,5},{8,10},{9,11},{10,... | collective-permute-start | bytes 393224 | tf_op jit(solution)/shard_map/ppermute | solution.py:170
  71.7 33.1 %collective-permute-start.2 = (bf16[1024,256]{1,0:T(8,128)(2,1)S(1)}, bf16[1024,256]{1,0:T(8,128)(2,1)S(1)}, u32[]{:S(2)}, u32[]{:S(2)}) collective-permute-start(bf16[1024,256]{1,0:T(8,128)(2,1)S(1)} %slice.24), channel_id=1, source_target_pairs={{0,16},{4,20},{8,24},{12,28},{16,0},{20,4},{24,8},{28,12},{1,17},{... | collective-permute-start | bytes 1572872 | tf_op jit(solution)/shard_map/ppermute | solution.py:164
  74.5 32.1 %collective-permute-start.3 = (bf16[1024,256]{1,0:T(8,128)(2,1)S(1)}, bf16[1024,256]{1,0:T(8,128)(2,1)S(1)}, u32[]{:S(2)}, u32[]{:S(2)}) collective-permute-start(bf16[1024,256]{1,0:T(8,128)(2,1)S(1)} %slice.25), channel_id=1, source_target_pairs={{0,8},{4,12},{8,0},{12,4},{16,24},{20,28},{24,16},{28,20},{1,9},{5... | collective-permute-start | bytes 1572872 | tf_op jit(solution)/shard_map/ppermute | solution.py:164
  98.7 12.7 %collective-permute-start.20 = (bf16[256,256]{1,0:T(8,128)(2,1)S(1)}, bf16[256,256]{1,0:T(8,128)(2,1)S(1)}, u32[]{:S(2)}, u32[]{:S(2)}) collective-permute-start(bf16[256,256]{1,0:T(8,128)(2,1)S(1)} %get-tuple-element.72), channel_id=1, source_target_pairs={{0,8},{4,12},{8,0},{12,4},{16,24},{20,28},{24,16},{28,20},{1,9},{5... | collective-permute-start | bytes 393224 | tf_op jit(solution)/shard_map/ppermute | solution.py:164
  106.6 13.8 %collective-permute-start.7 = (bf16[256,256]{1,0:T(8,128)(2,1)S(1)}, bf16[256,256]{1,0:T(8,128)(2,1)S(1)}, u32[]{:S(2)}, u32[]{:S(2)}) collective-permute-start(bf16[256,256]{1,0:T(8,128)(2,1)S(1)} %get-tuple-element.54), channel_id=1, source_target_pairs={{0,1},{1,2},{2,3},{3,0},{4,5},{5,6},{6,7},{7,4},{8,9},{9,10},{10,1... | collective-permute-start | bytes 393224 | tf_op jit(solution)/shard_map/ppermute | solution.py:170
  111.4 35.4 %collective-permute-start.33 = (bf16[2048,128]{1,0:T(8,128)(2,1)}, bf16[2048,128]{1,0:T(8,128)(2,1)}, u32[]{:S(2)}, u32[]{:S(2)}) collective-permute-start(bf16[2048,128]{1,0:T(8,128)(2,1)} %get-tuple-element.90), channel_id=1, source_target_pairs={{0,4},{4,0},{8,12},{12,8},{16,20},{20,16},{24,28},{28,24},{1,5},{5... | collective-permute-start | bytes 1572872 | tf_op jit(solution)/shard_map/ppermute | solution.py:164
  114.9 37.1 %collective-permute-start.23 = (bf16[2048,128]{1,0:T(8,128)(2,1)}, bf16[2048,128]{1,0:T(8,128)(2,1)}, u32[]{:S(2)}, u32[]{:S(2)}) collective-permute-start(bf16[2048,128]{1,0:T(8,128)(2,1)} %get-tuple-element.76), channel_id=1, source_target_pairs={{0,4},{4,0},{8,12},{12,8},{16,20},{20,16},{24,28},{28,24},{1,5},{5... | collective-permute-start | bytes 1572872 | tf_op jit(solution)/shard_map/ppermute | solution.py:164
  146.8 14.3 %collective-permute-start.13 = (bf16[2048,128]{1,0:T(8,128)(2,1)S(1)}, bf16[2048,128]{1,0:T(8,128)(2,1)S(1)}, u32[]{:S(2)}, u32[]{:S(2)}) collective-permute-start(bf16[2048,128]{1,0:T(8,128)(2,1)S(1)} %get-tuple-element.62), channel_id=1, source_target_pairs={{0,4},{4,0},{8,12},{12,8},{16,20},{20,16},{24,28},{28,24},{1,5},{5... | collective-permute-start | bytes 1572872 | tf_op jit(solution)/shard_map/ppermute | solution.py:164
  148.1 14.7 %collective-permute-start.36 = (bf16[512,128]{1,0:T(8,128)(2,1)S(1)}, bf16[512,128]{1,0:T(8,128)(2,1)S(1)}, u32[]{:S(2)}, u32[]{:S(2)}) collective-permute-start(bf16[512,128]{1,0:T(8,128)(2,1)S(1)} %get-tuple-element.94), channel_id=1, source_target_pairs={{0,3},{1,0},{2,1},{3,2},{4,7},{5,4},{6,5},{7,6},{8,11},{9,8},{10,9... | collective-permute-start | bytes 393224 | tf_op jit(solution)/shard_map/ppermute | solution.py:170
  151.9 12.6 %collective-permute-start.35 = (bf16[512,128]{1,0:T(8,128)(2,1)S(1)}, bf16[512,128]{1,0:T(8,128)(2,1)S(1)}, u32[]{:S(2)}, u32[]{:S(2)}) collective-permute-start(bf16[512,128]{1,0:T(8,128)(2,1)S(1)} %get-tuple-element.93), channel_id=1, source_target_pairs={{0,2},{1,3},{2,0},{3,1},{4,6},{5,7},{6,4},{7,5},{8,10},{9,11},{10,... | collective-permute-start | bytes 393224 | tf_op jit(solution)/shard_map/ppermute | solution.py:170
  151.9 14.8 %collective-permute-start.34 = (bf16[512,128]{1,0:T(8,128)(2,1)S(1)}, bf16[512,128]{1,0:T(8,128)(2,1)}, u32[]{:S(2)}, u32[]{:S(2)}) collective-permute-start(bf16[512,128]{1,0:T(8,128)(2,1)S(1)} %get-tuple-element.92), channel_id=1, source_target_pairs={{0,1},{1,2},{2,3},{3,0},{4,5},{5,6},{6,7},{7,4},{8,9},{9,10},{10,1... | collective-permute-start | bytes 393224 | tf_op jit(solution)/shard_map/ppermute | solution.py:170
  154.4 14.9 %collective-permute-start.26 = (bf16[512,128]{1,0:T(8,128)(2,1)}, bf16[512,128]{1,0:T(8,128)(2,1)}, u32[]{:S(2)}, u32[]{:S(2)}) collective-permute-start(bf16[512,128]{1,0:T(8,128)(2,1)} %get-tuple-element.80), channel_id=1, source_target_pairs={{0,3},{1,0},{2,1},{3,2},{4,7},{5,4},{6,5},{7,6},{8,11},{9,8},{10,9... | collective-permute-start | bytes 393224 | tf_op jit(solution)/shard_map/ppermute | solution.py:170
  161.1 18.1 %collective-permute-start.40 = (bf16[2048,128]{1,0:T(8,128)(2,1)}, bf16[2048,128]{1,0:T(8,128)(2,1)}, u32[]{:S(2)}, u32[]{:S(2)}) collective-permute-start(bf16[2048,128]{1,0:T(8,128)(2,1)} %get-tuple-element.106), channel_id=1, source_target_pairs={{0,24},{4,28},{8,16},{12,20},{16,8},{20,12},{24,0},{28,4},{1,25},{... | collective-permute-start | bytes 1572872 | tf_op jit(solution)/shard_map/ppermute | solution.py:164
  162.8 24.0 %collective-permute-start.39 = (bf16[2048,128]{1,0:T(8,128)(2,1)}, bf16[2048,128]{1,0:T(8,128)(2,1)}, u32[]{:S(2)}, u32[]{:S(2)}) collective-permute-start(bf16[2048,128]{1,0:T(8,128)(2,1)} %get-tuple-element.107), channel_id=1, source_target_pairs={{0,16},{4,20},{8,24},{12,28},{16,0},{20,4},{24,8},{28,12},{1,17},{... | collective-permute-start | bytes 1572872 | tf_op jit(solution)/shard_map/ppermute | solution.py:164
  165.2 21.7 %collective-permute-start.38 = (bf16[2048,128]{1,0:T(8,128)(2,1)}, bf16[2048,128]{1,0:T(8,128)(2,1)}, u32[]{:S(2)}, u32[]{:S(2)}) collective-permute-start(bf16[2048,128]{1,0:T(8,128)(2,1)} %get-tuple-element.105), channel_id=1, source_target_pairs={{0,8},{4,12},{8,0},{12,4},{16,24},{20,28},{24,16},{28,20},{1,9},{5... | collective-permute-start | bytes 1572872 | tf_op jit(solution)/shard_map/ppermute | solution.py:164
  177.9 13.7 %collective-permute-start.15 = (bf16[512,128]{1,0:T(8,128)(2,1)S(1)}, bf16[512,128]{1,0:T(8,128)(2,1)S(1)}, u32[]{:S(2)}, u32[]{:S(2)}) collective-permute-start(bf16[512,128]{1,0:T(8,128)(2,1)S(1)} %get-tuple-element.65), channel_id=1, source_target_pairs={{0,2},{1,3},{2,0},{3,1},{4,6},{5,7},{6,4},{7,5},{8,10},{9,11},{10,... | collective-permute-start | bytes 393224 | tf_op jit(solution)/shard_map/ppermute | solution.py:170
  179.2 12.5 %collective-permute-start.14 = (bf16[512,128]{1,0:T(8,128)(2,1)S(1)}, bf16[512,128]{1,0:T(8,128)(2,1)S(1)}, u32[]{:S(2)}, u32[]{:S(2)}) collective-permute-start(bf16[512,128]{1,0:T(8,128)(2,1)S(1)} %get-tuple-element.64), channel_id=1, source_target_pairs={{0,1},{1,2},{2,3},{3,0},{4,5},{5,6},{6,7},{7,4},{8,9},{9,10},{10,1... | collective-permute-start | bytes 393224 | tf_op jit(solution)/shard_map/ppermute | solution.py:170
  189.3 12.4 %collective-permute-start.42 = (bf16[512,128]{1,0:T(8,128)(2,1)S(1)}, bf16[512,128]{1,0:T(8,128)(2,1)S(1)}, u32[]{:S(2)}, u32[]{:S(2)}) collective-permute-start(bf16[512,128]{1,0:T(8,128)(2,1)S(1)} %get-tuple-element.110), channel_id=1, source_target_pairs={{0,2},{1,3},{2,0},{3,1},{4,6},{5,7},{6,4},{7,5},{8,10},{9,11},{10,... | collective-permute-start | bytes 393224 | tf_op jit(solution)/shard_map/ppermute | solution.py:170
  (57 other events, 525.1 us)

commit v2 on v1

--- a/solution.py
+++ b/solution.py
@@ -168,6 +168,11 @@
     count = lax.axis_size("blk")
     pairs = [(source, (source + steps) % count) for source in range(count)]
     return lax.ppermute(value, "blk", pairs)
+
+
+def traded(value, mask):
+    count = lax.axis_size("blk")
+    return lax.ppermute(value, "blk", [(source, source ^ mask) for source in range(count)])
 
 
 def split_three(value):
@@ -213,52 +218,52 @@
         outs[step][4 * rows :] = side.astype(jnp.bfloat16)
 
 
-def head_kernel(blocks, place_ref, *refs):
-    packs = refs[:blocks]
-    value_outs, key_outs, query_outs = (
-        refs[(1 + index) * blocks : (2 + index) * blocks] for index in range(3)
-    )
-    weight_ref, slope_ref = refs[4 * blocks :]
+def times(left, right, left_dim, right_dim):
+    return lax.dot_general(
+        left,
+        right,
+        (((left_dim,), (right_dim,)), ((), ())),
+        preferred_element_type=jnp.float32,
+    )
+
+
+def side_of(pack_ref):
+    rows = (pack_ref.shape[0] - 16) // 4
+    side = pack_ref[4 * rows :].astype(jnp.float32)
+    return side[0:1] + side[1:2] + side[2:3], side[3:4] + side[4:5] + side[5:6], side[6:7]
+
+
+def part_of(pack_ref, index):
+    rows = (pack_ref.shape[0] - 16) // 4
+    return pack_ref[index * rows : (index + 1) * rows]
+
+
+def weigh_kernel(blocks, place_ref, *refs):
+    packs, outs, weight_ref = refs[:blocks], refs[blocks : 2 * blocks], refs[2 * blocks]
     rows = weight_ref.shape[2]
     half = rows // 2
     scale_factor = 1.0 / math.sqrt(packs[0].shape[1])
     local_down = lax.broadcasted_iota(jnp.int32, (rows, 1), 0)
     local_across = lax.broadcasted_iota(jnp.int32, (1, rows), 1)
+    line = lax.broadcasted_iota(jnp.int32, (8, rows), 0)
     block_of = [lax.rem(place_ref[0] + step, blocks) for step in range(blocks)]
-
-    def part_of(step, index):
-        return packs[step][index * rows : (index + 1) * rows]
 
     def positions(local, block):
         lower = block * half + local
         upper = (2 * blocks - 1 - block) * half + local - half
         return jnp.where(local < half, lower, upper)
 
-    def times(left, right, left_dim, right_dim):
-        return lax.dot_general(
-            left,
-            right,
-            (((left_dim,), (right_dim,)), ((), ())),
-            preferred_element_type=jnp.float32,
-        )
-
-    sides = []
     for step in range(blocks):
-        side = packs[step][4 * rows :].astype(jnp.float32)
-        mass = side[0:1] + side[1:2] + side[2:3]
-        row_dot = side[3:4] + side[4:5] + side[5:6]
-        sides.append((mass, row_dot, side[6:7]))
-    for step in range(blocks):
-        visited = [(step + 1) % blocks, (step + 2) % blocks]
-        line = lax.broadcasted_iota(jnp.int32, (8, rows), 0)
-        down = jnp.where(line == 0, sides[step][0], jnp.where(line == 1, sides[step][1], sides[step][2])).T
-        mass, row_dot, docs = down[:, 0:1], down[:, 1:2], down[:, 2:3]
+        mass, _, docs = side_of(packs[step])
+        down = jnp.where(line == 0, mass, docs).T
+        mass, docs = down[:, 0:1], down[:, 1:2]
         own_pos = positions(local_down, block_of[step])
         scored = []
-        for other in visited:
-            score = times(part_of(step, 0), part_of(other, 1), 1, 1) * scale_factor
+        for far in range(2):
+            other = (step + 1 + far) % blocks
+            score = times(part_of(packs[step], 0), part_of(packs[other], 1), 1, 1) * scale_factor
             allowed = (positions(local_across, block_of[other]) <= own_pos) & (
-                sides[other][2] == docs
+                side_of(packs[other])[2] == docs
             )
             scored.append(jnp.where(allowed, score, -jnp.inf))
         peak = mass
@@ -269,24 +274,38 @@
         for part in shifted:
             total = total + jnp.sum(part, axis=1, keepdims=True)
         inverse = 1.0 / total
+        for far in range(2):
+            weight_ref[step, far] = (shifted[far] * inverse).astype(weight_ref.dtype)
+    for step in range(blocks):
+        near, far = (step - 1) % blocks, (step - 2) % blocks
+        value_step = times(
+            weight_ref[near, 0].astype(jnp.bfloat16), part_of(packs[near], 3), 0, 0
+        ) + times(weight_ref[far, 1].astype(jnp.bfloat16), part_of(packs[far], 3), 0, 0)
+        outs[step][...] = value_step.astype(jnp.bfloat16)
+
+
+def slope_kernel(blocks, place_ref, weight_ref, *refs):
+    packs, key_outs, query_outs = (refs[n * blocks : (n + 1) * blocks] for n in range(3))
+    slope_ref = refs[3 * blocks]
+    rows = weight_ref.shape[2]
+    scale_factor = 1.0 / math.sqrt(packs[0].shape[1])
+    line = lax.broadcasted_iota(jnp.int32, (8, rows), 0)
+    for step in range(blocks):
+        row_dot = jnp.where(line == 0, side_of(packs[step])[1], 0.0).T[:, 0:1]
         query_step = None
-        for index, other in enumerate(visited):
-            attention = shifted[index] * inverse
-            grad_attention = times(part_of(step, 3), part_of(other, 2), 1, 1)
-            slope = (attention * (grad_attention - row_dot) * scale_factor).astype(jnp.bfloat16)
-            weight_ref[step, index] = attention.astype(jnp.bfloat16)
-            slope_ref[step, index] = slope
-            part = times(slope, part_of(other, 1), 1, 0)
+        for far in range(2):
+            other = (step + 1 + far) % blocks
+            grad_attention = times(part_of(packs[step], 3), part_of(packs[other], 2), 1, 1)
+            slope = weight_ref[step, far] * (grad_attention - row_dot) * scale_factor
+            slope = slope.astype(jnp.bfloat16)
+            slope_ref[step, far] = slope
+            part = times(slope, part_of(packs[other], 1), 1, 0)
             query_step = part if query_step is None else query_step + part
         query_outs[step][...] = query_step.astype(jnp.bfloat16)
     for step in range(blocks):
         near, far = (step - 1) % blocks, (step - 2) % blocks
-        value_step = times(weight_ref[near, 0], part_of(near, 3), 0, 0) + times(
-            weight_ref[far, 1], part_of(far, 3), 0, 0
-        )
-        value_outs[step][...] = value_step.astype(jnp.bfloat16)
-        key_step = times(slope_ref[near, 0], part_of(near, 0), 0, 0) + times(
-            slope_ref[far, 1], part_of(far, 0), 0, 0
+        key_step = times(slope_ref[near, 0], part_of(packs[near], 0), 0, 0) + times(
+            slope_ref[far, 1], part_of(packs[far], 0), 0, 0
         )
         key_outs[step][...] = key_step.astype(jnp.bfloat16)
 
@@ -325,17 +344,29 @@
             part = jnp.dot(left, right[...], preferred_element_type=jnp.float32)
             total = part if total is None else total + part
         first, second = total[:, :width], total[:, width:]
-        keep_ref[where] = jnp.where(core == 0, first, second)
+        keep_ref[where] = jnp.where(core == 0, first, second).astype(jnp.bfloat16)
         send_ref[where] = jnp.where(core == 0, second, first).astype(jnp.bfloat16)
 
 
-def share_kernel(blocks, place_ref, keep_ref, other_ref, *outs):
-    chunk = keep_ref.shape[0] // blocks
-    for step in range(blocks):
-        start = lax.rem(place_ref[0] + step, blocks) * chunk
-        where = pl.ds(pl.multiple_of(start, chunk), chunk)
-        total = keep_ref[where] + other_ref[where].astype(jnp.float32)
-        outs[step][...] = total.astype(outs[step].dtype)
+def near_kernel(place_ref, *refs):
+    parts = refs[:-2]
+    keep_ref, send_ref = refs[-2:]
+    chunk = keep_ref.shape[1]
+    side = lax.bitwise_and(place_ref[0], 1)
+    for index in range(2):
+        for ref, parity in ((keep_ref, side), (send_ref, 1 - side)):
+            where = pl.ds(pl.multiple_of((2 * index + parity) * chunk, chunk), chunk)
+            total = parts[0][where].astype(jnp.float32)
+            for part in parts[1:]:
+                total = total + part[where].astype(jnp.float32)
+            ref[index] = total.astype(ref.dtype)
+
+
+def far_kernel(place_ref, held_ref, other_ref, keep_ref, send_ref):
+    side = lax.div(place_ref[0], 2)
+    keep_ref[...] = held_ref[side] + other_ref[side].astype(jnp.float32)
+    total = held_ref[1 - side] + other_ref[1 - side].astype(jnp.float32)
+    send_ref[...] = total.astype(jnp.bfloat16)
 
 
 def head_body(
@@ -370,7 +401,7 @@
     smem = pl.BlockSpec(memory_space=pltpu.SMEM)
     place = jnp.stack([block, chip, core])
 
-    def call(kernel, shapes, *arrays, scratch=(), read=vmem, mib=10):
+    def call(kernel, shapes, *arrays, scratch=(), read=vmem, mib=4):
         return pl.pallas_call(
             kernel,
             out_shape=shapes,
@@ -429,24 +460,37 @@
         columns_for(core).astype(jnp.float32)
         + swapped(columns_for(1 - core), 1).astype(jnp.float32)
     ).astype(jnp.bfloat16)
-    output_sum = lax.dynamic_index_in_dim(chip_output, chip, 0, False).astype(jnp.float32)
+    output_parts = [lax.dynamic_index_in_dim(chip_output, chip, 0, False)]
     for m in range(2, data_count, 2):
-        output_sum = output_sum + swapped(
-            lax.dynamic_index_in_dim(chip_output, chip ^ (m // 2), 0, False), m
-        ).astype(jnp.float32)
-
-    steps = call(
-        lambda *refs: head_kernel(blocks, *refs),
-        [low(rows, head_size)] * (3 * blocks),
+        piece = lax.dynamic_index_in_dim(chip_output, chip ^ (m // 2), 0, False)
+        output_parts.append(swapped(piece, m))
+
+    def halved(*parts):
+        chunk = features // blocks
+        wide = jax.ShapeDtypeStruct((2, chunk, width), jnp.float32)
+        held, sent = call(near_kernel, [wide, low(2, chunk, width)], *parts)
+        other = traded(sent, 1)
+        narrow = jax.ShapeDtypeStruct((chunk, width), jnp.float32)
+        held, sent = call(far_kernel, [narrow, low(chunk, width)], held, other)
+        return held, traded(sent, 2)
+
+    weighed = call(
+        lambda *refs: weigh_kernel(blocks, *refs),
+        [low(rows, head_size)] * blocks
+        + [jax.ShapeDtypeStruct((blocks, 2, rows, rows), jnp.float32)],
         *packs,
-        scratch=[pltpu.VMEM((blocks, 2, rows, rows), jnp.bfloat16)] * 2,
-    )
-    output_pieces = output_sum.reshape(blocks, features // blocks, width)
-    totals = {"o": lax.dynamic_index_in_dim(output_pieces, block, 0, False)}
-    for step in range(1, blocks):
-        piece = lax.dynamic_index_in_dim(output_pieces, (block + step) % blocks, 0, False)
-        piece = rotated(piece.astype(jnp.bfloat16), step)
-        totals["o"] = totals["o"] + piece.astype(jnp.float32)
+        mib=12,
+    )
+    sloped = call(
+        lambda *refs: slope_kernel(blocks, *refs),
+        [low(rows, head_size)] * (2 * blocks),
+        weighed[blocks],
+        *packs,
+        scratch=[pltpu.VMEM((blocks, 2, rows, rows), jnp.bfloat16)],
+        mib=12,
+    )
+    steps = list(weighed[:blocks]) + list(sloped)
+    totals = {"o": halved(*output_parts)}
     for g, (name, earlier) in enumerate(
         (("v", grad_values), ("k", grad_keys), ("q", grad_queries))
     ):
@@ -461,7 +505,7 @@
         rights = [rights[0]] + [swapped(rights[index], 2 * index) for index in range(1, blocks)]
         keep, send = call(
             lambda *refs: weight_kernel(blocks, *refs),
-            [jax.ShapeDtypeStruct((features, width), jnp.float32), low(features, width)],
+            [low(features, width)] * 2,
             turned,
             beside,
             below,
@@ -470,17 +514,10 @@
             *rights,
         )
         other = swapped(send, 1)
-        shape = (features // blocks, width)
-        shares = call(
-            lambda *refs: share_kernel(blocks, *refs),
-            [jax.ShapeDtypeStruct(shape, jnp.float32)] + [low(*shape)] * (blocks - 1),
-            keep,
-            other,
-        )
-        totals[name] = shares[0]
-        for step in range(1, blocks):
-            piece = rotated(shares[step], step)
-            totals[name] = totals[name] + piece.astype(jnp.float32)
+        totals[name] = halved(keep, other)
+    totals = {
+        name: sum(part.astype(jnp.float32) for part in parts) for name, parts in totals.items()
+    }
     all_tokens = data_count * blocks * rows
     gradient = jnp.stack([totals[name] for name in "qkvo"]) / all_tokens
     return factored_update(gradient, weights, row_factor, column_factor, blocks, data_count)

time: 220 us -> 208 us (0.945)
  waiting for transfers between devices: 106 us -> 90.2 us
  local copies, waits for them, and re-layouts: 12.6 us -> 20.6 us
  starting transfers between devices: 59 us -> 54.4 us
  Pallas kernels: 25.1 us -> 29.2 us
  other arithmetic: 10.7 us -> 7.76 us
    ppermute x27 -> x15, waiting for transfers between devices: 78.2 us -> 56.3 us  [rotated(): return lax.ppermute(value, 'blk', pairs)]
    ppermute x0 -> x8, waiting for transfers between devices: none -> 21 us  [traded(): lax.ppermute(value, 'blk', [(source, source ^ mask) for source in range(c...]
    ppermute x27 -> x15, starting transfers between devices: 40.6 us -> 22.5 us  [rotated(): return lax.ppermute(value, 'blk', pairs)]
    ppermute x24, waiting for transfers between devices: 28.2 us -> 12.9 us  [swapped(): lax.ppermute(value, 'dp', [(source, source ^ mask) for source in range(co...]
    ppermute x0 -> x8, starting transfers between devices: none -> 11.4 us  [traded(): lax.ppermute(value, 'blk', [(source, source ^ mask) for source in range(c...]
    unnamed x61 -> x73, local copies, waits for them, and re-layouts: 6.4 us -> 14.5 us
    pallas_call x11 -> x17, Pallas kernels: 25.1 us -> 29.2 us  [call(): pl.pallas_call(kernel, out_shape=shapes, in_specs=[smem] + [read] * len(a...]
  transfers between devices with their start and end apart: 51 -> 47, of which waited for: 25 -> 21; matrix products, arithmetic and copies ran while one was open for 9% -> 8% of each run, Pallas kernels for 11% -> 14%
where the time goes in v2:
time: 208 us
  waiting for transfers between devices  90.2 us (43%)
  starting transfers between devices  54.4 us (26%)
  Pallas kernels  29.2 us (14%)
  local copies, waits for them, and re-layouts  20.6 us (10%)
  other arithmetic  7.76 us (4%)
  matrix products  4.33 us (2%)
    ppermute x15, waiting for transfers between devices, rotated(): return lax.ppermute(value, 'blk', pairs)  56.3 us
    pallas_call x17, Pallas kernels, call(): pl.pallas_call(kernel, out_shape=shapes, in_specs=[smem] + [read] * len(a...  29.2 us
    ppermute x15, starting transfers between devices, rotated(): return lax.ppermute(value, 'blk', pairs)  22.5 us
    ppermute x8, waiting for transfers between devices, traded(): lax.ppermute(value, 'blk', [(source, source ^ mask) for source in range(c...  21 us
    ppermute x24, starting transfers between devices, swapped(): lax.ppermute(value, 'dp', [(source, source ^ mask) for source in range(co...  20.6 us
    unnamed x73, local copies, waits for them, and re-layouts  14.5 us
    ppermute x24, waiting for transfers between devices, swapped(): lax.ppermute(value, 'dp', [(source, source ^ mask) for source in range(co...  12.9 us
    ppermute x8, starting transfers between devices, traded(): lax.ppermute(value, 'blk', [(source, source ^ mask) for source in range(c...  11.4 us
  transfers between devices with their start and end apart: 47, of which 21 were waited for; matrix products, arithmetic and copies ran while one was open for 8% of the time, Pallas kernels for 14%

profile of v2, /device:TPU:0, one launch (start us, length us, event | category | flops | bytes accessed | tf_op | source)
XLA Modules:
  0.0 207.7 jit_solution(13120700068643731636)
XLA Ops:
  2.2 3.0 %collective-permute-start = (bf16[2048,256]{1,0:T(8,128)(2,1)S(1)}, bf16[2048,256]{1,0:T(8,128)(2,1)S(1)}, u32[]{:S(2)}, u32[]{:S(2)}) collective-permute-start(bf16[2048,256]{1,0:T(8,128)(2,1)S(1)} %bitcast.44), channel_id=1, source_target_pairs={{0,8},{4,12},{8,0},{12,4},{16,24},{20,28},{24,16},{28,20},{1,9},{5... | collective-permute-start | bytes 3145736 | tf_op jit(solution)/shard_map/ppermute | solution.py:164
  7.4 4.1 %shard_map.166 = (bf16[1040,256]{1,0:T(8,128)(2,1)}, bf16[1040,256]{1,0:T(8,128)(2,1)}, bf16[1040,256]{1,0:T(8,128)(2,1)}, bf16[1040,256]{1,0:T(8,128)(2,1)}) custom-call(s32[3]{0:T(128)} %pad_add_fusion.refs_0_.place_ref, bf16[1,256,1024]{2,1,0:T(8,128)(2,1)} %refs_1_.1, bf16[1,256,1024]{2,1,0:T(8,128)(2,1)} %refs_2_.1, bf16[1,256,1024]{2,1,0:T(8,128)(2,1)} %refs_3_.1, ...), custom_call_target="tpu_custom_call" | custom-call | tf_op jit(solution)/shard_map/pallas_call | solution.py:405
  11.5 3.7 %collective-permute-start.4 = (bf16[1040,256]{1,0:T(8,128)(2,1)}, bf16[1040,256]{1,0:T(8,128)(2,1)}, u32[]{:S(2)}, u32[]{:S(2)}) collective-permute-start(bf16[1040,256]{1,0:T(8,128)(2,1)} %get-tuple-element.55), channel_id=1, source_target_pairs={{0,3},{1,0},{2,1},{3,2},{4,7},{5,4},{6,5},{7,6},{8,11},{9,8},{10,9... | collective-permute-start | bytes 1597448 | tf_op jit(solution)/shard_map/ppermute | solution.py:170
  15.2 4.3 %convolution_convert_fusion = bf16[2048,1024]{1,0:T(8,128)(2,1)} fusion(bf16[1,256,2048]{2,1,0:T(8,128)(2,1)S(1)} %copy-done, bf16[1,256,1024]{2,1,0:T(8,128)(2,1)} %refs_5_.4), kind=kOutput, calls=%fused_computation.1 | convolution fusion | flops 1075838976 | bytes 5767168 | tf_op jit(solution)/shard_map/th,td->dh/dot_general | solution.py:447
  19.5 3.7 %dynamic-slice_bitcast_fusion.11 = (bf16[1,2048,128]{2,1,0:T(8,128)(2,1)}, bf16[1,2048,128]{2,1,0:T(8,128)(2,1)S(1)}, bf16[1,2048,128]{2,1,0:T(8,128)(2,1)S(1)},...) fusion(bf16[2048,1024]{1,0:T(8,128)(2,1)} %convolution_convert_, ...), kind=kLoop, calls=%fused_computation.21 | loop fusion | bytes 8388640 | tf_op jit(solution)/shard_map/stack | solution.py:452
  26.8 34.6 %collective-permute-done.5.refs_3_.refs_4_ = bf16[1040,256]{1,0:T(8,128)(2,1)S(1)} collective-permute-done((bf16[1040,256]{1,0:T(8,128)(2,1)S(1)}, bf16[1040,256]{1,0:T(8,128)(2,1)S(1)}, u32[]{:S(2)}, u32[]{:S(2)}) %collective-permute-start.5) | collective-permute-done | bytes 532512 | tf_op jit(solution)/shard_map/ppermute | solution.py:170
  61.4 3.6 %shard_map.167 = (bf16[256,256]{1,0:T(8,128)(2,1)S(1)}, bf16[256,256]{1,0:T(8,128)(2,1)S(1)}, bf16[256,256]{1,0:T(8,128)(2,1)S(1)}, bf16[256,256]{1,0:T(8,128)(2,1)S(1)}, f32[4,2,256,256]{3,2,1,0:T(8,128)S(1)}) custom-call(s32[3]{0:T(128)S(1)} %copy-done.18, bf16[1040,256]{1,0:T(8,128)(2,1)S(1)} %copy-done.6, ...), custom_call_target="tpu_custom_call" | custom-call | tf_op jit(solution)/shard_map/pallas_call | solution.py:405
  65.0 2.6 %shard_map.168 = (bf16[256,256]{1,0:T(8,128)(2,1)S(1)}, bf16[256,256]{1,0:T(8,128)(2,1)S(1)}, bf16[256,256]{1,0:T(8,128)(2,1)S(1)}, bf16[256,256]{1,0:T(8,128)(2...) custom-call(s32[3]{0:T(128)S(1)} %copy-done.18, ...), custom_call_target="tpu_custom_call" | custom-call | tf_op jit(solution)/shard_map/pallas_call | solution.py:405
  72.4 2.5 %collective-permute-done.7.refs_2_ = bf16[256,256]{1,0:T(8,128)(2,1)S(1)} collective-permute-done((bf16[256,256]{1,0:T(8,128)(2,1)S(1)}, bf16[256,256]{1,0:T(8,128)(2,1)S(1)}, u32[]{:S(2)}, u32[]{:S(2)}) %collective-permute-start.7) | collective-permute-done | bytes 131104 | tf_op jit(solution)/shard_map/ppermute | solution.py:170
  75.3 5.3 %collective-permute-done.8.refs_3_ = bf16[256,256]{1,0:T(8,128)(2,1)S(1)} collective-permute-done((bf16[256,256]{1,0:T(8,128)(2,1)S(1)}, bf16[256,256]{1,0:T(8,128)(2,1)S(1)}, u32[]{:S(2)}, u32[]{:S(2)}) %collective-permute-start.8) | collective-permute-done | bytes 131104 | tf_op jit(solution)/shard_map/ppermute | solution.py:170
  84.2 3.5 %collective-permute-done.10.refs_7_ = bf16[256,256]{1,0:T(8,128)(2,1)S(1)} collective-permute-done((bf16[256,256]{1,0:T(8,128)(2,1)S(1)}, bf16[256,256]{1,0:T(8,128)(2,1)S(1)}, u32[]{:S(2)}, u32[]{:S(2)}) %collective-permute-start.10) | collective-permute-done | bytes 131104 | tf_op jit(solution)/shard_map/ppermute | solution.py:164
  90.8 2.7 %collective-permute-done.12.refs_9_ = bf16[256,256]{1,0:T(8,128)(2,1)S(1)} collective-permute-done((bf16[256,256]{1,0:T(8,128)(2,1)S(1)}, bf16[256,256]{1,0:T(8,128)(2,1)S(1)}, u32[]{:S(2)}, u32[]{:S(2)}) %collective-permute-start.12) | collective-permute-done | bytes 131104 | tf_op jit(solution)/shard_map/ppermute | solution.py:164
  93.5 5.5 %collective-permute-start.17 = (bf16[256,256]{1,0:T(8,128)(2,1)S(1)}, bf16[256,256]{1,0:T(8,128)(2,1)S(1)}, u32[]{:S(2)}, u32[]{:S(2)}) collective-permute-start(bf16[256,256]{1,0:T(8,128)(2,1)S(1)} %get-tuple-element.75), channel_id=1, source_target_pairs={{0,2},{1,3},{2,0},{3,1},{4,6},{5,7},{6,4},{7,5},{8,10},{9,11},{10,... | collective-permute-start | bytes 393224 | tf_op jit(solution)/shard_map/ppermute | solution.py:170
  99.1 3.7 %shard_map.170 = (bf16[2048,128]{1,0:T(8,128)(2,1)S(1)}, bf16[2048,128]{1,0:T(8,128)(2,1)}) custom-call(s32[3]{0:T(128)S(1)} %copy-done.18, bf16[2048,256]{1,0:T(8,128)(2,1)S(1)} %bitcast.46, bf16[2048,256]{1,0:T(8,128)(2,1)S(1)} %collective-permute-done.refs_2_, bf16[2048,256]{1,0:T(8,128)(2,1)} %collective-permute-done.1.refs_3_, ...), custom_call_target="tpu_custom_call" | custom-call | tf_op jit(solution)/shard_map/pallas_call | solution.py:405
  108.7 3.3 %collective-permute-done.25.refs_2_ = bf16[256,256]{1,0:T(8,128)(2,1)S(1)} collective-permute-done((bf16[256,256]{1,0:T(8,128)(2,1)S(1)}, bf16[256,256]{1,0:T(8,128)(2,1)S(1)}, u32[]{:S(2)}, u32[]{:S(2)}) %collective-permute-start.25) | collective-permute-done | bytes 131104 | tf_op jit(solution)/shard_map/ppermute | solution.py:170
  112.0 5.1 %collective-permute-done.26.refs_3_ = bf16[256,256]{1,0:T(8,128)(2,1)S(1)} collective-permute-done((bf16[256,256]{1,0:T(8,128)(2,1)S(1)}, bf16[256,256]{1,0:T(8,128)(2,1)S(1)}, u32[]{:S(2)}, u32[]{:S(2)}) %collective-permute-start.26) | collective-permute-done | bytes 131104 | tf_op jit(solution)/shard_map/ppermute | solution.py:170
  132.5 2.5 %shard_map.174 = (bf16[2048,128]{1,0:T(8,128)(2,1)S(1)}, bf16[2048,128]{1,0:T(8,128)(2,1)S(1)}) custom-call(s32[3]{0:T(128)S(1)} %copy-done.18, bf16[2048,256]{1,0:T(8,128)(2,1)S(1)} %bitcast.47, bf16[2048,256]{1,0:T(8,128)(2,1)S(1)} %collective-permute-done.refs_2_, bf16[2048,256]{1,0:T(8,128)(2,1)} %collective-permute-done.1.refs_3_, ...), custom_call_target="tpu_custom_call" | custom-call | tf_op jit(solution)/shard_map/pallas_call | solution.py:405
  135.2 2.7 %shard_map.178 = (bf16[2048,128]{1,0:T(8,128)(2,1)S(1)}, bf16[2048,128]{1,0:T(8,128)(2,1)S(1)}) custom-call(s32[3]{0:T(128)S(1)} %copy-done.18, bf16[2048,256]{1,0:T(8,128)(2,1)S(1)} %bitcast.48, bf16[2048,256]{1,0:T(8,128)(2,1)S(1)} %collective-permute-done.refs_2_, bf16[2048,256]{1,0:T(8,128)(2,1)} %collective-permute-done.1.refs_3_, ...), custom_call_target="tpu_custom_call" | custom-call | tf_op jit(solution)/shard_map/pallas_call | solution.py:405
  153.3 4.4 %collective-permute-done.23.other_ref = bf16[2,512,128]{2,1,0:T(8,128)(2,1)S(1)} collective-permute-done((bf16[2,512,128]{2,1,0:T(8,128)(2,1)S(1)}, bf16[2,512,128]{2,1,0:T(8,128)(2,1)S(1)}, u32[]{:S(2)}, u32[]{:S(2)}) %collective-permute-start.23) | collective-permute-done | bytes 262176 | tf_op jit(solution)/shard_map/ppermute | solution.py:175
  158.5 3.8 %collective-permute-start.15 = (bf16[512,128]{1,0:T(8,128)(2,1)S(1)}, bf16[512,128]{1,0:T(8,128)(2,1)}, u32[]{:S(2)}, u32[]{:S(2)}) collective-permute-start(bf16[512,128]{1,0:T(8,128)(2,1)S(1)} %get-tuple-element.72), channel_id=1, source_target_pairs={{0,2},{1,3},{2,0},{3,1},{4,6},{5,7},{6,4},{7,5},{8,10},{9,11},{10,... | collective-permute-start | bytes 393224 | tf_op jit(solution)/shard_map/ppermute | solution.py:175
  174.3 2.6 %collective-permute-done.24 = bf16[512,128]{1,0:T(8,128)(2,1)S(1)} collective-permute-done((bf16[512,128]{1,0:T(8,128)(2,1)S(1)}, bf16[512,128]{1,0:T(8,128)(2,1)S(1)}, u32[]{:S(2)}, u32[]{:S(2)}) %collective-permute-start.24) | collective-permute-done | bytes 131104 | tf_op jit(solution)/shard_map/ppermute | solution.py:175
  176.9 6.3 %collective-permute-done.38.other_ref = bf16[2,512,128]{2,1,0:T(8,128)(2,1)S(1)} collective-permute-done((bf16[2,512,128]{2,1,0:T(8,128)(2,1)S(1)}, bf16[2,512,128]{2,1,0:T(8,128)(2,1)S(1)}, u32[]{:S(2)}, u32[]{:S(2)}) %collective-permute-start.38) | collective-permute-done | bytes 262176 | tf_op jit(solution)/shard_map/ppermute | solution.py:175
  184.2 7.7 %collective-permute-done.39 = bf16[512,128]{1,0:T(8,128)(2,1)S(1)} collective-permute-done((bf16[512,128]{1,0:T(8,128)(2,1)S(1)}, bf16[512,128]{1,0:T(8,128)(2,1)S(1)}, u32[]{:S(2)}, u32[]{:S(2)}) %collective-permute-start.39) | collective-permute-done | bytes 131104 | tf_op jit(solution)/shard_map/ppermute | solution.py:175
  192.4 2.6 %collective-permute-start.41 = (f32[4,256]{1,0:T(4,128)S(1)}, f32[4,256]{1,0:T(4,128)S(1)}, u32[]{:S(2)}, u32[]{:S(2)}) collective-permute-start(f32[4,256]{1,0:T(4,128)S(1)} %pad_maximum_fusion.3), channel_id=1, source_target_pairs={{0,2},{1,3},{2,0},{3,1},{4,6},{5,7},{6,4},{7,5},{8,10},{9,11},{10,... | collective-permute-start | bytes 12296 | tf_op jit(solution)/shard_map/ppermute | solution.py:170
  (185 shorter events, 82.6 us)
Async XLA Ops:
  2.2 66.0 %collective-permute-start = (bf16[2048,256]{1,0:T(8,128)(2,1)S(1)}, bf16[2048,256]{1,0:T(8,128)(2,1)S(1)}, u32[]{:S(2)}, u32[]{:S(2)}) collective-permute-start(bf16[2048,256]{1,0:T(8,128)(2,1)S(1)} %bitcast.44), channel_id=1, source_target_pairs={{0,8},{4,12},{8,0},{12,4},{16,24},{20,28},{24,16},{28,20},{1,9},{5... | collective-permute-start | bytes 3145736 | tf_op jit(solution)/shard_map/ppermute | solution.py:164
  5.3 63.6 %collective-permute-start.1 = (bf16[2048,256]{1,0:T(8,128)(2,1)S(1)}, bf16[2048,256]{1,0:T(8,128)(2,1)}, u32[]{:S(2)}, u32[]{:S(2)}) collective-permute-start(bf16[2048,256]{1,0:T(8,128)(2,1)S(1)} %bitcast.45), channel_id=1, source_target_pairs={{0,16},{4,20},{8,24},{12,28},{16,0},{20,4},{24,8},{28,12},{1,17},{... | collective-permute-start | bytes 3145736 | tf_op jit(solution)/shard_map/ppermute | solution.py:164
  11.5 15.2 %collective-permute-start.4 = (bf16[1040,256]{1,0:T(8,128)(2,1)}, bf16[1040,256]{1,0:T(8,128)(2,1)}, u32[]{:S(2)}, u32[]{:S(2)}) collective-permute-start(bf16[1040,256]{1,0:T(8,128)(2,1)} %get-tuple-element.55), channel_id=1, source_target_pairs={{0,3},{1,0},{2,1},{3,2},{4,7},{5,4},{6,5},{7,6},{8,11},{9,8},{10,9... | collective-permute-start | bytes 1597448 | tf_op jit(solution)/shard_map/ppermute | solution.py:170
  24.9 115.1 %collective-permute-start.34 = (bf16[4,2048,128]{2,1,0:T(8,128)(2,1)}, bf16[4,2048,128]{2,1,0:T(8,128)(2,1)}, u32[]{:S(2)}, u32[]{:S(2)}) collective-permute-start(bf16[4,2048,128]{2,1,0:T(8,128)(2,1)} %pad_maximum_fusion), channel_id=1, source_target_pairs={{0,4},{4,0},{8,12},{12,8},{16,20},{20,16},{24,28},{28,24},{1,5},{5... | collective-permute-start | bytes 6291464 | tf_op jit(solution)/shard_map/ppermute | solution.py:164
  24.9 36.4 %collective-permute-start.5 = (bf16[1040,256]{1,0:T(8,128)(2,1)S(1)}, bf16[1040,256]{1,0:T(8,128)(2,1)S(1)}, u32[]{:S(2)}, u32[]{:S(2)}) collective-permute-start(bf16[1040,256]{1,0:T(8,128)(2,1)S(1)} %copy-done.35), channel_id=1, source_target_pairs={{0,2},{1,3},{2,0},{3,1},{4,6},{5,7},{6,4},{7,5},{8,10},{9,11},{10,... | collective-permute-start | bytes 1597448 | tf_op jit(solution)/shard_map/ppermute | solution.py:170
  26.7 34.6 %collective-permute-start.6 = (bf16[1040,256]{1,0:T(8,128)(2,1)S(1)}, bf16[1040,256]{1,0:T(8,128)(2,1)S(1)}, u32[]{:S(2)}, u32[]{:S(2)}) collective-permute-start(bf16[1040,256]{1,0:T(8,128)(2,1)S(1)} %copy-done.34), channel_id=1, source_target_pairs={{0,1},{1,2},{2,3},{3,0},{4,5},{5,6},{6,7},{7,4},{8,9},{9,10},{10,1... | collective-permute-start | bytes 1597448 | tf_op jit(solution)/shard_map/ppermute | solution.py:170
  68.3 30.8 %collective-permute-start.2 = (bf16[1024,256]{1,0:T(8,128)(2,1)S(1)}, bf16[1024,256]{1,0:T(8,128)(2,1)S(1)}, u32[]{:S(2)}, u32[]{:S(2)}) collective-permute-start(bf16[1024,256]{1,0:T(8,128)(2,1)S(1)} %slice.24), channel_id=1, source_target_pairs={{0,16},{4,20},{8,24},{12,28},{16,0},{20,4},{24,8},{28,12},{1,17},{... | collective-permute-start | bytes 1572872 | tf_op jit(solution)/shard_map/ppermute | solution.py:164
  69.9 29.1 %collective-permute-start.3 = (bf16[1024,256]{1,0:T(8,128)(2,1)S(1)}, bf16[1024,256]{1,0:T(8,128)(2,1)S(1)}, u32[]{:S(2)}, u32[]{:S(2)}) collective-permute-start(bf16[1024,256]{1,0:T(8,128)(2,1)S(1)} %slice.25), channel_id=1, source_target_pairs={{0,8},{4,12},{8,0},{12,4},{16,24},{20,28},{24,16},{28,20},{1,9},{5... | collective-permute-start | bytes 1572872 | tf_op jit(solution)/shard_map/ppermute | solution.py:164
  88.6 15.1 %collective-permute-start.16 = (bf16[256,256]{1,0:T(8,128)(2,1)S(1)}, bf16[256,256]{1,0:T(8,128)(2,1)S(1)}, u32[]{:S(2)}, u32[]{:S(2)}) collective-permute-start(bf16[256,256]{1,0:T(8,128)(2,1)S(1)} %get-tuple-element.74), channel_id=1, source_target_pairs={{0,1},{1,2},{2,3},{3,0},{4,5},{5,6},{6,7},{7,4},{8,9},{9,10},{10,1... | collective-permute-start | bytes 393224 | tf_op jit(solution)/shard_map/ppermute | solution.py:170
  93.5 12.0 %collective-permute-start.17 = (bf16[256,256]{1,0:T(8,128)(2,1)S(1)}, bf16[256,256]{1,0:T(8,128)(2,1)S(1)}, u32[]{:S(2)}, u32[]{:S(2)}) collective-permute-start(bf16[256,256]{1,0:T(8,128)(2,1)S(1)} %get-tuple-element.75), channel_id=1, source_target_pairs={{0,2},{1,3},{2,0},{3,1},{4,6},{5,7},{6,4},{7,5},{8,10},{9,11},{10,... | collective-permute-start | bytes 393224 | tf_op jit(solution)/shard_map/ppermute | solution.py:170
  103.7 34.9 %collective-permute-start.13 = (bf16[2048,128]{1,0:T(8,128)(2,1)}, bf16[2048,128]{1,0:T(8,128)(2,1)}, u32[]{:S(2)}, u32[]{:S(2)}) collective-permute-start(bf16[2048,128]{1,0:T(8,128)(2,1)} %get-tuple-element.68), channel_id=1, source_target_pairs={{0,4},{4,0},{8,12},{12,8},{16,20},{20,16},{24,28},{28,24},{1,5},{5... | collective-permute-start | bytes 1572872 | tf_op jit(solution)/shard_map/ppermute | solution.py:164
  105.5 11.6 %collective-permute-start.26 = (bf16[256,256]{1,0:T(8,128)(2,1)S(1)}, bf16[256,256]{1,0:T(8,128)(2,1)S(1)}, u32[]{:S(2)}, u32[]{:S(2)}) collective-permute-start(bf16[256,256]{1,0:T(8,128)(2,1)S(1)} %get-tuple-element.89), channel_id=1, source_target_pairs={{0,2},{1,3},{2,0},{3,1},{4,6},{5,7},{6,4},{7,5},{8,10},{9,11},{10,... | collective-permute-start | bytes 393224 | tf_op jit(solution)/shard_map/ppermute | solution.py:170
  105.6 11.5 %collective-permute-start.27 = (bf16[256,256]{1,0:T(8,128)(2,1)S(1)}, bf16[256,256]{1,0:T(8,128)(2,1)S(1)}, u32[]{:S(2)}, u32[]{:S(2)}) collective-permute-start(bf16[256,256]{1,0:T(8,128)(2,1)S(1)} %get-tuple-element.90), channel_id=1, source_target_pairs={{0,3},{1,0},{2,1},{3,2},{4,7},{5,4},{6,5},{7,6},{8,11},{9,8},{10,9... | collective-permute-start | bytes 393224 | tf_op jit(solution)/shard_map/ppermute | solution.py:170
  120.5 14.5 %collective-permute-start.28 = (bf16[256,256]{1,0:T(8,128)(2,1)}, bf16[256,256]{1,0:T(8,128)(2,1)}, u32[]{:S(2)}, u32[]{:S(2)}) collective-permute-start(bf16[256,256]{1,0:T(8,128)(2,1)} %get-tuple-element.92), channel_id=1, source_target_pairs={{0,8},{4,12},{8,0},{12,4},{16,24},{20,28},{24,16},{28,20},{1,9},{5... | collective-permute-start | bytes 393224 | tf_op jit(solution)/shard_map/ppermute | solution.py:164
  135.1 11.7 %collective-permute-start.22 = (bf16[2048,128]{1,0:T(8,128)(2,1)S(1)}, bf16[2048,128]{1,0:T(8,128)(2,1)S(1)}, u32[]{:S(2)}, u32[]{:S(2)}) collective-permute-start(bf16[2048,128]{1,0:T(8,128)(2,1)S(1)} %get-tuple-element.82), channel_id=1, source_target_pairs={{0,4},{4,0},{8,12},{12,8},{16,20},{20,16},{24,28},{28,24},{1,5},{5... | collective-permute-start | bytes 1572872 | tf_op jit(solution)/shard_map/ppermute | solution.py:164
  139.7 13.0 %collective-permute-start.14 = (bf16[2,512,128]{2,1,0:T(8,128)(2,1)S(1)}, bf16[2,512,128]{2,1,0:T(8,128)(2,1)S(1)}, u32[]{:S(2)}, u32[]{:S(2)}) collective-permute-start(bf16[2,512,128]{2,1,0:T(8,128)(2,1)S(1)} %get-tuple-element.70), channel_id=1, source_target_pairs={{0,1},{1,0},{2,3},{3,2},{4,5},{5,4},{6,7},{7,6},{8,9},{9,8},{10,11... | collective-permute-start | bytes 786440 | tf_op jit(solution)/shard_map/ppermute | solution.py:175
  143.5 25.6 %collective-permute-start.35 = (bf16[2048,128]{1,0:T(8,128)(2,1)}, bf16[2048,128]{1,0:T(8,128)(2,1)S(1)}, u32[]{:S(2)}, u32[]{:S(2)}) collective-permute-start(bf16[2048,128]{1,0:T(8,128)(2,1)} %get-tuple-element.117), channel_id=1, source_target_pairs={{0,8},{4,12},{8,0},{12,4},{16,24},{20,28},{24,16},{28,20},{1,9},{5... | collective-permute-start | bytes 1572872 | tf_op jit(solution)/shard_map/ppermute | solution.py:164
  145.7 25.0 %collective-permute-start.36 = (bf16[2048,128]{1,0:T(8,128)(2,1)}, bf16[2048,128]{1,0:T(8,128)(2,1)S(1)}, u32[]{:S(2)}, u32[]{:S(2)}) collective-permute-start(bf16[2048,128]{1,0:T(8,128)(2,1)} %get-tuple-element.116), channel_id=1, source_target_pairs={{0,16},{4,20},{8,24},{12,28},{16,0},{20,4},{24,8},{28,12},{1,17},{... | collective-permute-start | bytes 1572872 | tf_op jit(solution)/shard_map/ppermute | solution.py:164
  146.7 24.0 %collective-permute-start.37 = (bf16[2048,128]{1,0:T(8,128)(2,1)}, bf16[2048,128]{1,0:T(8,128)(2,1)S(1)}, u32[]{:S(2)}, u32[]{:S(2)}) collective-permute-start(bf16[2048,128]{1,0:T(8,128)(2,1)} %get-tuple-element.115), channel_id=1, source_target_pairs={{0,24},{4,28},{8,16},{12,20},{16,8},{20,12},{24,0},{28,4},{1,25},{... | collective-permute-start | bytes 1572872 | tf_op jit(solution)/shard_map/ppermute | solution.py:164
  152.7 12.3 %collective-permute-start.32 = (bf16[2,512,128]{2,1,0:T(8,128)(2,1)}, bf16[2,512,128]{2,1,0:T(8,128)(2,1)}, u32[]{:S(2)}, u32[]{:S(2)}) collective-permute-start(bf16[2,512,128]{2,1,0:T(8,128)(2,1)} %get-tuple-element.98), channel_id=1, source_target_pairs={{0,1},{1,0},{2,3},{3,2},{4,5},{5,4},{6,7},{7,6},{8,9},{9,8},{10,11... | collective-permute-start | bytes 786440 | tf_op jit(solution)/shard_map/ppermute | solution.py:175
  158.5 14.8 %collective-permute-start.15 = (bf16[512,128]{1,0:T(8,128)(2,1)S(1)}, bf16[512,128]{1,0:T(8,128)(2,1)}, u32[]{:S(2)}, u32[]{:S(2)}) collective-permute-start(bf16[512,128]{1,0:T(8,128)(2,1)S(1)} %get-tuple-element.72), channel_id=1, source_target_pairs={{0,2},{1,3},{2,0},{3,1},{4,6},{5,7},{6,4},{7,5},{8,10},{9,11},{10,... | collective-permute-start | bytes 393224 | tf_op jit(solution)/shard_map/ppermute | solution.py:175
  165.0 11.8 %collective-permute-start.24 = (bf16[512,128]{1,0:T(8,128)(2,1)S(1)}, bf16[512,128]{1,0:T(8,128)(2,1)S(1)}, u32[]{:S(2)}, u32[]{:S(2)}) collective-permute-start(bf16[512,128]{1,0:T(8,128)(2,1)S(1)} %get-tuple-element.86), channel_id=1, source_target_pairs={{0,2},{1,3},{2,0},{3,1},{4,6},{5,7},{6,4},{7,5},{8,10},{9,11},{10,... | collective-permute-start | bytes 393224 | tf_op jit(solution)/shard_map/ppermute | solution.py:175
  169.2 15.0 %collective-permute-start.33 = (bf16[512,128]{1,0:T(8,128)(2,1)S(1)}, bf16[512,128]{1,0:T(8,128)(2,1)S(1)}, u32[]{:S(2)}, u32[]{:S(2)}) collective-permute-start(bf16[512,128]{1,0:T(8,128)(2,1)S(1)} %get-tuple-element.100), channel_id=1, source_target_pairs={{0,2},{1,3},{2,0},{3,1},{4,6},{5,7},{6,4},{7,5},{8,10},{9,11},{10,... | collective-permute-start | bytes 393224 | tf_op jit(solution)/shard_map/ppermute | solution.py:175
  171.5 11.7 %collective-permute-start.38 = (bf16[2,512,128]{2,1,0:T(8,128)(2,1)S(1)}, bf16[2,512,128]{2,1,0:T(8,128)(2,1)S(1)}, u32[]{:S(2)}, u32[]{:S(2)}) collective-permute-start(bf16[2,512,128]{2,1,0:T(8,128)(2,1)S(1)} %get-tuple-element.102), channel_id=1, source_target_pairs={{0,1},{1,0},{2,3},{3,2},{4,5},{5,4},{6,7},{7,6},{8,9},{9,8},{10,11... | collective-permute-start | bytes 786440 | tf_op jit(solution)/shard_map/ppermute | solution.py:175
  (59 other events, 424.8 us)

commit v3 on v2

--- a/solution.py
+++ b/solution.py
@@ -181,41 +181,79 @@
     return (high, middle, value - high - middle)
 
 
-def pack_kernel(blocks, place_ref, *refs):
-    stored, outs = refs[:7], refs[7 : 7 + blocks]
-    held, dot_ref, arrived = refs[7 + blocks : 14 + blocks], refs[14 + blocks], refs[15 + blocks]
+def pack_heads(blocks, place_ref, stored, outs, arrived):
+    rows = stored[0].shape[1]
+    head_size = stored[0].shape[2] // blocks
+    copies = []
+    for step in range(blocks):
+        head = lax.rem(place_ref[0] + step, blocks)
+        columns = pl.ds(pl.multiple_of(head * head_size, head_size), head_size)
+        for index, ref in enumerate(stored):
+            target = outs[step].at[index * rows : (index + 1) * rows]
+            copies.append(
+                pltpu.make_async_copy(ref.at[0, :, columns], target, arrived.at[len(copies)])
+            )
+    for copy in copies:
+        copy.start()
+    return copies
+
+
+def held_copies(stored, held, arrived, first):
     copies = [
-        pltpu.make_async_copy(source, target, arrived.at[index])
+        pltpu.make_async_copy(source, target, arrived.at[first + index])
         for index, (source, target) in enumerate(zip(stored, held))
     ]
     for copy in copies:
         copy.start()
+    return copies
+
+
+def pack_early_kernel(blocks, place_ref, query_ref, key_ref, mass_ref, docs_ref, *refs):
+    outs, held, arrived = refs[:blocks], refs[blocks : blocks + 2], refs[blocks + 2]
+    small = held_copies((mass_ref, docs_ref), held, arrived, 2 * blocks)
+    copies = pack_heads(blocks, place_ref, (query_ref, key_ref), outs, arrived)
+    rows = docs_ref.shape[1]
+    line = lax.broadcasted_iota(jnp.int32, (16, rows), 0)
+    for copy in small:
+        copy.wait()
+    docs = held[1][...].astype(jnp.float32)
+    for step in range(blocks):
+        head = lax.rem(place_ref[0] + step, blocks)
+        side = jnp.where(line == 3, docs, 0.0)
+        for index, term in enumerate(split_three(held[0][0, pl.ds(head, 1), :])):
+            side = jnp.where(line == index, term, side)
+        outs[step][2 * rows :] = side.astype(jnp.bfloat16)
     for copy in copies:
         copy.wait()
-    query_ref, key_ref, value_ref, grad_ref, context_ref, mass_ref, docs_ref = held
-    rows = query_ref.shape[1]
-    head_size = query_ref.shape[2] // blocks
+
+
+def pack_late_kernel(blocks, place_ref, value_ref, grad_ref, context_ref, *refs):
+    outs, held = refs[:blocks], refs[blocks : blocks + 2]
+    dot_ref, arrived = refs[blocks + 2 :]
+    large = held_copies((grad_ref, context_ref), held, arrived, 2 * blocks)
+    copies = pack_heads(blocks, place_ref, (value_ref, grad_ref), outs, arrived)
+    rows = value_ref.shape[1]
+    head_size = value_ref.shape[2] // blocks
+    for copy in large:
+        copy.wait()
     lane = lax.broadcasted_iota(jnp.int32, (rows, 128), 1)
     dots = jnp.zeros((rows, 128), jnp.float32)
     for head in range(blocks):
         columns = slice(head * head_size, (head + 1) * head_size)
-        product = context_ref[0, :, columns].astype(jnp.float32) * grad_ref[0, :, columns].astype(
+        product = held[0][0, :, columns].astype(jnp.float32) * held[1][0, :, columns].astype(
             jnp.float32
         )
         dots = jnp.where(lane == head, jnp.sum(product, axis=1, keepdims=True), dots)
     dot_ref[...] = dots.T
-    docs = docs_ref[...].astype(jnp.float32)
     line = lax.broadcasted_iota(jnp.int32, (16, rows), 0)
     for step in range(blocks):
         head = lax.rem(place_ref[0] + step, blocks)
-        columns = pl.ds(pl.multiple_of(head * head_size, head_size), head_size)
-        for index, ref in enumerate((query_ref, key_ref, value_ref, grad_ref)):
-            outs[step][index * rows : (index + 1) * rows] = ref[0, :, columns]
-        terms = split_three(mass_ref[0, pl.ds(head, 1), :]) + split_three(dot_ref[pl.ds(head, 1), :])
-        side = jnp.where(line == 6, docs, 0.0)
-        for index, term in enumerate(terms):
+        side = jnp.zeros((16, rows), jnp.float32)
+        for index, term in enumerate(split_three(dot_ref[pl.ds(head, 1), :])):
             side = jnp.where(line == index, term, side)
-        outs[step][4 * rows :] = side.astype(jnp.bfloat16)
+        outs[step][2 * rows :] = side.astype(jnp.bfloat16)
+    for copy in copies:
+        copy.wait()
 
 
 def times(left, right, left_dim, right_dim):
@@ -228,18 +266,18 @@
 
 
 def side_of(pack_ref):
-    rows = (pack_ref.shape[0] - 16) // 4
-    side = pack_ref[4 * rows :].astype(jnp.float32)
-    return side[0:1] + side[1:2] + side[2:3], side[3:4] + side[4:5] + side[5:6], side[6:7]
+    rows = (pack_ref.shape[0] - 16) // 2
+    side = pack_ref[2 * rows :].astype(jnp.float32)
+    return side[0:1] + side[1:2] + side[2:3], side[3:4]
 
 
 def part_of(pack_ref, index):
-    rows = (pack_ref.shape[0] - 16) // 4
+    rows = (pack_ref.shape[0] - 16) // 2
     return pack_ref[index * rows : (index + 1) * rows]
 
 
 def weigh_kernel(blocks, place_ref, *refs):
-    packs, outs, weight_ref = refs[:blocks], refs[blocks : 2 * blocks], refs[2 * blocks]
+    packs, weight_ref = refs[:blocks], refs[blocks]
     rows = weight_ref.shape[2]
     half = rows // 2
     scale_factor = 1.0 / math.sqrt(packs[0].shape[1])
@@ -254,7 +292,7 @@
         return jnp.where(local < half, lower, upper)
 
     for step in range(blocks):
-        mass, _, docs = side_of(packs[step])
+        mass, docs = side_of(packs[step])
         down = jnp.where(line == 0, mass, docs).T
         mass, docs = down[:, 0:1], down[:, 1:2]
         own_pos = positions(local_down, block_of[step])
@@ -263,7 +301,7 @@
             other = (step + 1 + far) % blocks
             score = times(part_of(packs[step], 0), part_of(packs[other], 1), 1, 1) * scale_factor
             allowed = (positions(local_across, block_of[other]) <= own_pos) & (
-                side_of(packs[other])[2] == docs
+                side_of(packs[other])[1] == docs
             )
             scored.append(jnp.where(allowed, score, -jnp.inf))
         peak = mass
@@ -275,27 +313,31 @@
             total = total + jnp.sum(part, axis=1, keepdims=True)
         inverse = 1.0 / total
         for far in range(2):
-            weight_ref[step, far] = (shifted[far] * inverse).astype(weight_ref.dtype)
+            weight_ref[step, far] = shifted[far] * inverse
+
+
+def value_kernel(blocks, place_ref, weight_ref, *refs):
+    late, outs = refs[:blocks], refs[blocks:]
     for step in range(blocks):
         near, far = (step - 1) % blocks, (step - 2) % blocks
         value_step = times(
-            weight_ref[near, 0].astype(jnp.bfloat16), part_of(packs[near], 3), 0, 0
-        ) + times(weight_ref[far, 1].astype(jnp.bfloat16), part_of(packs[far], 3), 0, 0)
+            weight_ref[near, 0].astype(jnp.bfloat16), part_of(late[near], 1), 0, 0
+        ) + times(weight_ref[far, 1].astype(jnp.bfloat16), part_of(late[far], 1), 0, 0)
         outs[step][...] = value_step.astype(jnp.bfloat16)
 
 
 def slope_kernel(blocks, place_ref, weight_ref, *refs):
-    packs, key_outs, query_outs = (refs[n * blocks : (n + 1) * blocks] for n in range(3))
-    slope_ref = refs[3 * blocks]
+    packs, late, key_outs, query_outs = (refs[n * blocks : (n + 1) * blocks] for n in range(4))
+    slope_ref = refs[4 * blocks]
     rows = weight_ref.shape[2]
     scale_factor = 1.0 / math.sqrt(packs[0].shape[1])
     line = lax.broadcasted_iota(jnp.int32, (8, rows), 0)
     for step in range(blocks):
-        row_dot = jnp.where(line == 0, side_of(packs[step])[1], 0.0).T[:, 0:1]
+        row_dot = jnp.where(line == 0, side_of(late[step])[0], 0.0).T[:, 0:1]
         query_step = None
         for far in range(2):
             other = (step + 1 + far) % blocks
-            grad_attention = times(part_of(packs[step], 3), part_of(packs[other], 2), 1, 1)
+            grad_attention = times(part_of(late[step], 1), part_of(late[other], 0), 1, 1)
             slope = weight_ref[step, far] * (grad_attention - row_dot) * scale_factor
             slope = slope.astype(jnp.bfloat16)
             slope_ref[step, far] = slope
@@ -346,6 +388,36 @@
         first, second = total[:, :width], total[:, width:]
         keep_ref[where] = jnp.where(core == 0, first, second).astype(jnp.bfloat16)
         send_ref[where] = jnp.where(core == 0, second, first).astype(jnp.bfloat16)
+
+
+def turn_kernel(place_ref, input_ref, out_ref):
+    out_ref[...] = input_ref[0].T
+
+
+def factor_kernel(place_ref, factor_ref, out_ref):
+    total = jnp.sum(factor_ref[...], axis=1, keepdims=True)
+    out_ref[...] = jnp.broadcast_to(total, out_ref.shape)
+
+
+def output_kernel(blocks, place_ref, context_ref, grad_ref, keep_ref, send_ref):
+    features, width = keep_ref.shape[1:]
+    chunk = features // blocks
+    core = place_ref[2]
+    for index in range(blocks):
+        where = slice(index * chunk, (index + 1) * chunk)
+        total = times(grad_ref[0, :, where], context_ref[0], 0, 0)
+        for chip in range(blocks):
+            first = total[:, 2 * chip * width : (2 * chip + 1) * width]
+            second = total[:, (2 * chip + 1) * width : (2 * chip + 2) * width]
+            keep_ref[chip, where] = jnp.where(core == 0, first, second).astype(jnp.bfloat16)
+            send_ref[chip, where] = jnp.where(core == 0, second, first).astype(jnp.bfloat16)
+
+
+def pair_kernel(place_ref, keep_ref, other_ref, *outs):
+    for index, out in enumerate(outs):
+        chip = lax.bitwise_xor(place_ref[1], index)
+        total = keep_ref[chip].astype(jnp.float32) + other_ref[chip].astype(jnp.float32)
+        out[...] = total.astype(jnp.bfloat16)
 
 
 def near_kernel(place_ref, *refs):
@@ -414,56 +486,51 @@
     def low(*shape):
         return jax.ShapeDtypeStruct(shape, jnp.bfloat16)
 
-    sent = call(
-        lambda *refs: pack_kernel(blocks, *refs),
-        [low(4 * rows + 16, head_size)] * blocks,
-        queries,
-        key_rows,
-        value_rows,
-        grad_context,
-        context,
-        earlier_mass,
-        documents,
-        scratch=[pltpu.VMEM((1, rows, units), jnp.bfloat16)] * 5
-        + [
+    def heads_moved(kernel, arrays, scratch, mib):
+        sent = call(
+            lambda *refs: kernel(blocks, *refs),
+            [low(2 * rows + 16, head_size)] * blocks,
+            *arrays,
+            scratch=scratch + [pltpu.SemaphoreType.DMA((2 * blocks + 2,))],
+            read=pl.BlockSpec(memory_space=pltpu.HBM),
+            mib=mib,
+        )
+        moved = [sent[0]] + [None] * (blocks - 1)
+        for step in range(1, blocks):
+            moved[blocks - step] = rotated(sent[step], step)
+        return moved
+
+    early = heads_moved(
+        pack_early_kernel,
+        (queries, key_rows, earlier_mass, documents),
+        [
             pltpu.VMEM(earlier_mass.shape, jnp.float32),
             pltpu.VMEM(documents.shape, jnp.int32),
-            pltpu.VMEM((128, rows), jnp.float32),
-            pltpu.SemaphoreType.DMA((7,)),
         ],
-        read=pl.BlockSpec(memory_space=pltpu.HBM),
-        mib=58,
-    )
-    packs = [sent[0]] + [None] * (blocks - 1)
-    for step in range(1, blocks):
-        packs[blocks - step] = rotated(sent[step], step)
-
-    turned = layer_input[0].T
+        58,
+    )
+    late = heads_moved(
+        pack_late_kernel,
+        (value_rows, grad_context, context),
+        [pltpu.VMEM((1, rows, units), jnp.bfloat16)] * 2 + [pltpu.VMEM((128, rows), jnp.float32)],
+        12,
+    )
+
+    (turned,) = call(turn_kernel, [low(features, rows)], layer_input)
     mid = features // 2
     beside, below = swapped(turned, 2), swapped(turned, 4)
     upper = swapped(beside[:mid], 4)
     lower = swapped(below[mid:], 2)
 
-    part_output = jnp.einsum(
-        "th,td->dh", context[0], grad_output[0], preferred_element_type=jnp.float32
-    ).astype(jnp.bfloat16)
-
-    def columns_for(core_index):
-        return jnp.stack(
-            [
-                lax.dynamic_slice(part_output, (0, (2 * g + core_index) * width), (features, width))
-                for g in range(blocks)
-            ]
-        )
-
-    chip_output = (
-        columns_for(core).astype(jnp.float32)
-        + swapped(columns_for(1 - core), 1).astype(jnp.float32)
-    ).astype(jnp.bfloat16)
-    output_parts = [lax.dynamic_index_in_dim(chip_output, chip, 0, False)]
-    for m in range(2, data_count, 2):
-        piece = lax.dynamic_index_in_dim(chip_output, chip ^ (m // 2), 0, False)
-        output_parts.append(swapped(piece, m))
+    keep, send = call(
+        lambda *refs: output_kernel(blocks, *refs),
+        [low(blocks, features, width)] * 2,
+        context,
+        grad_output,
+        mib=16,
+    )
+    pieces = call(pair_kernel, [low(features, width)] * blocks, keep, swapped(send, 1))
+    output_parts = [pieces[0]] + [swapped(pieces[index], 2 * index) for index in range(1, blocks)]
 
     def halved(*parts):
         chunk = features // blocks
@@ -474,22 +541,33 @@
         held, sent = call(far_kernel, [narrow, low(chunk, width)], held, other)
         return held, traded(sent, 2)
 
+    (factor_part,) = call(
+        factor_kernel, [jax.ShapeDtypeStruct((row_factor.shape[0], width), jnp.float32)], row_factor
+    )
+
     weighed = call(
         lambda *refs: weigh_kernel(blocks, *refs),
-        [low(rows, head_size)] * blocks
-        + [jax.ShapeDtypeStruct((blocks, 2, rows, rows), jnp.float32)],
-        *packs,
+        [jax.ShapeDtypeStruct((blocks, 2, rows, rows), jnp.float32)],
+        *early,
+        mib=12,
+    )
+    valued = call(
+        lambda *refs: value_kernel(blocks, *refs),
+        [low(rows, head_size)] * blocks,
+        weighed[0],
+        *late,
         mib=12,
     )
     sloped = call(
         lambda *refs: slope_kernel(blocks, *refs),
         [low(rows, head_size)] * (2 * blocks),
-        weighed[blocks],
-        *packs,
+        weighed[0],
+        *early,
+        *late,
         scratch=[pltpu.VMEM((blocks, 2, rows, rows), jnp.bfloat16)],
         mib=12,
     )
-    steps = list(weighed[:blocks]) + list(sloped)
+    steps = list(valued) + list(sloped)
     totals = {"o": halved(*output_parts)}
     for g, (name, earlier) in enumerate(
         (("v", grad_values), ("k", grad_keys), ("q", grad_queries))
@@ -520,18 +598,20 @@
     }
     all_tokens = data_count * blocks * rows
     gradient = jnp.stack([totals[name] for name in "qkvo"]) / all_tokens
-    return factored_update(gradient, weights, row_factor, column_factor, blocks, data_count)
-
-
-def factored_update(gradient, weights, row_factor, column_factor, blocks, data_count):
+    return factored_update(
+        gradient, weights, row_factor, column_factor, factor_part, blocks, data_count
+    )
+
+
+def factored_update(
+    gradient, weights, row_factor, column_factor, factor_part, blocks, data_count
+):
     matrices = gradient.shape[0]
     full_rows = gradient.shape[1] * blocks
     full_cols = gradient.shape[2] * data_count
     lanes = gradient.shape[2]
     squares = gradient * gradient + tiny_square
     row_part = jnp.sum(squares, axis=2)
-    factor_part = jnp.sum(row_factor, axis=1, keepdims=True)
-    factor_part = jnp.broadcast_to(factor_part, (matrices, lanes))
     sent = jnp.concatenate([jnp.sum(squares, axis=1), factor_part], axis=1)
     along = sent
     for step in range(1, blocks):

time: 208 us -> 192 us (0.923)
  starting transfers between devices: 54.4 us -> 83.2 us
  local copies, waits for them, and re-layouts: 20.6 us -> 2.04 us
  waiting for transfers between devices: 90.2 us -> 75.7 us
  other arithmetic: 7.76 us -> 2.75 us
  matrix products: 4.33 us -> 0 us
    ppermute x15 -> x18, waiting for transfers between devices: 56.3 us -> 33.1 us  [rotated(): return lax.ppermute(value, 'blk', pairs)]
    ppermute x15 -> x18, starting transfers between devices: 22.5 us -> 42.3 us  [rotated(): return lax.ppermute(value, 'blk', pairs)]
    unnamed x73 -> x32, local copies, waits for them, and re-layouts: 14.5 us -> 1.9 us
    ppermute x24, starting transfers between devices: 20.6 us -> 32.7 us  [swapped(): lax.ppermute(value, 'dp', [(source, source ^ mask) for source in range(co...]
    ppermute x8, waiting for transfers between devices: 21 us -> 29.5 us  [traded(): lax.ppermute(value, 'blk', [(source, source ^ mask) for source in range(c...]
    dot_general x1 -> x0, matrix products: 4.33 us -> none  [head_body(): jnp.einsum('th,td->dh', context[0], grad_output[0], preferred_element_typ...]
    another operation x1 -> x0, local copies, waits for them, and re-layouts: 3.69 us -> none  [columns_for(): jnp.stack([lax.dynamic_slice(part_output, (0, (2 * g + core_index) * widt...]
    ppermute x8, starting transfers between devices: 11.4 us -> 8.24 us  [traded(): lax.ppermute(value, 'blk', [(source, source ^ mask) for source in range(c...]
  transfers between devices with their start and end apart: 47 -> 50, of which waited for: 21 -> 28; matrix products, arithmetic and copies ran while one was open for 8% -> 0% of each run, Pallas kernels for 14% -> 13%
where the time goes in v3:
time: 192 us
  starting transfers between devices  83.2 us (43%)
  waiting for transfers between devices  75.7 us (39%)
  Pallas kernels  27.3 us (14%)
  other arithmetic  2.75 us (1%)
  local copies, waits for them, and re-layouts  2.04 us (1%)
    ppermute x18, starting transfers between devices, rotated(): return lax.ppermute(value, 'blk', pairs)  42.3 us
    ppermute x18, waiting for transfers between devices, rotated(): return lax.ppermute(value, 'blk', pairs)  33.1 us
    ppermute x24, starting transfers between devices, swapped(): lax.ppermute(value, 'dp', [(source, source ^ mask) for source in range(co...  32.7 us
    ppermute x8, waiting for transfers between devices, traded(): lax.ppermute(value, 'blk', [(source, source ^ mask) for source in range(c...  29.5 us
    pallas_call x23, Pallas kernels, call(): pl.pallas_call(kernel, out_shape=shapes, in_specs=[smem] + [read] * len(a...  27.3 us
    ppermute x24, waiting for transfers between devices, swapped(): lax.ppermute(value, 'dp', [(source, source ^ mask) for source in range(co...  13.1 us
    ppermute x8, starting transfers between devices, traded(): lax.ppermute(value, 'blk', [(source, source ^ mask) for source in range(c...  8.24 us
  transfers between devices with their start and end apart: 50, of which 28 were waited for; matrix products, arithmetic and copies ran while one was open for 0% of the time, Pallas kernels for 13%

profile of v3, /device:TPU:0, one launch (start us, length us, event | category | flops | bytes accessed | tf_op | source)
XLA Modules:
  0.0 192.3 jit_solution(5999815002737514348)
XLA Ops:
  1.3 3.2 %shard_map.167 = (bf16[528,256]{1,0:T(8,128)(2,1)}, bf16[528,256]{1,0:T(8,128)(2,1)}, bf16[528,256]{1,0:T(8,128)(2,1)}, bf16[528,256]{1,0:T(8,128)(2,1)}) custom-call(s32[3]{0:T(128)} %pad_add_fusion.place_ref.refs_0_, bf16[1,256,1024]{2,1,0:T(8,128)(2,1)} %refs_1_.3, bf16[1,256,1024]{2,1,0:T(8,128)(2,1)} %refs_2_.3, f32[1,4,256]{2,1,0:T(4,128)} %refs_3_.2, ...), custom_call_target="tpu_custom_call" | custom-call | tf_op jit(solution)/shard_map/pallas_call | solution.py:477
  4.5 5.1 %collective-permute-start.4 = (bf16[528,256]{1,0:T(8,128)(2,1)}, bf16[528,256]{1,0:T(8,128)(2,1)S(1)}, u32[]{:S(2)}, u32[]{:S(2)}) collective-permute-start(bf16[528,256]{1,0:T(8,128)(2,1)} %get-tuple-element.64), channel_id=1, source_target_pairs={{0,3},{1,0},{2,1},{3,2},{4,7},{5,4},{6,5},{7,6},{8,11},{9,8},{10,9... | collective-permute-start | bytes 811016 | tf_op jit(solution)/shard_map/ppermute | solution.py:170
  18.6 4.4 %collective-permute-start.6 = (bf16[528,256]{1,0:T(8,128)(2,1)S(1)}, bf16[528,256]{1,0:T(8,128)(2,1)S(1)}, u32[]{:S(2)}, u32[]{:S(2)}) collective-permute-start(bf16[528,256]{1,0:T(8,128)(2,1)S(1)} %copy-done.15), channel_id=1, source_target_pairs={{0,1},{1,2},{2,3},{3,0},{4,5},{5,6},{6,7},{7,4},{8,9},{9,10},{10,1... | collective-permute-start | bytes 811016 | tf_op jit(solution)/shard_map/ppermute | solution.py:170
  22.9 10.4 %collective-permute-done.5.refs_3_.refs_4_ = bf16[528,256]{1,0:T(8,128)(2,1)S(1)} collective-permute-done((bf16[528,256]{1,0:T(8,128)(2,1)}, bf16[528,256]{1,0:T(8,128)(2,1)S(1)}, u32[]{:S(2)}, u32[]{:S(2)}) %collective-permute-start.5) | collective-permute-done | bytes 270368 | tf_op jit(solution)/shard_map/ppermute | solution.py:170
  35.6 5.6 %collective-permute-done.7.refs_7_.refs_3_ = bf16[528,256]{1,0:T(8,128)(2,1)S(1)} collective-permute-done((bf16[528,256]{1,0:T(8,128)(2,1)S(1)}, bf16[528,256]{1,0:T(8,128)(2,1)S(1)}, u32[]{:S(2)}, u32[]{:S(2)}) %collective-permute-start.7) | collective-permute-done | bytes 270368 | tf_op jit(solution)/shard_map/ppermute | solution.py:170
  41.2 11.2 %collective-permute-start.9 = (bf16[528,256]{1,0:T(8,128)(2,1)S(1)}, bf16[528,256]{1,0:T(8,128)(2,1)S(1)}, u32[]{:S(2)}, u32[]{:S(2)}) collective-permute-start(bf16[528,256]{1,0:T(8,128)(2,1)S(1)} %get-tuple-element.70), channel_id=1, source_target_pairs={{0,1},{1,2},{2,3},{3,0},{4,5},{5,6},{6,7},{7,4},{8,9},{9,10},{10,1... | collective-permute-start | bytes 811016 | tf_op jit(solution)/shard_map/ppermute | solution.py:170
  52.5 2.6 %shard_map.168.refs_1_ = f32[4,2,256,256]{3,2,1,0:T(8,128)S(1)} custom-call(s32[3]{0:T(128)S(1)} %copy-done.9, bf16[528,256]{1,0:T(8,128)(2,1)S(1)} %copy-done.1, bf16[528,256]{1,0:T(8,128)(2,1)S(1)} %collective-permute-done.4.refs_2_.refs_3_, bf16[528,256]{1,0:T(8,128)(2,1)S(1)} %collective-permute-done.5.refs_3_.refs_4_, ...), custom_call_target="tpu_custom_call" | custom-call | tf_op jit(solution)/shard_map/pallas_call | solution.py:477
  58.5 2.5 %collective-permute-start.10 = (bf16[256,256]{1,0:T(8,128)(2,1)S(1)}, bf16[256,256]{1,0:T(8,128)(2,1)S(1)}, u32[]{:S(2)}, u32[]{:S(2)}) collective-permute-start(bf16[256,256]{1,0:T(8,128)(2,1)S(1)} %get-tuple-element.72), channel_id=1, source_target_pairs={{0,1},{1,2},{2,3},{3,0},{4,5},{5,6},{6,7},{7,4},{8,9},{9,10},{10,1... | collective-permute-start | bytes 393224 | tf_op jit(solution)/shard_map/ppermute | solution.py:170
  61.0 4.3 %collective-permute-done.10.refs_2_ = bf16[256,256]{1,0:T(8,128)(2,1)S(1)} collective-permute-done((bf16[256,256]{1,0:T(8,128)(2,1)S(1)}, bf16[256,256]{1,0:T(8,128)(2,1)S(1)}, u32[]{:S(2)}, u32[]{:S(2)}) %collective-permute-start.10) | collective-permute-done | bytes 131104 | tf_op jit(solution)/shard_map/ppermute | solution.py:170
  66.3 3.3 %collective-permute-done.11.refs_3_ = bf16[256,256]{1,0:T(8,128)(2,1)S(1)} collective-permute-done((bf16[256,256]{1,0:T(8,128)(2,1)S(1)}, bf16[256,256]{1,0:T(8,128)(2,1)S(1)}, u32[]{:S(2)}, u32[]{:S(2)}) %collective-permute-start.11) | collective-permute-done | bytes 131104 | tf_op jit(solution)/shard_map/ppermute | solution.py:170
  71.3 3.6 %collective-permute-start.20 = (bf16[256,256]{1,0:T(8,128)(2,1)S(1)}, bf16[256,256]{1,0:T(8,128)(2,1)S(1)}, u32[]{:S(2)}, u32[]{:S(2)}) collective-permute-start(bf16[256,256]{1,0:T(8,128)(2,1)S(1)} %get-tuple-element.87), channel_id=1, source_target_pairs={{0,2},{1,3},{2,0},{3,1},{4,6},{5,7},{6,4},{7,5},{8,10},{9,11},{10,... | collective-permute-start | bytes 393224 | tf_op jit(solution)/shard_map/ppermute | solution.py:170
  83.2 3.1 %collective-permute-start.29 = (bf16[256,256]{1,0:T(8,128)(2,1)S(1)}, bf16[256,256]{1,0:T(8,128)(2,1)S(1)}, u32[]{:S(2)}, u32[]{:S(2)}) collective-permute-start(bf16[256,256]{1,0:T(8,128)(2,1)S(1)} %get-tuple-element.101), channel_id=1, source_target_pairs={{0,2},{1,3},{2,0},{3,1},{4,6},{5,7},{6,4},{7,5},{8,10},{9,11},{10,... | collective-permute-start | bytes 393224 | tf_op jit(solution)/shard_map/ppermute | solution.py:170
  86.2 2.6 %collective-permute-done.28.refs_2_ = bf16[256,256]{1,0:T(8,128)(2,1)S(1)} collective-permute-done((bf16[256,256]{1,0:T(8,128)(2,1)S(1)}, bf16[256,256]{1,0:T(8,128)(2,1)S(1)}, u32[]{:S(2)}, u32[]{:S(2)}) %collective-permute-start.28) | collective-permute-done | bytes 131104 | tf_op jit(solution)/shard_map/ppermute | solution.py:170
  88.8 3.2 %collective-permute-start.30 = (bf16[256,256]{1,0:T(8,128)(2,1)S(1)}, bf16[256,256]{1,0:T(8,128)(2,1)S(1)}, u32[]{:S(2)}, u32[]{:S(2)}) collective-permute-start(bf16[256,256]{1,0:T(8,128)(2,1)S(1)} %get-tuple-element.102), channel_id=1, source_target_pairs={{0,3},{1,0},{2,1},{3,2},{4,7},{5,4},{6,5},{7,6},{8,11},{9,8},{10,9... | collective-permute-start | bytes 393224 | tf_op jit(solution)/shard_map/ppermute | solution.py:170
  94.5 3.3 %collective-permute-start.23 = (bf16[256,256]{1,0:T(8,128)(2,1)S(1)}, bf16[256,256]{1,0:T(8,128)(2,1)S(1)}, u32[]{:S(2)}, u32[]{:S(2)}) collective-permute-start(bf16[256,256]{1,0:T(8,128)(2,1)S(1)} %get-tuple-element.91), channel_id=1, source_target_pairs={{0,16},{4,20},{8,24},{12,28},{16,0},{20,4},{24,8},{28,12},{1,17},{... | collective-permute-start | bytes 393224 | tf_op jit(solution)/shard_map/ppermute | solution.py:164
  98.4 5.0 %collective-permute-start.24 = (bf16[256,256]{1,0:T(8,128)(2,1)S(1)}, bf16[256,256]{1,0:T(8,128)(2,1)S(1)}, u32[]{:S(2)}, u32[]{:S(2)}) collective-permute-start(bf16[256,256]{1,0:T(8,128)(2,1)S(1)} %get-tuple-element.92), channel_id=1, source_target_pairs={{0,24},{4,28},{8,16},{12,20},{16,8},{20,12},{24,0},{28,4},{1,25},{... | collective-permute-start | bytes 393224 | tf_op jit(solution)/shard_map/ppermute | solution.py:164
  107.4 2.6 %collective-permute-start.14 = (bf16[256,256]{1,0:T(8,128)(2,1)S(1)}, bf16[256,256]{1,0:T(8,128)(2,1)S(1)}, u32[]{:S(2)}, u32[]{:S(2)}) collective-permute-start(bf16[256,256]{1,0:T(8,128)(2,1)S(1)} %get-tuple-element.77), channel_id=1, source_target_pairs={{0,16},{4,20},{8,24},{12,28},{16,0},{20,4},{24,8},{28,12},{1,17},{... | collective-permute-start | bytes 393224 | tf_op jit(solution)/shard_map/ppermute | solution.py:164
  118.5 4.9 %collective-permute-done.32.refs_8_ = bf16[256,256]{1,0:T(8,128)(2,1)S(1)} collective-permute-done((bf16[256,256]{1,0:T(8,128)(2,1)S(1)}, bf16[256,256]{1,0:T(8,128)(2,1)S(1)}, u32[]{:S(2)}, u32[]{:S(2)}) %collective-permute-start.32) | collective-permute-done | bytes 131104 | tf_op jit(solution)/shard_map/ppermute | solution.py:164
  135.8 5.0 %collective-permute-done.17.other_ref = bf16[2,512,128]{2,1,0:T(8,128)(2,1)S(1)} collective-permute-done((bf16[2,512,128]{2,1,0:T(8,128)(2,1)S(1)}, bf16[2,512,128]{2,1,0:T(8,128)(2,1)S(1)}, u32[]{:S(2)}, u32[]{:S(2)}) %collective-permute-start.17) | collective-permute-done | bytes 262176 | tf_op jit(solution)/shard_map/ppermute | solution.py:175
  143.3 4.8 %collective-permute-done.35.other_ref = bf16[2,512,128]{2,1,0:T(8,128)(2,1)S(1)} collective-permute-done((bf16[2,512,128]{2,1,0:T(8,128)(2,1)S(1)}, bf16[2,512,128]{2,1,0:T(8,128)(2,1)S(1)}, u32[]{:S(2)}, u32[]{:S(2)}) %collective-permute-start.35) | collective-permute-done | bytes 262176 | tf_op jit(solution)/shard_map/ppermute | solution.py:175
  148.7 3.0 %collective-permute-start.36 = (bf16[512,128]{1,0:T(8,128)(2,1)S(1)}, bf16[512,128]{1,0:T(8,128)(2,1)S(1)}, u32[]{:S(2)}, u32[]{:S(2)}) collective-permute-start(bf16[512,128]{1,0:T(8,128)(2,1)S(1)} %get-tuple-element.112), channel_id=1, source_target_pairs={{0,2},{1,3},{2,0},{3,1},{4,6},{5,7},{6,4},{7,5},{8,10},{9,11},{10,... | collective-permute-start | bytes 393224 | tf_op jit(solution)/shard_map/ppermute | solution.py:175
  159.0 8.0 %collective-permute-done.41.other_ref = bf16[2,512,128]{2,1,0:T(8,128)(2,1)S(1)} collective-permute-done((bf16[2,512,128]{2,1,0:T(8,128)(2,1)S(1)}, bf16[2,512,128]{2,1,0:T(8,128)(2,1)S(1)}, u32[]{:S(2)}, u32[]{:S(2)}) %collective-permute-start.41) | collective-permute-done | bytes 262176 | tf_op jit(solution)/shard_map/ppermute | solution.py:175
  167.8 8.1 %collective-permute-done.42 = bf16[512,128]{1,0:T(8,128)(2,1)S(1)} collective-permute-done((bf16[512,128]{1,0:T(8,128)(2,1)S(1)}, bf16[512,128]{1,0:T(8,128)(2,1)S(1)}, u32[]{:S(2)}, u32[]{:S(2)}) %collective-permute-start.42) | collective-permute-done | bytes 131104 | tf_op jit(solution)/shard_map/ppermute | solution.py:175
  183.2 2.6 %collective-permute-start.48 = (f32[4,640]{1,0:T(4,128)S(1)}, f32[4,640]{1,0:T(4,128)S(1)}, u32[]{:S(2)}, u32[]{:S(2)}) collective-permute-start(f32[4,640]{1,0:T(4,128)S(1)} %pad_maximum_fusion.1), channel_id=1, source_target_pairs={{0,24},{4,28},{8,16},{12,20},{16,8},{20,12},{24,0},{28,4},{1,25},{... | collective-permute-start | bytes 30728 | tf_op jit(solution)/shard_map/ppermute | solution.py:164
  (149 shorter events, 78.6 us)
Async XLA Ops:
  4.5 14.1 %collective-permute-start.4 = (bf16[528,256]{1,0:T(8,128)(2,1)}, bf16[528,256]{1,0:T(8,128)(2,1)S(1)}, u32[]{:S(2)}, u32[]{:S(2)}) collective-permute-start(bf16[528,256]{1,0:T(8,128)(2,1)} %get-tuple-element.64), channel_id=1, source_target_pairs={{0,3},{1,0},{2,1},{3,2},{4,7},{5,4},{6,5},{7,6},{8,11},{9,8},{10,9... | collective-permute-start | bytes 811016 | tf_op jit(solution)/shard_map/ppermute | solution.py:170
  9.6 23.7 %collective-permute-start.5 = (bf16[528,256]{1,0:T(8,128)(2,1)}, bf16[528,256]{1,0:T(8,128)(2,1)S(1)}, u32[]{:S(2)}, u32[]{:S(2)}) collective-permute-start(bf16[528,256]{1,0:T(8,128)(2,1)} %get-tuple-element.65), channel_id=1, source_target_pairs={{0,2},{1,3},{2,0},{3,1},{4,6},{5,7},{6,4},{7,5},{8,10},{9,11},{10,... | collective-permute-start | bytes 811016 | tf_op jit(solution)/shard_map/ppermute | solution.py:170
  12.3 62.7 %collective-permute-start.1 = (bf16[2048,256]{1,0:T(8,128)(2,1)S(1)}, bf16[2048,256]{1,0:T(8,128)(2,1)S(1)}, u32[]{:S(2)}, u32[]{:S(2)}) collective-permute-start(bf16[2048,256]{1,0:T(8,128)(2,1)S(1)} %shard_map.166.refs_1_), channel_id=1, source_target_pairs={{0,16},{4,20},{8,24},{12,28},{16,0},{20,4},{24,8},{28,12},{1,17},{... | collective-permute-start | bytes 3145736 | tf_op jit(solution)/shard_map/ppermute | solution.py:164
  13.9 61.1 %collective-permute-start = (bf16[2048,256]{1,0:T(8,128)(2,1)S(1)}, bf16[2048,256]{1,0:T(8,128)(2,1)S(1)}, u32[]{:S(2)}, u32[]{:S(2)}) collective-permute-start(bf16[2048,256]{1,0:T(8,128)(2,1)S(1)} %shard_map.166.refs_1_), channel_id=1, source_target_pairs={{0,8},{4,12},{8,0},{12,4},{16,24},{20,28},{24,16},{28,20},{1,9},{5... | collective-permute-start | bytes 3145736 | tf_op jit(solution)/shard_map/ppermute | solution.py:164
  17.2 108.8 %collective-permute-start.37 = (bf16[4,2048,128]{2,1,0:T(8,128)(2,1)S(1)}, bf16[4,2048,128]{2,1,0:T(8,128)(2,1)S(1)}, u32[]{:S(2)}, u32[]{:S(2)}) collective-permute-start(bf16[4,2048,128]{2,1,0:T(8,128)(2,1)S(1)} %get-tuple-element.114), channel_id=1, source_target_pairs={{0,4},{4,0},{8,12},{12,8},{16,20},{20,16},{24,28},{28,24},{1,5},{5... | collective-permute-start | bytes 6291464 | tf_op jit(solution)/shard_map/ppermute | solution.py:164
  18.6 14.8 %collective-permute-start.6 = (bf16[528,256]{1,0:T(8,128)(2,1)S(1)}, bf16[528,256]{1,0:T(8,128)(2,1)S(1)}, u32[]{:S(2)}, u32[]{:S(2)}) collective-permute-start(bf16[528,256]{1,0:T(8,128)(2,1)S(1)} %copy-done.15), channel_id=1, source_target_pairs={{0,1},{1,2},{2,3},{3,0},{4,5},{5,6},{6,7},{7,4},{8,9},{9,10},{10,1... | collective-permute-start | bytes 811016 | tf_op jit(solution)/shard_map/ppermute | solution.py:170
  33.3 22.7 %collective-permute-start.8 = (bf16[528,256]{1,0:T(8,128)(2,1)S(1)}, bf16[528,256]{1,0:T(8,128)(2,1)S(1)}, u32[]{:S(2)}, u32[]{:S(2)}) collective-permute-start(bf16[528,256]{1,0:T(8,128)(2,1)S(1)} %get-tuple-element.69), channel_id=1, source_target_pairs={{0,2},{1,3},{2,0},{3,1},{4,6},{5,7},{6,4},{7,5},{8,10},{9,11},{10,... | collective-permute-start | bytes 811016 | tf_op jit(solution)/shard_map/ppermute | solution.py:170
  41.2 15.2 %collective-permute-start.9 = (bf16[528,256]{1,0:T(8,128)(2,1)S(1)}, bf16[528,256]{1,0:T(8,128)(2,1)S(1)}, u32[]{:S(2)}, u32[]{:S(2)}) collective-permute-start(bf16[528,256]{1,0:T(8,128)(2,1)S(1)} %get-tuple-element.70), channel_id=1, source_target_pairs={{0,1},{1,2},{2,3},{3,0},{4,5},{5,6},{6,7},{7,4},{8,9},{9,10},{10,1... | collective-permute-start | bytes 811016 | tf_op jit(solution)/shard_map/ppermute | solution.py:170
  71.3 9.9 %collective-permute-start.20 = (bf16[256,256]{1,0:T(8,128)(2,1)S(1)}, bf16[256,256]{1,0:T(8,128)(2,1)S(1)}, u32[]{:S(2)}, u32[]{:S(2)}) collective-permute-start(bf16[256,256]{1,0:T(8,128)(2,1)S(1)} %get-tuple-element.87), channel_id=1, source_target_pairs={{0,2},{1,3},{2,0},{3,1},{4,6},{5,7},{6,4},{7,5},{8,10},{9,11},{10,... | collective-permute-start | bytes 393224 | tf_op jit(solution)/shard_map/ppermute | solution.py:170
  75.0 35.0 %collective-permute-start.3 = (bf16[1024,256]{1,0:T(8,128)(2,1)S(1)}, bf16[1024,256]{1,0:T(8,128)(2,1)S(1)}, u32[]{:S(2)}, u32[]{:S(2)}) collective-permute-start(bf16[1024,256]{1,0:T(8,128)(2,1)S(1)} %slice.25), channel_id=1, source_target_pairs={{0,8},{4,12},{8,0},{12,4},{16,24},{20,28},{24,16},{28,20},{1,9},{5... | collective-permute-start | bytes 1572872 | tf_op jit(solution)/shard_map/ppermute | solution.py:164
  77.7 33.3 %collective-permute-start.2 = (bf16[1024,256]{1,0:T(8,128)(2,1)S(1)}, bf16[1024,256]{1,0:T(8,128)(2,1)S(1)}, u32[]{:S(2)}, u32[]{:S(2)}) collective-permute-start(bf16[1024,256]{1,0:T(8,128)(2,1)S(1)} %slice.24), channel_id=1, source_target_pairs={{0,16},{4,20},{8,24},{12,28},{16,0},{20,4},{24,8},{28,12},{1,17},{... | collective-permute-start | bytes 1572872 | tf_op jit(solution)/shard_map/ppermute | solution.py:164
  83.2 9.7 %collective-permute-start.29 = (bf16[256,256]{1,0:T(8,128)(2,1)S(1)}, bf16[256,256]{1,0:T(8,128)(2,1)S(1)}, u32[]{:S(2)}, u32[]{:S(2)}) collective-permute-start(bf16[256,256]{1,0:T(8,128)(2,1)S(1)} %get-tuple-element.101), channel_id=1, source_target_pairs={{0,2},{1,3},{2,0},{3,1},{4,6},{5,7},{6,4},{7,5},{8,10},{9,11},{10,... | collective-permute-start | bytes 393224 | tf_op jit(solution)/shard_map/ppermute | solution.py:170
  94.5 9.6 %collective-permute-start.23 = (bf16[256,256]{1,0:T(8,128)(2,1)S(1)}, bf16[256,256]{1,0:T(8,128)(2,1)S(1)}, u32[]{:S(2)}, u32[]{:S(2)}) collective-permute-start(bf16[256,256]{1,0:T(8,128)(2,1)S(1)} %get-tuple-element.91), channel_id=1, source_target_pairs={{0,16},{4,20},{8,24},{12,28},{16,0},{20,4},{24,8},{28,12},{1,17},{... | collective-permute-start | bytes 393224 | tf_op jit(solution)/shard_map/ppermute | solution.py:164
  104.1 10.3 %collective-permute-start.13 = (bf16[256,256]{1,0:T(8,128)(2,1)S(1)}, bf16[256,256]{1,0:T(8,128)(2,1)S(1)}, u32[]{:S(2)}, u32[]{:S(2)}) collective-permute-start(bf16[256,256]{1,0:T(8,128)(2,1)S(1)} %get-tuple-element.76), channel_id=1, source_target_pairs={{0,8},{4,12},{8,0},{12,4},{16,24},{20,28},{24,16},{28,20},{1,9},{5... | collective-permute-start | bytes 393224 | tf_op jit(solution)/shard_map/ppermute | solution.py:164
  114.4 10.9 %collective-permute-start.25 = (bf16[2048,128]{1,0:T(8,128)(2,1)S(1)}, bf16[2048,128]{1,0:T(8,128)(2,1)S(1)}, u32[]{:S(2)}, u32[]{:S(2)}) collective-permute-start(bf16[2048,128]{1,0:T(8,128)(2,1)S(1)} %get-tuple-element.94), channel_id=1, source_target_pairs={{0,4},{4,0},{8,12},{12,8},{16,20},{20,16},{24,28},{28,24},{1,5},{5... | collective-permute-start | bytes 1572872 | tf_op jit(solution)/shard_map/ppermute | solution.py:164
  118.3 11.4 %collective-permute-start.16 = (bf16[2048,128]{1,0:T(8,128)(2,1)S(1)}, bf16[2048,128]{1,0:T(8,128)(2,1)S(1)}, u32[]{:S(2)}, u32[]{:S(2)}) collective-permute-start(bf16[2048,128]{1,0:T(8,128)(2,1)S(1)} %get-tuple-element.80), channel_id=1, source_target_pairs={{0,4},{4,0},{8,12},{12,8},{16,20},{20,16},{24,28},{28,24},{1,5},{5... | collective-permute-start | bytes 1572872 | tf_op jit(solution)/shard_map/ppermute | solution.py:164
  127.1 21.6 %collective-permute-start.38 = (bf16[2048,128]{1,0:T(8,128)(2,1)S(1)}, bf16[2048,128]{1,0:T(8,128)(2,1)S(1)}, u32[]{:S(2)}, u32[]{:S(2)}) collective-permute-start(bf16[2048,128]{1,0:T(8,128)(2,1)S(1)} %get-tuple-element.116), channel_id=1, source_target_pairs={{0,8},{4,12},{8,0},{12,4},{16,24},{20,28},{24,16},{28,20},{1,9},{5... | collective-permute-start | bytes 1572872 | tf_op jit(solution)/shard_map/ppermute | solution.py:164
  127.9 24.3 %collective-permute-start.39 = (bf16[2048,128]{1,0:T(8,128)(2,1)S(1)}, bf16[2048,128]{1,0:T(8,128)(2,1)S(1)}, u32[]{:S(2)}, u32[]{:S(2)}) collective-permute-start(bf16[2048,128]{1,0:T(8,128)(2,1)S(1)} %get-tuple-element.117), channel_id=1, source_target_pairs={{0,16},{4,20},{8,24},{12,28},{16,0},{20,4},{24,8},{28,12},{1,17},{... | collective-permute-start | bytes 1572872 | tf_op jit(solution)/shard_map/ppermute | solution.py:164
  129.7 24.2 %collective-permute-start.40 = (bf16[2048,128]{1,0:T(8,128)(2,1)S(1)}, bf16[2048,128]{1,0:T(8,128)(2,1)S(1)}, u32[]{:S(2)}, u32[]{:S(2)}) collective-permute-start(bf16[2048,128]{1,0:T(8,128)(2,1)S(1)} %get-tuple-element.118), channel_id=1, source_target_pairs={{0,24},{4,28},{8,16},{12,20},{16,8},{20,12},{24,0},{28,4},{1,25},{... | collective-permute-start | bytes 1572872 | tf_op jit(solution)/shard_map/ppermute | solution.py:164
  135.2 12.9 %collective-permute-start.35 = (bf16[2,512,128]{2,1,0:T(8,128)(2,1)S(1)}, bf16[2,512,128]{2,1,0:T(8,128)(2,1)S(1)}, u32[]{:S(2)}, u32[]{:S(2)}) collective-permute-start(bf16[2,512,128]{2,1,0:T(8,128)(2,1)S(1)} %get-tuple-element.110), channel_id=1, source_target_pairs={{0,1},{1,0},{2,3},{3,2},{4,5},{5,4},{6,7},{7,6},{8,9},{9,8},{10,11... | collective-permute-start | bytes 786440 | tf_op jit(solution)/shard_map/ppermute | solution.py:175
  140.8 15.7 %collective-permute-start.27 = (bf16[512,128]{1,0:T(8,128)(2,1)S(1)}, bf16[512,128]{1,0:T(8,128)(2,1)S(1)}, u32[]{:S(2)}, u32[]{:S(2)}) collective-permute-start(bf16[512,128]{1,0:T(8,128)(2,1)S(1)} %get-tuple-element.98), channel_id=1, source_target_pairs={{0,2},{1,3},{2,0},{3,1},{4,6},{5,7},{6,4},{7,5},{8,10},{9,11},{10,... | collective-permute-start | bytes 393224 | tf_op jit(solution)/shard_map/ppermute | solution.py:175
  148.1 10.9 %collective-permute-start.18 = (bf16[512,128]{1,0:T(8,128)(2,1)S(1)}, bf16[512,128]{1,0:T(8,128)(2,1)S(1)}, u32[]{:S(2)}, u32[]{:S(2)}) collective-permute-start(bf16[512,128]{1,0:T(8,128)(2,1)S(1)} %get-tuple-element.84), channel_id=1, source_target_pairs={{0,2},{1,3},{2,0},{3,1},{4,6},{5,7},{6,4},{7,5},{8,10},{9,11},{10,... | collective-permute-start | bytes 393224 | tf_op jit(solution)/shard_map/ppermute | solution.py:175
  148.7 19.0 %collective-permute-start.36 = (bf16[512,128]{1,0:T(8,128)(2,1)S(1)}, bf16[512,128]{1,0:T(8,128)(2,1)S(1)}, u32[]{:S(2)}, u32[]{:S(2)}) collective-permute-start(bf16[512,128]{1,0:T(8,128)(2,1)S(1)} %get-tuple-element.112), channel_id=1, source_target_pairs={{0,2},{1,3},{2,0},{3,1},{4,6},{5,7},{6,4},{7,5},{8,10},{9,11},{10,... | collective-permute-start | bytes 393224 | tf_op jit(solution)/shard_map/ppermute | solution.py:175
  154.7 12.4 %collective-permute-start.41 = (bf16[2,512,128]{2,1,0:T(8,128)(2,1)S(1)}, bf16[2,512,128]{2,1,0:T(8,128)(2,1)S(1)}, u32[]{:S(2)}, u32[]{:S(2)}) collective-permute-start(bf16[2,512,128]{2,1,0:T(8,128)(2,1)S(1)} %get-tuple-element.120), channel_id=1, source_target_pairs={{0,1},{1,0},{2,3},{3,2},{4,5},{5,4},{6,7},{7,6},{8,9},{9,8},{10,11... | collective-permute-start | bytes 786440 | tf_op jit(solution)/shard_map/ppermute | solution.py:175
  (42 other events, 418.8 us)

commit v4 on v3

--- a/solution.py
+++ b/solution.py
@@ -208,22 +208,31 @@
     return copies
 
 
-def pack_early_kernel(blocks, place_ref, query_ref, key_ref, mass_ref, docs_ref, *refs):
-    outs, held, arrived = refs[:blocks], refs[blocks : blocks + 2], refs[blocks + 2]
+def pack_early_kernel(blocks, query_ref, key_ref, mass_ref, docs_ref, *refs):
+    outs, held = refs[:blocks], refs[blocks : blocks + 2]
+    packed_ref, arrived, left = refs[blocks + 2 :]
+    place = (lax.axis_index("blk"),)
+    slots = [packed_ref.at[step] for step in range(blocks)]
     small = held_copies((mass_ref, docs_ref), held, arrived, 2 * blocks)
-    copies = pack_heads(blocks, place_ref, (query_ref, key_ref), outs, arrived)
+    copies = pack_heads(blocks, place, (query_ref, key_ref), slots, arrived)
     rows = docs_ref.shape[1]
     line = lax.broadcasted_iota(jnp.int32, (16, rows), 0)
     for copy in small:
         copy.wait()
     docs = held[1][...].astype(jnp.float32)
     for step in range(blocks):
-        head = lax.rem(place_ref[0] + step, blocks)
+        head = lax.rem(place[0] + step, blocks)
         side = jnp.where(line == 3, docs, 0.0)
         for index, term in enumerate(split_three(held[0][0, pl.ds(head, 1), :])):
             side = jnp.where(line == index, term, side)
-        outs[step][2 * rows :] = side.astype(jnp.bfloat16)
-    for copy in copies:
+        packed_ref[step, 2 * rows :] = side.astype(jnp.bfloat16)
+    leaving = []
+    for step in [*range(1, blocks), 0]:
+        for copy in copies[2 * step : 2 * step + 2]:
+            copy.wait()
+        leaving.append(pltpu.make_async_copy(packed_ref.at[step], outs[step], left.at[step]))
+        leaving[-1].start()
+    for copy in leaving:
         copy.wait()
 
 
@@ -473,27 +482,29 @@
     smem = pl.BlockSpec(memory_space=pltpu.SMEM)
     place = jnp.stack([block, chip, core])
 
-    def call(kernel, shapes, *arrays, scratch=(), read=vmem, mib=4):
-        return pl.pallas_call(
+    def call(kernel, shapes, *arrays, scratch=(), read=vmem, mib=4, placed=True):
+        made = pl.pallas_call(
             kernel,
             out_shape=shapes,
-            in_specs=[smem] + [read] * len(arrays),
-            out_specs=[vmem] * len(shapes),
+            in_specs=[smem] * placed + [read] * len(arrays),
+            out_specs=[vmem if placed else read] * len(shapes),
             scratch_shapes=list(scratch),
             compiler_params=pltpu.CompilerParams(vmem_limit_bytes=mib * 2**20),
-        )(place, *arrays)
+        )
+        return made(place, *arrays) if placed else made(*arrays)
 
     def low(*shape):
         return jax.ShapeDtypeStruct(shape, jnp.bfloat16)
 
-    def heads_moved(kernel, arrays, scratch, mib):
+    def heads_moved(kernel, arrays, scratch, mib, placed):
         sent = call(
             lambda *refs: kernel(blocks, *refs),
             [low(2 * rows + 16, head_size)] * blocks,
             *arrays,
-            scratch=scratch + [pltpu.SemaphoreType.DMA((2 * blocks + 2,))],
+            scratch=scratch,
             read=pl.BlockSpec(memory_space=pltpu.HBM),
             mib=mib,
+            placed=placed,
         )
         moved = [sent[0]] + [None] * (blocks - 1)
         for step in range(1, blocks):
@@ -506,14 +517,20 @@
         [
             pltpu.VMEM(earlier_mass.shape, jnp.float32),
             pltpu.VMEM(documents.shape, jnp.int32),
+            pltpu.VMEM((blocks, 2 * rows + 16, head_size), jnp.bfloat16),
+            pltpu.SemaphoreType.DMA((2 * blocks + 2,)),
+            pltpu.SemaphoreType.DMA((blocks,)),
         ],
         58,
+        False,
     )
     late = heads_moved(
         pack_late_kernel,
         (value_rows, grad_context, context),
-        [pltpu.VMEM((1, rows, units), jnp.bfloat16)] * 2 + [pltpu.VMEM((128, rows), jnp.float32)],
+        [pltpu.VMEM((1, rows, units), jnp.bfloat16)] * 2
+        + [pltpu.VMEM((128, rows), jnp.float32), pltpu.SemaphoreType.DMA((2 * blocks + 2,))],
         12,
+        True,
     )
 
     (turned,) = call(turn_kernel, [low(features, rows)], layer_input)

time: 192 us -> 190 us (0.990)
  waiting for transfers between devices: 75.7 us -> 73 us
  starting transfers between devices: 83.2 us -> 85.8 us
  transfers between devices with their start and end apart: 50 -> 50, of which waited for: 28 -> 26; matrix products, arithmetic and copies ran while one was open for 0% -> 0% of each run, Pallas kernels for 13% -> 13%
where the time goes in v4:
time: 190 us
  starting transfers between devices  85.8 us (45%)
  waiting for transfers between devices  73 us (38%)
  Pallas kernels  26.5 us (14%)
  other arithmetic  2.22 us (1%)
    ppermute x18, starting transfers between devices, rotated(): return lax.ppermute(value, 'blk', pairs)  42.5 us
    ppermute x24, starting transfers between devices, swapped(): lax.ppermute(value, 'dp', [(source, source ^ mask) for source in range(co...  33.2 us
    ppermute x18, waiting for transfers between devices, rotated(): return lax.ppermute(value, 'blk', pairs)  32.6 us
    ppermute x8, waiting for transfers between devices, traded(): lax.ppermute(value, 'blk', [(source, source ^ mask) for source in range(c...  27.7 us
    pallas_call x23, Pallas kernels, call(): return made(place, *arrays) if placed else made(*arrays)  26.5 us
    ppermute x24, waiting for transfers between devices, swapped(): lax.ppermute(value, 'dp', [(source, source ^ mask) for source in range(co...  12.7 us
    ppermute x8, starting transfers between devices, traded(): lax.ppermute(value, 'blk', [(source, source ^ mask) for source in range(c...  10.1 us
  transfers between devices with their start and end apart: 50, of which 26 were waited for; matrix products, arithmetic and copies ran while one was open for 0% of the time, Pallas kernels for 13%

profile of v4, /device:TPU:0, one launch (start us, length us, event | category | flops | bytes accessed | tf_op | source)
XLA Modules:
  0.0 190.1 jit_solution(10673983448765195296)
XLA Ops:
  3.0 5.1 %collective-permute-start.4 = (bf16[528,256]{1,0:T(8,128)(2,1)}, bf16[528,256]{1,0:T(8,128)(2,1)S(1)}, u32[]{:S(2)}, u32[]{:S(2)}) collective-permute-start(bf16[528,256]{1,0:T(8,128)(2,1)} %get-tuple-element.64), channel_id=1, source_target_pairs={{0,3},{1,0},{2,1},{3,2},{4,7},{5,4},{6,5},{7,6},{8,11},{9,8},{10,9... | collective-permute-start | bytes 811016 | tf_op jit(solution)/shard_map/ppermute | solution.py:170
  16.6 4.9 %collective-permute-start.6 = (bf16[528,256]{1,0:T(8,128)(2,1)S(1)}, bf16[528,256]{1,0:T(8,128)(2,1)S(1)}, u32[]{:S(2)}, u32[]{:S(2)}) collective-permute-start(bf16[528,256]{1,0:T(8,128)(2,1)S(1)} %copy-done.14), channel_id=1, source_target_pairs={{0,1},{1,2},{2,3},{3,0},{4,5},{5,6},{6,7},{7,4},{8,9},{9,10},{10,1... | collective-permute-start | bytes 811016 | tf_op jit(solution)/shard_map/ppermute | solution.py:170
  21.5 10.4 %collective-permute-done.5.refs_3_.refs_4_ = bf16[528,256]{1,0:T(8,128)(2,1)S(1)} collective-permute-done((bf16[528,256]{1,0:T(8,128)(2,1)}, bf16[528,256]{1,0:T(8,128)(2,1)S(1)}, u32[]{:S(2)}, u32[]{:S(2)}) %collective-permute-start.5) | collective-permute-done | bytes 270368 | tf_op jit(solution)/shard_map/ppermute | solution.py:170
  34.2 5.6 %collective-permute-done.7.refs_7_.refs_3_ = bf16[528,256]{1,0:T(8,128)(2,1)S(1)} collective-permute-done((bf16[528,256]{1,0:T(8,128)(2,1)S(1)}, bf16[528,256]{1,0:T(8,128)(2,1)S(1)}, u32[]{:S(2)}, u32[]{:S(2)}) %collective-permute-start.7) | collective-permute-done | bytes 270368 | tf_op jit(solution)/shard_map/ppermute | solution.py:170
  39.8 11.2 %collective-permute-start.9 = (bf16[528,256]{1,0:T(8,128)(2,1)S(1)}, bf16[528,256]{1,0:T(8,128)(2,1)S(1)}, u32[]{:S(2)}, u32[]{:S(2)}) collective-permute-start(bf16[528,256]{1,0:T(8,128)(2,1)S(1)} %get-tuple-element.70), channel_id=1, source_target_pairs={{0,1},{1,2},{2,3},{3,0},{4,5},{5,6},{6,7},{7,4},{8,9},{9,10},{10,1... | collective-permute-start | bytes 811016 | tf_op jit(solution)/shard_map/ppermute | solution.py:170
  51.0 2.6 %shard_map.168.refs_1_ = f32[4,2,256,256]{3,2,1,0:T(8,128)S(1)} custom-call(s32[3]{0:T(128)S(1)} %pad_add_fusion.place_ref.refs_0_, bf16[528,256]{1,0:T(8,128)(2,1)S(1)} %copy-done.1, bf16[528,256]{1,0:T(8,128)(2,1)S(1)} %collective-permute-done.4.refs_2_.refs_3_, bf16[528,256]{1,0:T(8,128)(2,1)S(1)} %collective-permute-done.5.refs_3_.refs_4_, ...), custom_call_target="tpu_custom_call" | custom-call | tf_op jit(solution)/shard_map/pallas_call | solution.py:494
  57.0 2.5 %collective-permute-start.10 = (bf16[256,256]{1,0:T(8,128)(2,1)S(1)}, bf16[256,256]{1,0:T(8,128)(2,1)S(1)}, u32[]{:S(2)}, u32[]{:S(2)}) collective-permute-start(bf16[256,256]{1,0:T(8,128)(2,1)S(1)} %get-tuple-element.72), channel_id=1, source_target_pairs={{0,1},{1,2},{2,3},{3,0},{4,5},{5,6},{6,7},{7,4},{8,9},{9,10},{10,1... | collective-permute-start | bytes 393224 | tf_op jit(solution)/shard_map/ppermute | solution.py:170
  59.5 4.3 %collective-permute-done.10.refs_2_ = bf16[256,256]{1,0:T(8,128)(2,1)S(1)} collective-permute-done((bf16[256,256]{1,0:T(8,128)(2,1)S(1)}, bf16[256,256]{1,0:T(8,128)(2,1)S(1)}, u32[]{:S(2)}, u32[]{:S(2)}) %collective-permute-start.10) | collective-permute-done | bytes 131104 | tf_op jit(solution)/shard_map/ppermute | solution.py:170
  64.8 3.3 %collective-permute-done.11.refs_3_ = bf16[256,256]{1,0:T(8,128)(2,1)S(1)} collective-permute-done((bf16[256,256]{1,0:T(8,128)(2,1)S(1)}, bf16[256,256]{1,0:T(8,128)(2,1)S(1)}, u32[]{:S(2)}, u32[]{:S(2)}) %collective-permute-start.11) | collective-permute-done | bytes 131104 | tf_op jit(solution)/shard_map/ppermute | solution.py:170
  69.9 3.6 %collective-permute-start.20 = (bf16[256,256]{1,0:T(8,128)(2,1)S(1)}, bf16[256,256]{1,0:T(8,128)(2,1)S(1)}, u32[]{:S(2)}, u32[]{:S(2)}) collective-permute-start(bf16[256,256]{1,0:T(8,128)(2,1)S(1)} %get-tuple-element.87), channel_id=1, source_target_pairs={{0,2},{1,3},{2,0},{3,1},{4,6},{5,7},{6,4},{7,5},{8,10},{9,11},{10,... | collective-permute-start | bytes 393224 | tf_op jit(solution)/shard_map/ppermute | solution.py:170
  73.6 3.3 %collective-permute-start.3 = (bf16[1024,256]{1,0:T(8,128)(2,1)S(1)}, bf16[1024,256]{1,0:T(8,128)(2,1)S(1)}, u32[]{:S(2)}, u32[]{:S(2)}) collective-permute-start(bf16[1024,256]{1,0:T(8,128)(2,1)S(1)} %slice.25), channel_id=1, source_target_pairs={{0,8},{4,12},{8,0},{12,4},{16,24},{20,28},{24,16},{28,20},{1,9},{5... | collective-permute-start | bytes 1572872 | tf_op jit(solution)/shard_map/ppermute | solution.py:164
  81.7 3.1 %collective-permute-start.29 = (bf16[256,256]{1,0:T(8,128)(2,1)S(1)}, bf16[256,256]{1,0:T(8,128)(2,1)S(1)}, u32[]{:S(2)}, u32[]{:S(2)}) collective-permute-start(bf16[256,256]{1,0:T(8,128)(2,1)S(1)} %get-tuple-element.101), channel_id=1, source_target_pairs={{0,2},{1,3},{2,0},{3,1},{4,6},{5,7},{6,4},{7,5},{8,10},{9,11},{10,... | collective-permute-start | bytes 393224 | tf_op jit(solution)/shard_map/ppermute | solution.py:170
  84.8 2.6 %collective-permute-done.28.refs_2_ = bf16[256,256]{1,0:T(8,128)(2,1)S(1)} collective-permute-done((bf16[256,256]{1,0:T(8,128)(2,1)S(1)}, bf16[256,256]{1,0:T(8,128)(2,1)S(1)}, u32[]{:S(2)}, u32[]{:S(2)}) %collective-permute-start.28) | collective-permute-done | bytes 131104 | tf_op jit(solution)/shard_map/ppermute | solution.py:170
  87.3 3.2 %collective-permute-start.30 = (bf16[256,256]{1,0:T(8,128)(2,1)S(1)}, bf16[256,256]{1,0:T(8,128)(2,1)S(1)}, u32[]{:S(2)}, u32[]{:S(2)}) collective-permute-start(bf16[256,256]{1,0:T(8,128)(2,1)S(1)} %get-tuple-element.102), channel_id=1, source_target_pairs={{0,3},{1,0},{2,1},{3,2},{4,7},{5,4},{6,5},{7,6},{8,11},{9,8},{10,9... | collective-permute-start | bytes 393224 | tf_op jit(solution)/shard_map/ppermute | solution.py:170
  91.5 3.4 %collective-permute-start.22 = (bf16[256,256]{1,0:T(8,128)(2,1)S(1)}, bf16[256,256]{1,0:T(8,128)(2,1)S(1)}, u32[]{:S(2)}, u32[]{:S(2)}) collective-permute-start(bf16[256,256]{1,0:T(8,128)(2,1)S(1)} %get-tuple-element.90), channel_id=1, source_target_pairs={{0,8},{4,12},{8,0},{12,4},{16,24},{20,28},{24,16},{28,20},{1,9},{5... | collective-permute-start | bytes 393224 | tf_op jit(solution)/shard_map/ppermute | solution.py:164
  94.8 3.2 %collective-permute-start.23 = (bf16[256,256]{1,0:T(8,128)(2,1)S(1)}, bf16[256,256]{1,0:T(8,128)(2,1)S(1)}, u32[]{:S(2)}, u32[]{:S(2)}) collective-permute-start(bf16[256,256]{1,0:T(8,128)(2,1)S(1)} %get-tuple-element.91), channel_id=1, source_target_pairs={{0,16},{4,20},{8,24},{12,28},{16,0},{20,4},{24,8},{28,12},{1,17},{... | collective-permute-start | bytes 393224 | tf_op jit(solution)/shard_map/ppermute | solution.py:164
  98.9 2.7 %collective-permute-start.24 = (bf16[256,256]{1,0:T(8,128)(2,1)S(1)}, bf16[256,256]{1,0:T(8,128)(2,1)S(1)}, u32[]{:S(2)}, u32[]{:S(2)}) collective-permute-start(bf16[256,256]{1,0:T(8,128)(2,1)S(1)} %get-tuple-element.92), channel_id=1, source_target_pairs={{0,24},{4,28},{8,16},{12,20},{16,8},{20,12},{24,0},{28,4},{1,25},{... | collective-permute-start | bytes 393224 | tf_op jit(solution)/shard_map/ppermute | solution.py:164
  116.3 4.0 %collective-permute-done.32.refs_8_ = bf16[256,256]{1,0:T(8,128)(2,1)S(1)} collective-permute-done((bf16[256,256]{1,0:T(8,128)(2,1)S(1)}, bf16[256,256]{1,0:T(8,128)(2,1)S(1)}, u32[]{:S(2)}, u32[]{:S(2)}) %collective-permute-start.32) | collective-permute-done | bytes 131104 | tf_op jit(solution)/shard_map/ppermute | solution.py:164
  134.5 4.7 %collective-permute-done.17.other_ref = bf16[2,512,128]{2,1,0:T(8,128)(2,1)S(1)} collective-permute-done((bf16[2,512,128]{2,1,0:T(8,128)(2,1)S(1)}, bf16[2,512,128]{2,1,0:T(8,128)(2,1)S(1)}, u32[]{:S(2)}, u32[]{:S(2)}) %collective-permute-start.17) | collective-permute-done | bytes 262176 | tf_op jit(solution)/shard_map/ppermute | solution.py:175
  142.2 3.4 %collective-permute-done.35.other_ref = bf16[2,512,128]{2,1,0:T(8,128)(2,1)S(1)} collective-permute-done((bf16[2,512,128]{2,1,0:T(8,128)(2,1)S(1)}, bf16[2,512,128]{2,1,0:T(8,128)(2,1)S(1)}, u32[]{:S(2)}, u32[]{:S(2)}) %collective-permute-start.35) | collective-permute-done | bytes 262176 | tf_op jit(solution)/shard_map/ppermute | solution.py:175
  153.5 4.2 %collective-permute-done.18 = bf16[512,128]{1,0:T(8,128)(2,1)S(1)} collective-permute-done((bf16[512,128]{1,0:T(8,128)(2,1)S(1)}, bf16[512,128]{1,0:T(8,128)(2,1)S(1)}, u32[]{:S(2)}, u32[]{:S(2)}) %collective-permute-start.18) | collective-permute-done | bytes 131104 | tf_op jit(solution)/shard_map/ppermute | solution.py:175
  157.7 6.8 %collective-permute-done.41.other_ref = bf16[2,512,128]{2,1,0:T(8,128)(2,1)S(1)} collective-permute-done((bf16[2,512,128]{2,1,0:T(8,128)(2,1)S(1)}, bf16[2,512,128]{2,1,0:T(8,128)(2,1)S(1)}, u32[]{:S(2)}, u32[]{:S(2)}) %collective-permute-start.41) | collective-permute-done | bytes 262176 | tf_op jit(solution)/shard_map/ppermute | solution.py:175
  165.7 7.7 %collective-permute-done.42 = bf16[512,128]{1,0:T(8,128)(2,1)S(1)} collective-permute-done((bf16[512,128]{1,0:T(8,128)(2,1)S(1)}, bf16[512,128]{1,0:T(8,128)(2,1)S(1)}, u32[]{:S(2)}, u32[]{:S(2)}) %collective-permute-start.42) | collective-permute-done | bytes 131104 | tf_op jit(solution)/shard_map/ppermute | solution.py:175
  178.5 2.8 %collective-permute-done.43 = f32[4,256]{1,0:T(4,128)S(1)} collective-permute-done((f32[4,256]{1,0:T(4,128)S(1)}, f32[4,256]{1,0:T(4,128)S(1)}, u32[]{:S(2)}, u32[]{:S(2)}) %collective-permute-start.43) | collective-permute-done | bytes 4128 | tf_op jit(solution)/shard_map/ppermute | solution.py:170
  (147 shorter events, 80.1 us)
Async XLA Ops:
  3.0 13.6 %collective-permute-start.4 = (bf16[528,256]{1,0:T(8,128)(2,1)}, bf16[528,256]{1,0:T(8,128)(2,1)S(1)}, u32[]{:S(2)}, u32[]{:S(2)}) collective-permute-start(bf16[528,256]{1,0:T(8,128)(2,1)} %get-tuple-element.64), channel_id=1, source_target_pairs={{0,3},{1,0},{2,1},{3,2},{4,7},{5,4},{6,5},{7,6},{8,11},{9,8},{10,9... | collective-permute-start | bytes 811016 | tf_op jit(solution)/shard_map/ppermute | solution.py:170
  8.1 23.7 %collective-permute-start.5 = (bf16[528,256]{1,0:T(8,128)(2,1)}, bf16[528,256]{1,0:T(8,128)(2,1)S(1)}, u32[]{:S(2)}, u32[]{:S(2)}) collective-permute-start(bf16[528,256]{1,0:T(8,128)(2,1)} %get-tuple-element.65), channel_id=1, source_target_pairs={{0,2},{1,3},{2,0},{3,1},{4,6},{5,7},{6,4},{7,5},{8,10},{9,11},{10,... | collective-permute-start | bytes 811016 | tf_op jit(solution)/shard_map/ppermute | solution.py:170
  10.3 63.2 %collective-permute-start.1 = (bf16[2048,256]{1,0:T(8,128)(2,1)S(1)}, bf16[2048,256]{1,0:T(8,128)(2,1)S(1)}, u32[]{:S(2)}, u32[]{:S(2)}) collective-permute-start(bf16[2048,256]{1,0:T(8,128)(2,1)S(1)} %shard_map.166.refs_1_), channel_id=1, source_target_pairs={{0,16},{4,20},{8,24},{12,28},{16,0},{20,4},{24,8},{28,12},{1,17},{... | collective-permute-start | bytes 3145736 | tf_op jit(solution)/shard_map/ppermute | solution.py:164
  11.9 61.7 %collective-permute-start = (bf16[2048,256]{1,0:T(8,128)(2,1)S(1)}, bf16[2048,256]{1,0:T(8,128)(2,1)S(1)}, u32[]{:S(2)}, u32[]{:S(2)}) collective-permute-start(bf16[2048,256]{1,0:T(8,128)(2,1)S(1)} %shard_map.166.refs_1_), channel_id=1, source_target_pairs={{0,8},{4,12},{8,0},{12,4},{16,24},{20,28},{24,16},{28,20},{1,9},{5... | collective-permute-start | bytes 3145736 | tf_op jit(solution)/shard_map/ppermute | solution.py:164
  15.3 109.5 %collective-permute-start.37 = (bf16[4,2048,128]{2,1,0:T(8,128)(2,1)S(1)}, bf16[4,2048,128]{2,1,0:T(8,128)(2,1)S(1)}, u32[]{:S(2)}, u32[]{:S(2)}) collective-permute-start(bf16[4,2048,128]{2,1,0:T(8,128)(2,1)S(1)} %get-tuple-element.114), channel_id=1, source_target_pairs={{0,4},{4,0},{8,12},{12,8},{16,20},{20,16},{24,28},{28,24},{1,5},{5... | collective-permute-start | bytes 6291464 | tf_op jit(solution)/shard_map/ppermute | solution.py:164
  16.6 15.3 %collective-permute-start.6 = (bf16[528,256]{1,0:T(8,128)(2,1)S(1)}, bf16[528,256]{1,0:T(8,128)(2,1)S(1)}, u32[]{:S(2)}, u32[]{:S(2)}) collective-permute-start(bf16[528,256]{1,0:T(8,128)(2,1)S(1)} %copy-done.14), channel_id=1, source_target_pairs={{0,1},{1,2},{2,3},{3,0},{4,5},{5,6},{6,7},{7,4},{8,9},{9,10},{10,1... | collective-permute-start | bytes 811016 | tf_op jit(solution)/shard_map/ppermute | solution.py:170
  31.9 22.7 %collective-permute-start.8 = (bf16[528,256]{1,0:T(8,128)(2,1)S(1)}, bf16[528,256]{1,0:T(8,128)(2,1)S(1)}, u32[]{:S(2)}, u32[]{:S(2)}) collective-permute-start(bf16[528,256]{1,0:T(8,128)(2,1)S(1)} %get-tuple-element.69), channel_id=1, source_target_pairs={{0,2},{1,3},{2,0},{3,1},{4,6},{5,7},{6,4},{7,5},{8,10},{9,11},{10,... | collective-permute-start | bytes 811016 | tf_op jit(solution)/shard_map/ppermute | solution.py:170
  39.8 15.2 %collective-permute-start.9 = (bf16[528,256]{1,0:T(8,128)(2,1)S(1)}, bf16[528,256]{1,0:T(8,128)(2,1)S(1)}, u32[]{:S(2)}, u32[]{:S(2)}) collective-permute-start(bf16[528,256]{1,0:T(8,128)(2,1)S(1)} %get-tuple-element.70), channel_id=1, source_target_pairs={{0,1},{1,2},{2,3},{3,0},{4,5},{5,6},{6,7},{7,4},{8,9},{9,10},{10,1... | collective-permute-start | bytes 811016 | tf_op jit(solution)/shard_map/ppermute | solution.py:170
  68.1 8.9 %collective-permute-start.19 = (bf16[256,256]{1,0:T(8,128)(2,1)S(1)}, bf16[256,256]{1,0:T(8,128)(2,1)S(1)}, u32[]{:S(2)}, u32[]{:S(2)}) collective-permute-start(bf16[256,256]{1,0:T(8,128)(2,1)S(1)} %get-tuple-element.86), channel_id=1, source_target_pairs={{0,1},{1,2},{2,3},{3,0},{4,5},{5,6},{6,7},{7,4},{8,9},{9,10},{10,1... | collective-permute-start | bytes 393224 | tf_op jit(solution)/shard_map/ppermute | solution.py:170
  69.9 10.4 %collective-permute-start.20 = (bf16[256,256]{1,0:T(8,128)(2,1)S(1)}, bf16[256,256]{1,0:T(8,128)(2,1)S(1)}, u32[]{:S(2)}, u32[]{:S(2)}) collective-permute-start(bf16[256,256]{1,0:T(8,128)(2,1)S(1)} %get-tuple-element.87), channel_id=1, source_target_pairs={{0,2},{1,3},{2,0},{3,1},{4,6},{5,7},{6,4},{7,5},{8,10},{9,11},{10,... | collective-permute-start | bytes 393224 | tf_op jit(solution)/shard_map/ppermute | solution.py:170
  73.6 33.4 %collective-permute-start.3 = (bf16[1024,256]{1,0:T(8,128)(2,1)S(1)}, bf16[1024,256]{1,0:T(8,128)(2,1)S(1)}, u32[]{:S(2)}, u32[]{:S(2)}) collective-permute-start(bf16[1024,256]{1,0:T(8,128)(2,1)S(1)} %slice.25), channel_id=1, source_target_pairs={{0,8},{4,12},{8,0},{12,4},{16,24},{20,28},{24,16},{28,20},{1,9},{5... | collective-permute-start | bytes 1572872 | tf_op jit(solution)/shard_map/ppermute | solution.py:164
  77.0 31.9 %collective-permute-start.2 = (bf16[1024,256]{1,0:T(8,128)(2,1)S(1)}, bf16[1024,256]{1,0:T(8,128)(2,1)S(1)}, u32[]{:S(2)}, u32[]{:S(2)}) collective-permute-start(bf16[1024,256]{1,0:T(8,128)(2,1)S(1)} %slice.24), channel_id=1, source_target_pairs={{0,16},{4,20},{8,24},{12,28},{16,0},{20,4},{24,8},{28,12},{1,17},{... | collective-permute-start | bytes 1572872 | tf_op jit(solution)/shard_map/ppermute | solution.py:164
  81.7 9.8 %collective-permute-start.29 = (bf16[256,256]{1,0:T(8,128)(2,1)S(1)}, bf16[256,256]{1,0:T(8,128)(2,1)S(1)}, u32[]{:S(2)}, u32[]{:S(2)}) collective-permute-start(bf16[256,256]{1,0:T(8,128)(2,1)S(1)} %get-tuple-element.101), channel_id=1, source_target_pairs={{0,2},{1,3},{2,0},{3,1},{4,6},{5,7},{6,4},{7,5},{8,10},{9,11},{10,... | collective-permute-start | bytes 393224 | tf_op jit(solution)/shard_map/ppermute | solution.py:170
  111.5 10.7 %collective-permute-start.25 = (bf16[2048,128]{1,0:T(8,128)(2,1)S(1)}, bf16[2048,128]{1,0:T(8,128)(2,1)S(1)}, u32[]{:S(2)}, u32[]{:S(2)}) collective-permute-start(bf16[2048,128]{1,0:T(8,128)(2,1)S(1)} %get-tuple-element.94), channel_id=1, source_target_pairs={{0,4},{4,0},{8,12},{12,8},{16,20},{20,16},{24,28},{28,24},{1,5},{5... | collective-permute-start | bytes 1572872 | tf_op jit(solution)/shard_map/ppermute | solution.py:164
  116.2 12.1 %collective-permute-start.16 = (bf16[2048,128]{1,0:T(8,128)(2,1)S(1)}, bf16[2048,128]{1,0:T(8,128)(2,1)S(1)}, u32[]{:S(2)}, u32[]{:S(2)}) collective-permute-start(bf16[2048,128]{1,0:T(8,128)(2,1)S(1)} %get-tuple-element.80), channel_id=1, source_target_pairs={{0,4},{4,0},{8,12},{12,8},{16,20},{20,16},{24,28},{28,24},{1,5},{5... | collective-permute-start | bytes 1572872 | tf_op jit(solution)/shard_map/ppermute | solution.py:164
  125.8 21.5 %collective-permute-start.38 = (bf16[2048,128]{1,0:T(8,128)(2,1)S(1)}, bf16[2048,128]{1,0:T(8,128)(2,1)S(1)}, u32[]{:S(2)}, u32[]{:S(2)}) collective-permute-start(bf16[2048,128]{1,0:T(8,128)(2,1)S(1)} %get-tuple-element.116), channel_id=1, source_target_pairs={{0,8},{4,12},{8,0},{12,4},{16,24},{20,28},{24,16},{28,20},{1,9},{5... | collective-permute-start | bytes 1572872 | tf_op jit(solution)/shard_map/ppermute | solution.py:164
  126.7 24.1 %collective-permute-start.39 = (bf16[2048,128]{1,0:T(8,128)(2,1)S(1)}, bf16[2048,128]{1,0:T(8,128)(2,1)S(1)}, u32[]{:S(2)}, u32[]{:S(2)}) collective-permute-start(bf16[2048,128]{1,0:T(8,128)(2,1)S(1)} %get-tuple-element.117), channel_id=1, source_target_pairs={{0,16},{4,20},{8,24},{12,28},{16,0},{20,4},{24,8},{28,12},{1,17},{... | collective-permute-start | bytes 1572872 | tf_op jit(solution)/shard_map/ppermute | solution.py:164
  128.3 24.0 %collective-permute-start.40 = (bf16[2048,128]{1,0:T(8,128)(2,1)S(1)}, bf16[2048,128]{1,0:T(8,128)(2,1)S(1)}, u32[]{:S(2)}, u32[]{:S(2)}) collective-permute-start(bf16[2048,128]{1,0:T(8,128)(2,1)S(1)} %get-tuple-element.118), channel_id=1, source_target_pairs={{0,24},{4,28},{8,16},{12,20},{16,8},{20,12},{24,0},{28,4},{1,25},{... | collective-permute-start | bytes 1572872 | tf_op jit(solution)/shard_map/ppermute | solution.py:164
  130.0 9.2 %collective-permute-start.17 = (bf16[2,512,128]{2,1,0:T(8,128)(2,1)S(1)}, bf16[2,512,128]{2,1,0:T(8,128)(2,1)S(1)}, u32[]{:S(2)}, u32[]{:S(2)}) collective-permute-start(bf16[2,512,128]{2,1,0:T(8,128)(2,1)S(1)} %get-tuple-element.82), channel_id=1, source_target_pairs={{0,1},{1,0},{2,3},{3,2},{4,5},{5,4},{6,7},{7,6},{8,9},{9,8},{10,11... | collective-permute-start | bytes 786440 | tf_op jit(solution)/shard_map/ppermute | solution.py:175
  131.7 13.9 %collective-permute-start.35 = (bf16[2,512,128]{2,1,0:T(8,128)(2,1)S(1)}, bf16[2,512,128]{2,1,0:T(8,128)(2,1)S(1)}, u32[]{:S(2)}, u32[]{:S(2)}) collective-permute-start(bf16[2,512,128]{2,1,0:T(8,128)(2,1)S(1)} %get-tuple-element.110), channel_id=1, source_target_pairs={{0,1},{1,0},{2,3},{3,2},{4,5},{5,4},{6,7},{7,6},{8,9},{9,8},{10,11... | collective-permute-start | bytes 786440 | tf_op jit(solution)/shard_map/ppermute | solution.py:175
  139.3 14.1 %collective-permute-start.27 = (bf16[512,128]{1,0:T(8,128)(2,1)S(1)}, bf16[512,128]{1,0:T(8,128)(2,1)S(1)}, u32[]{:S(2)}, u32[]{:S(2)}) collective-permute-start(bf16[512,128]{1,0:T(8,128)(2,1)S(1)} %get-tuple-element.98), channel_id=1, source_target_pairs={{0,2},{1,3},{2,0},{3,1},{4,6},{5,7},{6,4},{7,5},{8,10},{9,11},{10,... | collective-permute-start | bytes 393224 | tf_op jit(solution)/shard_map/ppermute | solution.py:175
  145.7 12.0 %collective-permute-start.18 = (bf16[512,128]{1,0:T(8,128)(2,1)S(1)}, bf16[512,128]{1,0:T(8,128)(2,1)S(1)}, u32[]{:S(2)}, u32[]{:S(2)}) collective-permute-start(bf16[512,128]{1,0:T(8,128)(2,1)S(1)} %get-tuple-element.84), channel_id=1, source_target_pairs={{0,2},{1,3},{2,0},{3,1},{4,6},{5,7},{6,4},{7,5},{8,10},{9,11},{10,... | collective-permute-start | bytes 393224 | tf_op jit(solution)/shard_map/ppermute | solution.py:175
  147.3 18.4 %collective-permute-start.36 = (bf16[512,128]{1,0:T(8,128)(2,1)S(1)}, bf16[512,128]{1,0:T(8,128)(2,1)S(1)}, u32[]{:S(2)}, u32[]{:S(2)}) collective-permute-start(bf16[512,128]{1,0:T(8,128)(2,1)S(1)} %get-tuple-element.112), channel_id=1, source_target_pairs={{0,2},{1,3},{2,0},{3,1},{4,6},{5,7},{6,4},{7,5},{8,10},{9,11},{10,... | collective-permute-start | bytes 393224 | tf_op jit(solution)/shard_map/ppermute | solution.py:175
  153.0 11.4 %collective-permute-start.41 = (bf16[2,512,128]{2,1,0:T(8,128)(2,1)S(1)}, bf16[2,512,128]{2,1,0:T(8,128)(2,1)S(1)}, u32[]{:S(2)}, u32[]{:S(2)}) collective-permute-start(bf16[2,512,128]{2,1,0:T(8,128)(2,1)S(1)} %get-tuple-element.120), channel_id=1, source_target_pairs={{0,1},{1,0},{2,3},{3,2},{4,5},{5,4},{6,7},{7,6},{8,9},{9,8},{10,11... | collective-permute-start | bytes 786440 | tf_op jit(solution)/shard_map/ppermute | solution.py:175
  (41 other events, 414.3 us)
